TPU v7x, 32 devices: a whole 2x2x4 slice. The times are simulated.
32 devices in a mesh: seq: 16 (over z, y, core), fsdp: 2 (over x).
Axes of the slice: x: 2, y: 2, z: 4, core: 2. Of those that a mesh axis runs over, the one named last changes fastest.
Arguments:
- inputs: bfloat16 [2, 2048, 2048], P('fsdp', 'seq'), may hold values from -10 to 10
- routes: int32 [2, 2048, 8], P('fsdp', 'seq'), may hold values from 0 to 15, all different within a row; in each aligned block of 128 rows (0 to 127, 128 to 255, ..., all dimensions but the last counted through in order) at most 80 rows name the same one
- w_qkv: bfloat16 [2048, 6144], P(('seq', 'fsdp')), may hold values from -1 to 1
- w_out: bfloat16 [2048, 2048], P(('seq', 'fsdp')), may hold values from -0.375 to 0.375
- w_router: bfloat16 [2048, 16], P(('seq', 'fsdp')), may hold values from -2.5 to 2.5
- norm_gains: bfloat16 [2048, 4], P(('seq', 'fsdp')), may hold values from 0.5 to 1.5
- w_gate: bfloat16 [16, 2048, 1024], P('seq', None, 'fsdp'), may hold values from -0.125 to 0.125
- w_up: bfloat16 [16, 2048, 1024], P('seq', None, 'fsdp'), may hold values from -0.125 to 0.125
- w_down: bfloat16 [16, 2048, 1024], P('seq', None, 'fsdp'), may hold values from -0.75 to 0.75
- cotangent: bfloat16 [2, 2048, 2048], P('fsdp', 'seq'), may hold values from -6 to 6
Outputs:
- result: bfloat16 [2, 2048, 2048], P('fsdp', 'seq')
- grad_inputs: float32 [2, 2048, 2048], P('fsdp', 'seq')
- grad_qkv: float32 [2048, 6144], P(('seq', 'fsdp'))
- grad_proj: float32 [2048, 2048], P(('seq', 'fsdp'))
- grad_router: float32 [2048, 16], P(('seq', 'fsdp'))
- grad_gains: float32 [2048, 4], P(('seq', 'fsdp'))
- grad_gate: float32 [16, 2048, 1024], P('seq', None, 'fsdp')
- grad_up: float32 [16, 2048, 1024], P('seq', None, 'fsdp')
- grad_down: float32 [16, 2048, 1024], P('seq', None, 'fsdp')
Inputs may be any that keep to these rules, and one draw needn't show every extreme that they name: `routes`: each row names 8 different experts. In the rows of one device (aligned blocks of 128 rows of a sequence) no expert is named by more than 80 rows, a bound that some block reaches.
All inputs are finite; a program needn't handle non-finite values.
Results may differ from a plain program's by a relative error of at most 0.024.
The roundings to bfloat16 on the way count: a program that leaves them out, or rounds other values in their place, can miss the bound.
Values may be sent and summed in bfloat16 or wider, within the bound.
A program may use at most 256 MiB of HBM per device.

v0:
```python
from functools import partial

import jax
import jax.numpy as jnp
from jax import lax
from jax.sharding import PartitionSpec as P

HEADS = 16
TOPK = 8


EPS = 1e-05
NEG = -1e30
HIGH = lax.Precision.HIGHEST


def normalize(values, gain):
    return values * lax.rsqrt(jnp.mean(values * values, -1, keepdims=True) + EPS) * gain


def rotate(values, positions):
    half = values.shape[-1] // 2
    freqs = 10000.0 ** (-jnp.arange(half, dtype=jnp.float32) / half)
    angles = positions.astype(jnp.float32)[:, None] * freqs[None, :]
    cosine = jnp.concatenate([jnp.cos(angles), jnp.cos(angles)], -1)[:, None, :]
    sine = jnp.concatenate([jnp.sin(angles), jnp.sin(angles)], -1)[:, None, :]
    turned = jnp.concatenate([-values[..., half:], values[..., :half]], -1)
    return values * cosine + turned * sine


def prepare(mixed, gain_query, gain_key, positions):
    width = gain_query.shape[0]
    shaped = (mixed.shape[0], HEADS, width // HEADS)
    queries = normalize(mixed[:, :width], gain_query).reshape(shaped)
    key_rows = normalize(mixed[:, width : 2 * width], gain_key).reshape(shaped)
    value_rows = mixed[:, 2 * width :].reshape(shaped)
    return (rotate(queries, positions), rotate(key_rows, positions), value_rows)


def route_weights(logits, routes):
    top = jnp.max(logits, -1, keepdims=True)
    expd = jnp.exp(logits - top)
    probs = expd / jnp.sum(expd, -1, keepdims=True)
    return jnp.take_along_axis(probs, routes, 1)


def swiglu(gate_act, up_act):
    return jax.nn.silu(gate_act) * up_act


def arrange(block_routes, experts, capacity):
    flat = block_routes.reshape(-1)
    onehot = (flat[:, None] == jnp.arange(experts, dtype=jnp.int32)[None, :]).astype(jnp.int32)
    before = jnp.cumsum(onehot, 0) - onehot
    places = jnp.sum(before * onehot, 1)
    slot = flat * capacity + places
    entries = flat.shape[0]
    entry = (
        jnp.zeros((experts * capacity,), jnp.int32)
        .at[slot]
        .set(jnp.arange(entries, dtype=jnp.int32))
    )
    filled = jnp.zeros((experts * capacity,), jnp.int32).at[slot].set(1)
    return (slot, entry, filled)


def shards(inputs, routes, w_qkv, w_out, w_router, norm_gains, w_gate, w_up, w_down, cotangent):
    tokens = inputs[0].astype(jnp.float32)
    upstream = cotangent[0].astype(jnp.float32)
    local_routes = routes[0]
    seq_count = lax.axis_size("seq")
    tok_count = tokens.shape[0]
    width = tokens.shape[1]
    length = tok_count * seq_count
    head_size = width // HEADS
    local_heads = HEADS // seq_count
    local_width = local_heads * head_size
    head_shape = (tok_count, HEADS, head_size)
    experts_here = w_gate.shape[0]
    experts = experts_here * seq_count
    capacity = min(tok_count, 5 * tok_count * TOPK // (4 * experts))
    positions = lax.axis_index("seq") * tok_count + jnp.arange(tok_count, dtype=jnp.int32)
    block = min(512, length)
    blocks = length // block
    factor = head_size ** (-0.5)
    w_qkv_all, w_out_all, w_router_all, gains_all = (
        lax.all_gather(w_qkv, ("seq", "fsdp"), axis=0, tiled=True),
        lax.all_gather(w_out, ("seq", "fsdp"), axis=0, tiled=True),
        lax.all_gather(w_router, ("seq", "fsdp"), axis=0, tiled=True),
        lax.all_gather(norm_gains, ("seq", "fsdp"), axis=0, tiled=True),
    )
    gains32 = gains_all.astype(jnp.float32)
    normed_one, norm_one_back = jax.vjp(normalize, tokens, gains32[:, 0])
    hidden_one = normed_one.astype(jnp.bfloat16)
    mixed = jnp.dot(hidden_one, w_qkv_all, preferred_element_type=jnp.float32)
    prepared, prepare_back = jax.vjp(
        partial(prepare, positions=positions), mixed, gains32[:, 1], gains32[:, 2]
    )
    members = [prepared[0], prepared[1], prepared[2], normed_one.reshape(head_shape)]
    by_heads = lax.all_to_all(
        jnp.stack(members).astype(jnp.bfloat16), "seq", split_axis=2, concat_axis=1, tiled=True
    )
    queries, key_rows, value_rows = (by_heads[0], by_heads[1], by_heads[2])
    key_pos = jnp.arange(length, dtype=jnp.int32)

    def block_scores(index):
        start = index * block
        part = lax.dynamic_slice_in_dim(queries, start, block, 0)
        scores = (
            jnp.einsum("qhd,khd->hqk", part, key_rows, preferred_element_type=jnp.float32) * factor
        )
        allowed = key_pos[None, :] <= (start + jnp.arange(block, dtype=jnp.int32))[:, None]
        return (part, jnp.where(allowed[None], scores, NEG))

    def forward_block(index):
        part, scores = block_scores(index)
        top = jnp.max(scores, -1, keepdims=True)
        expd = jnp.exp(scores - top)
        total = jnp.sum(expd, -1, keepdims=True)
        probs = (expd / total).astype(jnp.bfloat16)
        outcome = jnp.einsum("hqk,khd->qhd", probs, value_rows, preferred_element_type=jnp.float32)
        return (outcome.astype(jnp.bfloat16), (top + jnp.log(total))[..., 0])

    attended, log_sums = lax.map(forward_block, jnp.arange(blocks, dtype=jnp.int32))
    attended = attended.reshape(length, local_heads, head_size)
    attended_tok = lax.all_to_all(attended, "seq", split_axis=0, concat_axis=1, tiled=True).reshape(
        tok_count, width
    )
    attn_out = jnp.dot(attended_tok, w_out_all, preferred_element_type=jnp.float32)
    middle = tokens + attn_out
    normed_two, norm_two_back = jax.vjp(normalize, middle, gains32[:, 3])
    hidden_two = normed_two.astype(jnp.bfloat16)
    logits = jnp.dot(hidden_two, w_router_all, preferred_element_type=jnp.float32)
    weights, route_back = jax.vjp(partial(route_weights, routes=local_routes), logits)
    slot, entry, filled = arrange(local_routes, experts, capacity)
    source = entry // TOPK
    occupied = filled[:, None] > 0
    sending = jnp.where(occupied, hidden_two[source], jnp.zeros((), jnp.bfloat16))
    entry_weight = weights.reshape(-1)[entry]
    d_sending = jnp.where(occupied, entry_weight[:, None] * upstream[source], 0.0).astype(
        jnp.bfloat16
    )
    outgoing = jnp.stack([sending, d_sending]).reshape(2, seq_count, experts_here, capacity, width)
    arrived = lax.all_to_all(outgoing, "seq", split_axis=1, concat_axis=3, tiled=True)
    expert_rows = arrived[0, 0]
    d_produced = arrived[1, 0]
    gate_all, up_all, down_all = (
        lax.all_gather(w_gate, "fsdp", axis=2, tiled=True),
        lax.all_gather(w_up, "fsdp", axis=2, tiled=True),
        lax.all_gather(w_down, "fsdp", axis=2, tiled=True),
    )
    gate_act = jnp.einsum("jrd,jdf->jrf", expert_rows, gate_all, preferred_element_type=jnp.float32)
    up_act = jnp.einsum("jrd,jdf->jrf", expert_rows, up_all, preferred_element_type=jnp.float32)
    inner, inner_back = jax.vjp(swiglu, gate_act, up_act)
    inner_low = inner.astype(jnp.bfloat16)
    produced = jnp.einsum(
        "jrf,jdf->jrd", inner_low, down_all, preferred_element_type=jnp.float32
    ).astype(jnp.bfloat16)
    returned = lax.all_to_all(
        produced[None], "seq", split_axis=2, concat_axis=0, tiled=True
    ).reshape(experts * capacity, width)
    chosen = returned[slot].reshape(tok_count, TOPK, width).astype(jnp.float32)
    moe = jnp.einsum("tk,tkd->td", weights, chosen, precision=HIGH)
    result = (middle + moe).astype(jnp.bfloat16)
    d_weights = jnp.einsum("td,tkd->tk", upstream, chosen, precision=HIGH)
    d_inner = jnp.einsum("jrd,jdf->jrf", d_produced, down_all, preferred_element_type=jnp.float32)
    d_gate_act, d_up_act = inner_back(d_inner)
    d_gate_low = d_gate_act.astype(jnp.bfloat16)
    d_up_low = d_up_act.astype(jnp.bfloat16)
    d_rows = jnp.einsum("jrf,jdf->jrd", d_gate_low, gate_all, preferred_element_type=jnp.float32)
    d_rows = (
        d_rows + jnp.einsum("jrf,jdf->jrd", d_up_low, up_all, preferred_element_type=jnp.float32)
    ).astype(jnp.bfloat16)
    gate_part = jnp.einsum(
        "jrd,jrf->jdf", expert_rows, d_gate_low, preferred_element_type=jnp.float32
    )
    up_part = jnp.einsum("jrd,jrf->jdf", expert_rows, d_up_low, preferred_element_type=jnp.float32)
    down_part = jnp.einsum(
        "jrd,jrf->jdf", d_produced, inner_low, preferred_element_type=jnp.float32
    )
    grad_gate, grad_up, grad_down = (
        lax.psum_scatter(
            gate_part.astype(jnp.bfloat16), "fsdp", scatter_dimension=2, tiled=True
        ).astype(jnp.float32),
        lax.psum_scatter(
            up_part.astype(jnp.bfloat16), "fsdp", scatter_dimension=2, tiled=True
        ).astype(jnp.float32),
        lax.psum_scatter(
            down_part.astype(jnp.bfloat16), "fsdp", scatter_dimension=2, tiled=True
        ).astype(jnp.float32),
    )
    d_returned = lax.all_to_all(
        d_rows[None], "seq", split_axis=2, concat_axis=0, tiled=True
    ).reshape(experts * capacity, width)
    d_hidden_moe = jnp.sum(d_returned[slot].reshape(tok_count, TOPK, width).astype(jnp.float32), 1)
    d_logits = route_back(d_weights)[0].astype(jnp.bfloat16)
    d_hidden_two = d_hidden_moe + jnp.dot(
        d_logits, w_router_all.T, preferred_element_type=jnp.float32
    )
    d_middle_norm, gain_two_part = norm_two_back(d_hidden_two)
    d_middle = upstream + d_middle_norm
    d_attn = d_middle.astype(jnp.bfloat16)
    d_attended_tok = jnp.dot(d_attn, w_out_all.T, preferred_element_type=jnp.float32).astype(
        jnp.bfloat16
    )
    heads_grad = d_attended_tok.reshape(head_shape)
    carried = jnp.stack([heads_grad, hidden_two.reshape(head_shape)])
    arrived_heads = lax.all_to_all(carried, "seq", split_axis=2, concat_axis=1, tiled=True)
    d_attended = arrived_heads[0]

    def backward_block(carry, index):
        d_key_sum, d_value_sum = carry
        part, scores = block_scores(index)
        d_part = lax.dynamic_slice_in_dim(d_attended, index * block, block, 0)
        probs = jnp.exp(scores - log_sums[index][..., None])
        d_probs = jnp.einsum("qhd,khd->hqk", d_part, value_rows, preferred_element_type=jnp.float32)
        delta = jnp.sum(probs * d_probs, -1, keepdims=True)
        d_scores = (probs * (d_probs - delta)).astype(jnp.bfloat16)
        d_query = (
            jnp.einsum("hqk,khd->qhd", d_scores, key_rows, preferred_element_type=jnp.float32)
            * factor
        )
        d_key_sum = (
            d_key_sum
            + jnp.einsum("hqk,qhd->khd", d_scores, part, preferred_element_type=jnp.float32)
            * factor
        )
        d_value_sum = d_value_sum + jnp.einsum(
            "hqk,qhd->khd", probs.astype(jnp.bfloat16), d_part, preferred_element_type=jnp.float32
        )
        return ((d_key_sum, d_value_sum), d_query)

    zero_heads = jnp.zeros((length, local_heads, head_size), jnp.float32)
    (d_keys, d_values), d_queries = lax.scan(
        backward_block, (zero_heads, zero_heads), jnp.arange(blocks, dtype=jnp.int32)
    )
    d_heads = jnp.stack(
        [d_queries.reshape(length, local_heads, head_size), d_keys, d_values]
    ).astype(jnp.bfloat16)
    d_prepared = lax.all_to_all(d_heads, "seq", split_axis=1, concat_axis=2, tiled=True).astype(
        jnp.float32
    )
    d_mixed, gain_query_part, gain_key_part = prepare_back(
        (d_prepared[0], d_prepared[1], d_prepared[2])
    )
    d_mixed_low = d_mixed.astype(jnp.bfloat16)
    d_hidden_one = jnp.dot(d_mixed_low, w_qkv_all.T, preferred_element_type=jnp.float32)
    d_tokens_norm, gain_one_part = norm_one_back(d_hidden_one)
    grad_inputs = (d_middle + d_tokens_norm)[None]
    gain_part = jnp.stack([gain_one_part, gain_query_part, gain_key_part, gain_two_part], 1)
    hidden_cols = by_heads[3].reshape(length, local_width)
    attended_cols = attended.reshape(length, local_width)
    second_cols = arrived_heads[1].reshape(length, local_width)
    qkv_total = jnp.einsum(
        "tc,tk->ck",
        hidden_cols,
        lax.all_gather(d_mixed_low, "seq", axis=0, tiled=True),
        preferred_element_type=jnp.float32,
    )
    proj_total = jnp.einsum(
        "tc,tk->ck",
        attended_cols,
        lax.all_gather(d_attn, "seq", axis=0, tiled=True),
        preferred_element_type=jnp.float32,
    )
    router_total = jnp.einsum(
        "tc,tk->ck",
        second_cols,
        lax.all_gather(d_logits, "seq", axis=0, tiled=True),
        preferred_element_type=jnp.float32,
    )
    grad_qkv, grad_proj, grad_router = (
        lax.psum_scatter(
            qkv_total.astype(jnp.bfloat16), "fsdp", scatter_dimension=0, tiled=True
        ).astype(jnp.float32),
        lax.psum_scatter(
            proj_total.astype(jnp.bfloat16), "fsdp", scatter_dimension=0, tiled=True
        ).astype(jnp.float32),
        lax.psum_scatter(
            router_total.astype(jnp.bfloat16), "fsdp", scatter_dimension=0, tiled=True
        ).astype(jnp.float32),
    )
    grad_gains = lax.psum_scatter(gain_part, ("seq", "fsdp"), scatter_dimension=0, tiled=True)
    return (
        result[None],
        grad_inputs,
        grad_qkv,
        grad_proj,
        grad_router,
        grad_gains,
        grad_gate,
        grad_up,
        grad_down,
    )


def solution(mesh):
    return jax.shard_map(
        shards,
        mesh=mesh,
        in_specs=(
            P("fsdp", "seq", None),
            P("fsdp", "seq", None),
            P(("seq", "fsdp"), None),
            P(("seq", "fsdp"), None),
            P(("seq", "fsdp"), None),
            P(("seq", "fsdp"), None),
            P("seq", None, "fsdp"),
            P("seq", None, "fsdp"),
            P("seq", None, "fsdp"),
            P("fsdp", "seq", None),
        ),
        out_specs=(
            P("fsdp", "seq", None),
            P("fsdp", "seq", None),
            P(("seq", "fsdp"), None),
            P(("seq", "fsdp"), None),
            P(("seq", "fsdp"), None),
            P(("seq", "fsdp"), None),
            P("seq", None, "fsdp"),
            P("seq", None, "fsdp"),
            P("seq", None, "fsdp"),
        ),
        check_vma=False,
    )
```

profile of v0, /device:TPU:0, one launch (start us, length us, event | category | flops | bytes accessed | tf_op | source)
XLA Modules:
  0.0 1776.1 jit_solution(17824849690963854128)
XLA Ops:
  9.5 72.3 %all-gather = bf16[32,64,4]{1,2,0:T(4,128)(2,1)S(1)} all-gather(bf16[1,64,4]{1,2,0:T(4,128)(2,1)} %bitcast.519), channel_id=1, replica_groups=mesh['seq'=16,'fsdp'=2] {'seq','fsdp'}, dimensions={0}, use_global_device_ids=true | all-gather | bytes 16896 | tf_op jit(solution)/shard_map/all_gather | solution.py:90
  85.6 83.2 %all-gather.10.cloned.1.call-done = bf16[2048,6144]{1,0:T(8,128)(2,1)} async-done(((bf16[64,6144]{1,0:T(8,128)(2,1)}), bf16[2048,6144]{1,0:T(8,128)(2,1)}) %all-gather.10.cloned.1.call-update) | async-done | bytes 25165840 | tf_op jit(solution)/shard_map/all_gather | solution.py:87
  168.8 10.2 fusion.86
  200.1 44.8 %all-to-all-done = bf16[4,128,16,128]{3,1,0,2:T(8,128)(2,1)S(1)} async-done(((bf16[4,128,16,128]{3,1,0,2:T(8,128)(2,1)}), bf16[4,128,16,128]{3,1,0,2:T(8,128)(2,1)S(1)}, u32[]{:S(2)}, u32[]{:S(2)}) %all-to-all-start) | async-done | bytes 2097184 | tf_op jit(solution)/shard_map/all_to_all | solution.py:100
  245.9 17.8 %while.28 = (s32[]{:T(128)}, bf16[4,512,1,128]{3,1,2,0:T(8,128)(2,1)S(1)}, f32[4,1,512]{2,1,0:T(1,128)}, s32[4]{0:T(128)S(1)}, bf16[2048,1,128]{2,0,1:T(8,128)(2...) while((s32[]{:T(128)}, ...), condition=%wide.region_6.7_spmd.clone, body=%wide.region_3.6_spmd.clone.sunk | while | flops 546373632 | bytes 13918899 | solution.py:124
  266.3 30.5 %all-to-all-start.1 = ((bf16[16,2,8192]{2,1,0:T(2,128)(2,1)}), bf16[16,2,8192]{2,1,0:T(2,128)(2,1)S(1)}, u32[]{:S(2)}, u32[]{:S(2)}) async-start(bf16[16,2,8192]{2,1,0:T(2,128)(2,1)} %reshape.833), calls=%async_computation.1 | async-start | bytes 1048576 | tf_op jit(solution)/shard_map/all_to_all | solution.py:126
  301.3 68.7 %all-gather.1 = bf16[32,64,16]{1,2,0:T(8,128)(2,1)S(1)} all-gather(bf16[1,64,16]{1,2,0:T(8,128)(2,1)S(1)} %bitcast.518), channel_id=1, replica_groups=mesh['seq'=16,'fsdp'=2] {'seq','fsdp'}, dimensions={0}, use_global_device_ids=true | all-gather | bytes 67584 | tf_op jit(solution)/shard_map/all_gather | solution.py:89
  415.8 8.9 pad_maximum_fusion
  431.3 185.3 %all-to-all-done.2 = bf16[2,16,1,80,2048]{4,3,2,0,1:T(8,128)(2,1)} async-done(((bf16[2,16,1,80,2048]{4,3,2,0,1:T(8,128)(2,1)}), bf16[2,16,1,80,2048]{4,3,2,0,1:T(8,128)(2,1)}, u32[]{:S(2)}, u32[]{:S(2)}) %all-to-all-start.2) | async-done | bytes 10485792 | tf_op jit(solution)/shard_map/all_to_all | solution.py:144
  616.5 10.1 fusion.113
  626.7 10.6 fusion.50
  637.3 10.3 fusion.54
  647.6 14.5 multiply_convert_fusion.1
  668.1 30.7 %copy.281 = bf16[1,1,1280,2048]{3,1,0,2:T(2,128)(2,1)} copy(bf16[1,1,1280,2048]{3,2,1,0:T(8,128)(2,1)S(1)} %fusion.36) | data formatting | bytes 10485760 | tf_op jit(solution)/shard_map/broadcast_in_dim | solution.py:160
  698.8 32.7 %reduce.12 = bf16[1280,2048]{1,0:T(8,128)(2,1)} reduce(bf16[1280,1,1,2048]{3,2,1,0:T(2,128)(2,1)} %bitcast.452, bf16[]{:T(256)} %broadcast.547), dimensions={1,2}, to_apply=%bitcast.406.reduce_sub_computation | reduce | bytes 10485762
  731.5 12.2 reshape.835
  743.7 44.9 %all-to-all-start.3 = ((bf16[16,2,81920]{2,1,0:T(2,128)(2,1)}), bf16[16,2,81920]{2,1,0:T(2,128)(2,1)}, u32[]{:S(2)}, u32[]{:S(2)}) async-start(bf16[16,2,81920]{2,1,0:T(2,128)(2,1)} %reshape.835), calls=%async_computation.3 | async-start | bytes 10485760 | tf_op jit(solution)/shard_map/all_to_all | solution.py:159
  788.7 8.5 fusion.52
  797.2 7.9 fusion.37
  805.0 30.6 %copy.280 = bf16[1,1,1280,2048]{3,1,0,2:T(2,128)(2,1)} copy(bf16[1,1,1280,2048]{3,2,1,0:T(8,128)(2,1)S(1)} %fusion.37) | data formatting | bytes 10485760 | tf_op jit(solution)/shard_map/broadcast_in_dim | solution.py:193
  835.6 32.9 %reduce.11 = bf16[1280,2048]{1,0:T(8,128)(2,1)} reduce(bf16[1280,1,1,2048]{3,2,1,0:T(2,128)(2,1)} %bitcast.451, bf16[]{:T(256)} %broadcast.547), dimensions={1,2}, to_apply=%bitcast.405.reduce_sub_computation | reduce | bytes 10485762
  868.5 12.2 reshape.837
  884.5 24.1 %all-to-all-start.4 = ((bf16[16,2,81920]{2,1,0:T(2,128)(2,1)}), bf16[16,2,81920]{2,1,0:T(2,128)(2,1)}, u32[]{:S(2)}, u32[]{:S(2)}) async-start(bf16[16,2,81920]{2,1,0:T(2,128)(2,1)} %reshape.837), calls=%async_computation.4 | async-start | bytes 10485760 | tf_op jit(solution)/shard_map/all_to_all | solution.py:192
  910.3 13.3 reshape.836
  923.6 9.6 copy.274
  933.2 12.0 gather_fusion.3
  956.8 47.6 %all-to-all-done.4 = bf16[16,2,81920]{2,1,0:T(2,128)(2,1)} async-done(((bf16[16,2,81920]{2,1,0:T(2,128)(2,1)}), bf16[16,2,81920]{2,1,0:T(2,128)(2,1)}, u32[]{:S(2)}, u32[]{:S(2)}) %all-to-all-start.4) | async-done | bytes 5242912 | tf_op jit(solution)/shard_map/all_to_all | solution.py:192
  1004.4 13.7 reshape.838
  1018.1 9.6 copy.273
  1027.6 12.0 gather_fusion.4
  1054.5 23.8 %all-to-all-start.5 = ((bf16[2,128,16,128]{3,1,0,2:T(8,128)(2,1)}), bf16[2,128,16,128]{3,1,0,2:T(8,128)(2,1)S(1)}, u32[]{:S(2)}, u32[]{:S(2)}) async-start(bf16[2,128,16,128]{3,1,0,2:T(8,128)(2,1)} %pad_maximum_fusion.3), calls=%async_computation.5 | async-start | bytes 2097152 | tf_op jit(solution)/shard_map/all_to_all | solution.py:208
  1079.1 28.2 %all-to-all-done.5 = bf16[2,128,16,128]{3,1,0,2:T(8,128)(2,1)S(1)} async-done(((bf16[2,128,16,128]{3,1,0,2:T(8,128)(2,1)}), bf16[2,128,16,128]{3,1,0,2:T(8,128)(2,1)S(1)}, u32[]{:S(2)}, u32[]{:S(2)}) %all-to-all-start.5) | async-done | bytes 1048608 | tf_op jit(solution)/shard_map/all_to_all | solution.py:208
  1108.4 80.2 %while.29 = (s32[]{:T(128)}, f32[2048,1,128]{0,2,1:T(8,128)}, f32[2048,1,128]{0,2,1:T(8,128)}, bf16[4,512,1,128]{3,1,2,0:T(8,128)(2,1)}, s32[4]{0:T(128)S(1)}, /...) while((s32[]{:T(128)}, f32[2048,1,128]{0,2,1:T(8,128)}, ...), condition=%wide.region_23.24_spmd.clone, body=%wide.region_21.23_spmd.clone.sunk | while | flops 1354039296 | bytes 92552088 | solution.py:234
  1192.8 9.8 copy.205
  1202.5 63.4 %all_to_all.81 = bf16[3,2048,1,128]{3,0,2,1:T(4,128)(2,1)S(1)} all-to-all(bf16[3,2048,1,128]{3,0,2,1:T(4,128)(2,1)S(1)} %copy.205), channel_id=1, replica_groups=mesh['seq'=16,'fsdp'=2] {'seq'}, dimensions={1} | all-to-all | bytes 3145728 | tf_op jit(solution)/shard_map/all_to_all | solution.py:240
  1274.5 9.7 convert_bitcast_fusion.2
  1286.0 9.9 convert_bitcast_fusion.1
  1297.6 10.4 convert_bitcast_fusion
  1308.1 22.1 %all_gather.39 = bf16[2048,16]{0,1:T(8,128)(2,1)S(1)} all-gather(bf16[128,16]{0,1:T(8,128)(2,1)S(1)} %add_convert_fusion.2), channel_id=1, replica_groups=mesh['seq'=16,'fsdp'=2] {'seq'}, dimensions={0}, use_global_device_ids=true | all-gather | bytes 69632 | tf_op jit(solution)/shard_map/all_gather | solution.py:269
  1331.2 14.7 fusion.64
  1353.2 48.8 %all-gather.20.cloned.1.call-done = bf16[2048,6144]{1,0:T(8,128)(2,1)} async-done(((bf16[128,6144]{1,0:T(8,128)(2,1)}), bf16[2048,6144]{1,0:T(8,128)(2,1)}) %all-gather.20.cloned.1.call-update) | async-done | bytes 25165840 | tf_op jit(solution)/shard_map/all_gather | solution.py:257
  1402.0 12.9 convolution_convert_fusion.1
  1415.1 44.4 %reduce-scatter.16.cloned.1.call-done = bf16[1,2048,512]{2,1,0:T(8,128)(2,1)} async-done(((bf16[1,2048,1024]{2,1,0:T(8,128)(2,1)}), bf16[1,2048,512]{2,1,0:T(8,128)(2,1)}) %reduce-scatter.16.cloned.1.call-update) | async-done | bytes 2097168 | tf_op jit(solution)/shard_map/reduce_scatter | solution.py:182
  1463.7 52.9 %reduce-scatter.18.cloned.1.call-done = bf16[1,2048,512]{2,1,0:T(8,128)(2,1)} async-done(((bf16[1,2048,1024]{2,1,0:T(8,128)(2,1)}), bf16[1,2048,512]{2,1,0:T(8,128)(2,1)}) %reduce-scatter.18.cloned.1.call-update) | async-done | bytes 2097168 | tf_op jit(solution)/shard_map/reduce_scatter | solution.py:185
  1520.8 52.3 %reduce-scatter.20.cloned.1.call-done = bf16[1,2048,512]{2,1,0:T(8,128)(2,1)} async-done(((bf16[1,2048,1024]{2,1,0:T(8,128)(2,1)}), bf16[1,2048,512]{2,1,0:T(8,128)(2,1)}) %reduce-scatter.20.cloned.1.call-update) | async-done | bytes 2097168 | tf_op jit(solution)/shard_map/reduce_scatter | solution.py:188
  1589.9 134.0 %reduce-scatter.24.cloned.1.call-done = f32[64,4]{1,0:T(8,128)} async-done(((f32[2048,4]{1,0:T(8,128)}), f32[64,4]{1,0:T(8,128)}) %reduce-scatter.24.cloned.1.call-update) | async-done | bytes 1040
  1725.4 11.8 reduce-scatter.14.cloned.1.call-done
  1738.9 27.2 %reduce-scatter.12.cloned.1.call-done = bf16[64,6144]{1,0:T(8,128)(2,1)} async-done(((bf16[128,6144]{1,0:T(8,128)(2,1)}), bf16[64,6144]{1,0:T(8,128)(2,1)}) %reduce-scatter.12.cloned.1.call-update) | async-done | bytes 786448 | tf_op jit(solution)/shard_map/reduce_scatter | solution.py:273
  (450 shorter events, 265.1 us)
Async XLA Ops:
  8.0 160.8 %all-gather.10.cloned.1.call-start = ((), (), s32[]{:S(2)}) async-start(), calls=%async_computation.14 | async-start | bytes 25952256 | tf_op jit(solution)/shard_map/all_gather | solution.py:87
  8.7 369.9 %all-gather.12.cloned.1.call-start = ((), (), s32[]{:S(2)}) async-start(), calls=%async_computation.15 | async-start | bytes 8650752 | tf_op jit(solution)/shard_map/all_gather | solution.py:88
  81.9 97.1 %copy-start.42 = (f32[2048,1]{0,1:T(1,128)}, f32[2048,1]{0,1:T(1,128)S(1)}, u32[]{:S(2)}) copy-start(f32[2048,1]{0,1:T(1,128)S(1)} %get-tuple-element.255) | copy-start | bytes 24580
  81.9 97.4 %copy-start.46 = (f32[2048,1]{0,1:T(1,128)}, f32[2048,1]{0,1:T(1,128)S(1)}, u32[]{:S(2)}) copy-start(f32[2048,1]{0,1:T(1,128)S(1)} %get-tuple-element.253) | copy-start | bytes 24580
  81.9 97.4 %copy-start.48 = (f32[2048,1]{0,1:T(1,128)}, f32[2048,1]{0,1:T(1,128)S(1)}, u32[]{:S(2)}) copy-start(f32[2048,1]{0,1:T(1,128)S(1)} %get-tuple-element.254) | copy-start | bytes 24580
  82.0 301.6 %copy-start.40 = (f32[2048,1]{0,1:T(1,128)}, f32[2048,1]{0,1:T(1,128)S(1)}, u32[]{:S(2)}) copy-start(f32[2048,1]{0,1:T(1,128)S(1)} %get-tuple-element.252) | copy-start | bytes 24580
  83.2 95.8 %copy-start.56 = (f32[128]{0:T(128)}, f32[128]{0:T(128)S(1)}, u32[]{:S(2)}) copy-start(f32[128]{0:T(128)S(1)} %fusion.106) | copy-start | bytes 1540
  84.2 98.8 %copy-start.34 = (f32[128,128]{1,0:T(8,128)}, f32[128,128]{1,0:T(8,128)S(1)}, u32[]{:S(2)}) copy-start(f32[128,128]{1,0:T(8,128)S(1)} %pad_maximum_fusion.4) | copy-start | bytes 196612
  84.3 98.8 %copy-start.36 = (f32[128,128]{1,0:T(8,128)}, f32[128,128]{1,0:T(8,128)S(1)}, u32[]{:S(2)}) copy-start(f32[128,128]{1,0:T(8,128)S(1)} %pad_maximum_fusion.5) | copy-start | bytes 196612
  185.6 59.2 %all-to-all-start = ((bf16[4,128,16,128]{3,1,0,2:T(8,128)(2,1)}), bf16[4,128,16,128]{3,1,0,2:T(8,128)(2,1)S(1)}, u32[]{:S(2)}, u32[]{:S(2)}) async-start(bf16[4,128,16,128]{3,1,0,2:T(8,128)(2,1)} %pad_maximum_fusion.1), calls=%async_computation | async-start | bytes 4194304 | tf_op jit(solution)/shard_map/all_to_all | solution.py:100
  189.5 56.4 %copy-start.32 = (s32[1,128,8]{2,1,0:T(8,128)}, s32[1,128,8]{2,1,0:T(8,128)S(1)}, u32[]{:S(2)}) copy-start(s32[1,128,8]{2,1,0:T(8,128)S(1)} %copy.186) | copy-start | bytes 12292
  194.9 101.9 %copy-start.54 = (s32[1024,1]{0,1:T(1,128)}, s32[1024,1]{0,1:T(1,128)S(1)}, u32[]{:S(2)}) copy-start(s32[1024,1]{0,1:T(1,128)S(1)} %compare_select_fusion.1) | copy-start | bytes 12292
  245.9 55.3 %copy-start.66 = (bf16[64,16]{0,1:T(8,128)(2,1)S(1)}, bf16[64,16]{0,1:T(8,128)(2,1)}, u32[]{:S(2)}) copy-start(bf16[64,16]{0,1:T(8,128)(2,1)} %param.18) | copy-start | bytes 6148
  263.8 106.5 %copy-start.18 = (bf16[2048,1,128]{2,0,1:T(8,128)(2,1)}, bf16[2048,1,128]{2,0,1:T(8,128)(2,1)S(1)}, u32[]{:S(2)}) copy-start(bf16[2048,1,128]{2,0,1:T(8,128)(2,1)S(1)} %get-tuple-element.492) | copy-start | bytes 1572868
  263.8 106.7 %copy-start.3 = (bf16[2048,1,128]{2,0,1:T(8,128)(2,1)}, bf16[2048,1,128]{2,0,1:T(8,128)(2,1)S(1)}, u32[]{:S(2)}) copy-start(bf16[2048,1,128]{2,0,1:T(8,128)(2,1)S(1)} %get-tuple-element.477) | copy-start | bytes 1572868
  263.8 106.7 %copy-start.13 = (bf16[2048,1,128]{2,0,1:T(8,128)(2,1)}, bf16[2048,1,128]{2,0,1:T(8,128)(2,1)S(1)}, u32[]{:S(2)}) copy-start(bf16[2048,1,128]{2,0,1:T(8,128)(2,1)S(1)} %get-tuple-element.488) | copy-start | bytes 1572868
  263.8 113.9 %copy-start.25 = (bf16[4,512,1,128]{3,1,2,0:T(8,128)(2,1)}, bf16[4,512,1,128]{3,1,2,0:T(8,128)(2,1)S(1)}, u32[]{:S(2)}) copy-start(bf16[4,512,1,128]{3,1,2,0:T(8,128)(2,1)S(1)} %get-tuple-element.111) | copy-start | bytes 1572868
  263.8 106.7 %copy-start.21 = (bf16[1,128,2048]{2,1,0:T(8,128)(2,1)S(1)}, bf16[1,128,2048]{2,1,0:T(8,128)(2,1)}, u32[]{:S(2)}) copy-start(bf16[1,128,2048]{2,1,0:T(8,128)(2,1)} %param.23) | copy-start | bytes 1572868
  266.3 111.4 %all-to-all-start.1 = ((bf16[16,2,8192]{2,1,0:T(2,128)(2,1)}), bf16[16,2,8192]{2,1,0:T(2,128)(2,1)S(1)}, u32[]{:S(2)}, u32[]{:S(2)}) async-start(bf16[16,2,8192]{2,1,0:T(2,128)(2,1)} %reshape.833), calls=%async_computation.1 | async-start | bytes 1048576 | tf_op jit(solution)/shard_map/all_to_all | solution.py:126
  424.7 191.9 %all-to-all-start.2 = ((bf16[2,16,1,80,2048]{4,3,2,0,1:T(8,128)(2,1)}), bf16[2,16,1,80,2048]{4,3,2,0,1:T(8,128)(2,1)}, u32[]{:S(2)}, u32[]{:S(2)}) async-start(bf16[2,16,1,80,2048]{4,3,2,0,1:T(8,128)(2,1)} %pad_maximum_fusion), calls=%async_computation.2 | async-start | bytes 20971520 | tf_op jit(solution)/shard_map/all_to_all | solution.py:144
  429.5 197.2 %all-gather.16.cloned.1.call-start = ((), (), s32[]{:S(2)}) async-start(), calls=%async_computation.17 | async-start | bytes 6291456 | tf_op jit(solution)/shard_map/all_gather | solution.py:149
  430.1 207.2 %all-gather.14.cloned.1.call-start = ((), (), s32[]{:S(2)}) async-start(), calls=%async_computation.16 | async-start | bytes 6291456 | tf_op jit(solution)/shard_map/all_gather | solution.py:148
  430.7 216.9 %all-gather.18.cloned.1.call-start = ((), (), s32[]{:S(2)}) async-start(), calls=%async_computation.18 | async-start | bytes 6291456 | tf_op jit(solution)/shard_map/all_gather | solution.py:150
  743.7 140.8 %all-to-all-start.3 = ((bf16[16,2,81920]{2,1,0:T(2,128)(2,1)}), bf16[16,2,81920]{2,1,0:T(2,128)(2,1)}, u32[]{:S(2)}, u32[]{:S(2)}) async-start(bf16[16,2,81920]{2,1,0:T(2,128)(2,1)} %reshape.835), calls=%async_computation.3 | async-start | bytes 10485760 | tf_op jit(solution)/shard_map/all_to_all | solution.py:159
  880.6 28.0 %copy-start.51 = (s32[128,8,1]{0,1,2:T(8,128)S(1)}, s32[128,8,1]{0,1,2:T(8,128)}, u32[]{:S(2)}) copy-start(s32[128,8,1]{0,1,2:T(8,128)} %get-tuple-element.259) | copy-start | bytes 12292
  880.6 28.0 %copy-start.76 = (s32[2]{0:T(128)S(1)}, s32[2]{0:T(128)}, u32[]{:S(2)}) copy-start(s32[2]{0:T(128)} %constant.156) | copy-start | bytes 28
  880.6 28.0 %copy-start.75 = (s32[2]{0:T(128)S(1)}, s32[2]{0:T(128)}, u32[]{:S(2)}) copy-start(s32[2]{0:T(128)} %constant.159) | copy-start | bytes 28
  880.6 28.3 %copy-start.55 = (s32[1024,1]{0,1:T(1,128)S(1)}, s32[1024,1]{0,1:T(1,128)}, u32[]{:S(2)}) copy-start(s32[1024,1]{0,1:T(1,128)} %copy-done.54) | copy-start | bytes 12292
  880.7 28.3 %copy-start.8 = (f32[128,2048]{1,0:T(8,128)S(1)}, f32[128,2048]{1,0:T(8,128)}, u32[]{:S(2)}) copy-start(f32[128,2048]{1,0:T(8,128)} %copy-done.7) | copy-start | bytes 3145732
  880.7 28.3 %copy-start.41 = (f32[2048,1]{0,1:T(1,128)S(1)}, f32[2048,1]{0,1:T(1,128)}, u32[]{:S(2)}) copy-start(f32[2048,1]{0,1:T(1,128)} %copy-done.40) | copy-start | bytes 24580
  880.7 28.3 %copy-start.59 = (f32[128]{0:T(128)S(1)}, f32[128]{0:T(128)}, u32[]{:S(2)}) copy-start(f32[128]{0:T(128)} %copy-done.58) | copy-start | bytes 1540
  880.7 29.6 %copy-start.61 = (f32[128]{0:T(128)S(1)}, f32[128]{0:T(128)}, u32[]{:S(2)}) copy-start(f32[128]{0:T(128)} %copy-done.60) | copy-start | bytes 1540
  884.5 119.9 %all-to-all-start.4 = ((bf16[16,2,81920]{2,1,0:T(2,128)(2,1)}), bf16[16,2,81920]{2,1,0:T(2,128)(2,1)}, u32[]{:S(2)}, u32[]{:S(2)}) async-start(bf16[16,2,81920]{2,1,0:T(2,128)(2,1)} %reshape.837), calls=%async_computation.4 | async-start | bytes 10485760 | tf_op jit(solution)/shard_map/all_to_all | solution.py:192
  1053.4 55.0 %copy-start.4 = (bf16[2048,1,128]{2,0,1:T(8,128)(2,1)S(1)}, bf16[2048,1,128]{2,0,1:T(8,128)(2,1)}, u32[]{:S(2)}) copy-start(bf16[2048,1,128]{2,0,1:T(8,128)(2,1)} %copy-done.3) | copy-start | bytes 1572868
  1053.4 55.0 %copy-start.14 = (bf16[2048,1,128]{2,0,1:T(8,128)(2,1)S(1)}, bf16[2048,1,128]{2,0,1:T(8,128)(2,1)}, u32[]{:S(2)}) copy-start(bf16[2048,1,128]{2,0,1:T(8,128)(2,1)} %copy-done.13) | copy-start | bytes 1572868
  1054.5 52.8 %all-to-all-start.5 = ((bf16[2,128,16,128]{3,1,0,2:T(8,128)(2,1)}), bf16[2,128,16,128]{3,1,0,2:T(8,128)(2,1)S(1)}, u32[]{:S(2)}, u32[]{:S(2)}) async-start(bf16[2,128,16,128]{3,1,0,2:T(8,128)(2,1)} %pad_maximum_fusion.3), calls=%async_computation.5 | async-start | bytes 2097152 | tf_op jit(solution)/shard_map/all_to_all | solution.py:208
  1078.3 269.0 %all-gather.22.cloned.1.call-start = ((), (), s32[]{:S(2)}) async-start(), calls=%async_computation.21 | async-start | bytes 8912896 | tf_op jit(solution)/shard_map/all_gather | solution.py:263
  1079.1 323.0 %all-gather.20.cloned.1.call-start = ((), (), s32[]{:S(2)}) async-start(), calls=%async_computation.19 | async-start | bytes 26738688 | tf_op jit(solution)/shard_map/all_gather | solution.py:257
  1273.6 186.0 %reduce-scatter.16.cloned.1.call-start = ((), (), s32[]{:S(2)}) async-start(), calls=%async_computation.23 | async-start | bytes 6291456 | tf_op jit(solution)/shard_map/reduce_scatter | solution.py:182
  1284.2 232.4 %reduce-scatter.18.cloned.1.call-start = ((), (), s32[]{:S(2)}) async-start(), calls=%async_computation.24 | async-start | bytes 6291456 | tf_op jit(solution)/shard_map/reduce_scatter | solution.py:185
  1295.9 277.3 %reduce-scatter.20.cloned.1.call-start = ((), (), s32[]{:S(2)}) async-start(), calls=%async_computation.25 | async-start | bytes 6291456 | tf_op jit(solution)/shard_map/reduce_scatter | solution.py:188
  1308.0 23.2 %copy-start.43 = (f32[2048,1]{0,1:T(1,128)S(1)}, f32[2048,1]{0,1:T(1,128)}, u32[]{:S(2)}) copy-start(f32[2048,1]{0,1:T(1,128)} %copy-done.42) | copy-start | bytes 24580
  1308.0 23.2 %copy-start.57 = (f32[128]{0:T(128)S(1)}, f32[128]{0:T(128)}, u32[]{:S(2)}) copy-start(f32[128]{0:T(128)} %copy-done.56) | copy-start | bytes 1540
  1308.0 277.1 %reduce-scatter.22.cloned.1.call-start = ((), (), s32[]{:S(2)}) async-start(), calls=%async_computation.26 | async-start | bytes 49152
  1331.1 392.9 %reduce-scatter.24.cloned.1.call-start = ((), (), s32[]{:S(2)}) async-start(), calls=%async_computation.27 | async-start | bytes 1081344
  1347.3 389.9 %reduce-scatter.14.cloned.1.call-start = ((), (), s32[]{:S(2)}) async-start(), calls=%async_computation.22 | async-start | bytes 786432 | tf_op jit(solution)/shard_map/reduce_scatter | solution.py:276
  1347.4 54.7 %copy-start.27 = (bf16[1,16,128,1,128]{4,2,1,3,0:T(8,128)(2,1)S(1)}, bf16[1,16,128,1,128]{4,2,1,3,0:T(8,128)(2,1)}, u32[]{:S(2)}) copy-start(bf16[1,16,128,1,128]{4,2,1,3,0:T(8,128)(2,1)} %get-tuple-element.228) | copy-start | bytes 1572868
  1353.0 413.1 %reduce-scatter.12.cloned.1.call-start = ((), (), s32[]{:S(2)}) async-start(), calls=%async_computation.20 | async-start | bytes 2359296 | tf_op jit(solution)/shard_map/reduce_scatter | solution.py:273
  (70 other events, 440.8 us)
Sparse Core Ops, SparseCore 0:
  11.7 157.0 all-gather.9
  171.8 102.4 all-gather.11
Sparse Core Ops, SparseCore 1:
  431.5 56.9 all-gather.15
  489.9 56.6 all-gather.13
  547.9 56.6 all-gather.17
  1081.3 84.7 all-gather.21
  1273.7 128.3 all-gather.19
  1404.9 54.6 reduce-scatter.15
  1462.3 54.3 reduce-scatter.17
  1518.8 54.3 reduce-scatter.19
  1575.2 9.9 reduce-scatter.21
  1587.4 136.5 reduce-scatter.23
  1726.7 10.4 reduce-scatter.13
  1740.0 26.1 reduce-scatter.11
where the time goes:
time: 1790 us; the launch traced here: 1780 us
  waiting for transfers between devices  771 us (43%)
  local copies, waits for them, and re-layouts  254 us (14%)
  blocking collectives  226 us (13%)
  matrix products  215 us (12%)
  other arithmetic  146 us (8%)
  starting transfers between devices  133 us (7%)
    all_to_all x1, waiting for transfers between devices, shards(): lax.all_to_all(outgoing, 'seq', split_axis=1, concat_axis=3, tiled=True)  185 us
    unnamed x16, waiting for transfers between devices  141 us
    unnamed x182, local copies, waits for them, and re-layouts  87.2 us
    all_gather x1, waiting for transfers between devices, shards(): lax.all_gather(w_qkv, ('seq', 'fsdp'), axis=0, tiled=True)  83.2 us
    unnamed x11, other arithmetic  73.5 us
    all_gather x1, blocking collectives, shards(): lax.all_gather(norm_gains, ('seq', 'fsdp'), axis=0, tiled=True)  72.3 us
    all_gather x1, blocking collectives, shards(): lax.all_gather(w_router, ('seq', 'fsdp'), axis=0, tiled=True)  68.7 us
    all_to_all x1, blocking collectives, shards(): lax.all_to_all(d_heads, 'seq', split_axis=1, concat_axis=2, tiled=True)  63.4 us
  transfers between devices with their start and end apart: 20, of which 14 were waited for; matrix products, arithmetic and copies ran while one was open for 23% of the time, Pallas kernels for 0%

commit v1 on v0

v1 whole, which is shorter than its diff:
```python
from functools import partial

import jax
import jax.numpy as jnp
from jax import lax
from jax.experimental import pallas as pl
from jax.experimental.pallas import tpu as pltpu
from jax.sharding import PartitionSpec as P

HEADS = 16
TOPK = 8
EPS = 1e-05
NEG = -1e30
F32 = jnp.float32
BF16 = jnp.bfloat16
MESH = pl.DeviceIdType.MESH
PIECES = 2
ANY = pl.BlockSpec(memory_space=pl.ANY)
VMEM = pl.BlockSpec(memory_space=pltpu.VMEM)
MATMUL = (((1,), (0,)), ((), ()))
BY_LAST = (((1,), (1,)), ((), ()))
BY_FIRST = (((0,), (0,)), ((), ()))


def dot(a, b, dims):
    return lax.dot_general(a, b, dims, preferred_element_type=F32)


class Ring:
    def __init__(self, n, f):
        self.n, self.f = n, f
        self.chips = n // 2
        self.half = self.chips // 2
        self.pairs_minor = f == 2
        self.me = lax.axis_index("seq")
        self.mine = lax.axis_index("fsdp")
        chip = self.me // 2
        self.core = self.me % 2
        if self.pairs_minor:
            along, side = chip // 2, chip % 2
        else:
            along, side = chip % self.half, chip // self.half
        self.pos = along + side * (self.chips - 1 - 2 * along)
        self.right = self.at(self.pos + 1)
        self.left = self.at(self.pos + self.chips - 1)
        self.mate = self.me + 1 - 2 * self.core

    def at(self, place, other=False):
        place = lax.rem(place + self.chips, self.chips)
        side = place // self.half
        along = place + side * (self.chips - 1 - 2 * place)
        chip = along * 2 + side if self.pairs_minor else side * self.half + along
        core = 1 - self.core if other else self.core
        return chip * 2 + core

    def peer(self, step):
        return lax.rem(self.me + step, self.n)

    def beside(self, step):
        return lax.rem(self.mine + step, self.f)


def greet(ring, everyone, beside):
    barrier = pltpu.get_barrier_semaphore()
    count = 0
    if everyone:
        for step in range(1, ring.n):
            pl.semaphore_signal(
                barrier, inc=1, device_id={"seq": ring.peer(step)}, device_id_type=MESH
            )
        count += ring.n - 1
    else:
        for other in (ring.right, ring.left, ring.mate):
            pl.semaphore_signal(barrier, inc=1, device_id={"seq": other}, device_id_type=MESH)
        count += 3
    if beside:
        for step in range(1, ring.f):
            pl.semaphore_signal(
                barrier, inc=1, device_id={"fsdp": ring.beside(step)}, device_id_type=MESH
            )
        count += ring.f - 1
    pl.semaphore_wait(barrier, count)


def remote(src, dst, send, recv, where):
    return pltpu.make_async_remote_copy(
        src_ref=src,
        dst_ref=dst,
        send_sem=send,
        recv_sem=recv,
        device_id=where,
        device_id_type=MESH,
    )


class Gather:
    def __init__(self, ring, own, out, sems):
        self.ring, self.own, self.out = ring, own, out
        self.send, self.recv, self.mate_send, self.mate_recv, self.keep = sems
        self.piece = own.shape[0] // (2 * PIECES)

    @staticmethod
    def semaphores(n):
        hops = n // 2 - 1
        kind = pltpu.SemaphoreType.DMA
        return [
            kind((2, hops, PIECES)),
            kind((2, hops, PIECES)),
            kind((2, hops + 1, PIECES)),
            kind((2, hops + 1, PIECES)),
            kind((1,)),
        ]

    def rows(self, way, s):
        return pl.ds((way * PIECES + s) * self.piece, self.piece)

    def hop(self, way, step, s, first):
        ring = self.ring
        chunk = ring.at(ring.pos - step if way == 0 else ring.pos + step)
        rows = self.rows(way, s)
        there = self.out.at[chunk, rows]
        return remote(
            self.own.at[rows] if first else there,
            there,
            self.send.at[way, step, s],
            self.recv.at[way, step, s],
            {"seq": ring.right if way == 0 else ring.left},
        )

    def share(self, way, step, s, first):
        ring = self.ring
        chunk = ring.at(ring.pos - step if way == 0 else ring.pos + step)
        rows = self.rows(way, s)
        there = self.out.at[chunk, rows]
        return remote(
            self.own.at[rows] if first else there,
            there,
            self.mate_send.at[way, step, s],
            self.mate_recv.at[way, step, s],
            {"seq": ring.mate},
        )

    def local(self):
        return pltpu.make_async_copy(self.own, self.out.at[self.ring.me], self.keep.at[0])

    def begin(self):
        for s in range(PIECES):
            for way in (0, 1):
                self.hop(way, 0, s, True).start()
        for s in range(PIECES):
            for way in (0, 1):
                self.share(way, 0, s, True).start()
        self.local().start()

    def run(self):
        hops = self.ring.chips - 1

        def body(step, carry):
            for s in range(PIECES):
                for way in (0, 1):
                    self.hop(way, step - 1, s, False).wait_recv()
                    self.hop(way, step, s, False).start()
                    self.share(way, step, s, False).start()
            return carry

        lax.fori_loop(1, hops, body, 0)
        for s in range(PIECES):
            for way in (0, 1):
                self.hop(way, hops - 1, s, False).wait_recv()
                self.share(way, hops, s, False).start()

    def finish(self):
        hops = self.ring.chips - 1

        def body(step, carry):
            for s in range(PIECES):
                for way in (0, 1):
                    self.hop(way, step, s, False).wait_send()
                    self.share(way, step, s, False).wait()
            return carry

        lax.fori_loop(0, hops, body, 0)
        for s in range(PIECES):
            for way in (0, 1):
                self.share(way, hops, s, False).wait()
        self.local().wait()


class Scatter:
    def __init__(self, ring, part, tok, width, buffers, sems):
        self.ring, self.part, self.tok, self.width = ring, part, tok, width
        self.mate_out, self.mate_in, self.own, self.going, self.coming = buffers
        self.send, self.recv, self.mate_send, self.mate_recv = sems
        self.piece = tok // (2 * PIECES)

    @staticmethod
    def buffers(n, tok, width):
        chips = n // 2
        return [
            pltpu.VMEM((chips, tok, width), BF16),
            pltpu.VMEM((chips, tok, width), BF16),
            pltpu.VMEM((2, tok, width), F32),
            pltpu.VMEM((chips - 1, tok, width), BF16),
            pltpu.VMEM((chips - 1, tok, width), BF16),
        ]

    @staticmethod
    def semaphores(n):
        chips = n // 2
        kind = pltpu.SemaphoreType.DMA
        return [
            kind((2, chips - 1, PIECES)),
            kind((2, chips - 1, PIECES)),
            kind((chips,)),
            kind((chips,)),
        ]

    def rows(self, way, s):
        return pl.ds((way * PIECES + s) * self.piece, self.piece)

    def exchange(self, i):
        return remote(
            self.mate_out.at[i],
            self.mate_in.at[i],
            self.mate_send.at[i],
            self.mate_recv.at[i],
            {"seq": self.ring.mate},
        )

    def hop(self, way, i, s):
        ring = self.ring
        rows = self.rows(way, s)
        return remote(
            self.going.at[i, rows],
            self.coming.at[i, rows],
            self.send.at[way, i, s],
            self.recv.at[way, i, s],
            {"seq": ring.right if way == 0 else ring.left},
        )

    def produce(self, i):
        ring = self.ring
        half = self.tok // 2
        places = (ring.pos - 1 - i, ring.pos + 1 + i)
        for way in (0, 1):
            chunk = ring.at(places[way] + ring.chips, True)
            self.part(chunk, way, self.mate_out, i)
        self.exchange(i).start()
        slot = lax.rem(i, 2)
        for way in (0, 1):
            chunk = ring.at(places[way] + ring.chips)
            self.part(chunk, way, self.own, slot)

    def step(self, i, first):
        self.exchange(i).wait_recv()
        slot = lax.rem(i, 2)
        for s in range(PIECES):
            for way in (0, 1):
                rows = self.rows(way, s)
                value = self.own[slot, rows] + self.mate_in[i, rows].astype(F32)
                if not first:
                    self.hop(way, i - 1, s).wait_recv()
                    value = value + self.coming[i - 1, rows].astype(F32)
                self.going[i, rows] = value.astype(BF16)
                self.hop(way, i, s).start()

    def run(self, finish):
        last = self.ring.chips - 1
        self.produce(0)
        self.produce(1)
        self.step(0, True)

        def body(i, carry):
            self.produce(i + 1)
            self.step(i, False)
            return carry

        lax.fori_loop(1, last, body, 0)
        self.exchange(last).wait_recv()
        slot = last % 2
        for s in range(PIECES):
            for way in (0, 1):
                rows = self.rows(way, s)
                self.hop(way, last - 1, s).wait_recv()
                value = self.own[slot, rows] + self.mate_in[last, rows].astype(F32)
                value = value + self.coming[last - 1, rows].astype(F32)
                finish(rows, value)

    def close(self):
        last = self.ring.chips - 1

        def body(i, carry):
            self.exchange(i).wait_send()
            for s in range(PIECES):
                for way in (0, 1):
                    self.hop(way, i, s).wait_send()
            return carry

        lax.fori_loop(0, last, body, 0)
        self.exchange(last).wait_send()


def first_kernel(n, f, *refs):
    own, by_head, out_rows, small, routes = refs[:5]
    own_all, w_head, w_out_head, small_all, routes_all = refs[5:10]
    sems = refs[10:15]
    send, recv, beside_send, beside_recv, keep, wide_send, wide_recv = refs[15:]
    ring = Ring(n, f)
    greet(ring, True, True)
    gather = Gather(ring, own, own_all, sems)

    def push(kind, step):
        there = ring.peer(step)
        source, target = [
            (by_head.at[there], w_head.at[ring.me, ring.mine]),
            (small, small_all.at[ring.me, ring.mine]),
            (routes, routes_all.at[ring.me]),
        ][kind]
        return remote(
            source, target, send.at[kind, step], recv.at[kind, step], {"seq": there}
        )

    def wide(step):
        return remote(
            out_rows,
            w_out_head.at[ring.mine],
            wide_send.at[step],
            wide_recv.at[step],
            {"fsdp": ring.beside(step)},
        )

    def aside(kind, step, over, first):
        origin = lax.rem(ring.me + n - step, n)
        block = [w_head, small_all][kind].at[origin, ring.mine]
        source = [by_head.at[ring.me], small][kind] if first else block
        return remote(
            source,
            block,
            beside_send.at[kind, step, over],
            beside_recv.at[kind, step, over],
            {"fsdp": ring.beside(over)},
        )

    gather.begin()
    copies = [
        pltpu.make_async_copy(by_head.at[ring.me], w_head.at[ring.me, ring.mine], keep.at[0]),
        pltpu.make_async_copy(small, small_all.at[ring.me, ring.mine], keep.at[1]),
        pltpu.make_async_copy(routes, routes_all.at[ring.me], keep.at[2]),
        pltpu.make_async_copy(out_rows, w_out_head.at[ring.mine], keep.at[3]),
    ]
    for copy in copies:
        copy.start()
    for step in range(1, n):
        for kind in (1, 0, 2):
            push(kind, step).start()
    for over in range(1, f):
        aside(1, 0, over, True).start()
        aside(0, 0, over, True).start()
        wide(over).start()
    for step in range(1, n):
        for kind in (1, 0):
            push(kind, step).wait_recv()
            for over in range(1, f):
                aside(kind, step, over, False).start()
    gather.run()
    gather.finish()
    for step in range(1, n):
        push(2, step).wait_recv()
        for kind in (0, 1, 2):
            push(kind, step).wait_send()
    for step in range(n):
        for kind in (0, 1):
            for over in range(1, f):
                aside(kind, step, over, False).wait()
    for over in range(1, f):
        wide(over).wait()
    for copy in copies:
        copy.wait()


def first_gather(n, f, own, by_head, out_rows, small, routes):
    tok, width = own.shape
    kind = pltpu.SemaphoreType.DMA
    shape = jax.ShapeDtypeStruct
    return pl.pallas_call(
        partial(first_kernel, n, f),
        out_shape=[
            shape((n, tok, width), BF16),
            shape((n, f) + by_head.shape[1:], BF16),
            shape((f,) + out_rows.shape, BF16),
            shape((n, f) + small.shape, BF16),
            shape((n,) + routes.shape, jnp.int32),
        ],
        in_specs=[VMEM] * 5,
        out_specs=[ANY] * 5,
        scratch_shapes=Gather.semaphores(n)
        + [kind((3, n)), kind((3, n)), kind((2, n, f)), kind((2, n, f)), kind((4,))]
        + [kind((f,)), kind((f,))],
        compiler_params=pltpu.CompilerParams(
            collective_id=0, has_side_effects=True, vmem_limit_bytes=32 << 20
        ),
        name="first_gather",
    )(own, by_head, out_rows, small, routes)


def spread_kernel(n, f, block, out, send, recv, keep):
    ring = Ring(n, f)
    greet(ring, True, False)

    def push(step):
        return remote(
            block, out.at[ring.me], send.at[step], recv.at[step], {"seq": ring.peer(step)}
        )

    local = pltpu.make_async_copy(block, out.at[ring.me], keep.at[0])
    for step in range(1, n):
        push(step).start()
    local.start()
    for step in range(1, n):
        push(step).wait()
    local.wait()


def spread(n, f, block, ident):
    kind = pltpu.SemaphoreType.DMA
    return pl.pallas_call(
        partial(spread_kernel, n, f),
        out_shape=jax.ShapeDtypeStruct((n,) + block.shape, block.dtype),
        in_specs=[VMEM],
        out_specs=VMEM,
        scratch_shapes=[kind((n,)), kind((n,)), kind((1,))],
        compiler_params=pltpu.CompilerParams(
            collective_id=ident, has_side_effects=True, vmem_limit_bytes=16 << 20
        ),
        name="spread",
    )(block)


def blocks_of(length):
    block = min(512, length)
    return block, length // block


def attention_kernel(factor, q_ref, k_ref, v_ref, out_ref, exact_ref, sums_ref):
    length, head = q_ref.shape
    block, count = blocks_of(length)
    rows = lax.broadcasted_iota(jnp.int32, (block, block), 0)
    cols = lax.broadcasted_iota(jnp.int32, (block, block), 1)

    def outer(i, carry):
        here = pl.ds(pl.multiple_of(i * block, block), block)
        part = q_ref[here, :]

        def inner(j, state, masked):
            top, total, acc = state
            there = pl.ds(pl.multiple_of(j * block, block), block)
            scores = dot(part, k_ref[there, :], BY_LAST) * factor
            if masked:
                scores = jnp.where(cols <= rows, scores, NEG)
            new = jnp.maximum(top, jnp.max(scores, -1, keepdims=True))
            scale = jnp.exp(top - new)
            expd = jnp.exp(scores - new)
            total = total * scale + jnp.sum(expd, -1, keepdims=True)
            acc = acc * scale + dot(expd.astype(BF16), v_ref[there, :], MATMUL)
            return new, total, acc

        state = (
            jnp.full((block, 1), NEG, F32),
            jnp.zeros((block, 1), F32),
            jnp.zeros((block, head), F32),
        )
        state = lax.fori_loop(0, i, lambda j, s: inner(j, s, False), state)
        top, total, acc = inner(i, state, True)
        exact = acc / total
        exact_ref[here, :] = exact
        out_ref[here, :] = exact.astype(BF16)
        sums_ref[here, :] = top + jnp.log(total)
        return carry

    lax.fori_loop(0, count, outer, 0)


def attention(queries, keys, values, factor):
    length, head = queries.shape
    shape = jax.ShapeDtypeStruct
    return pl.pallas_call(
        partial(attention_kernel, factor),
        out_shape=[
            shape((length, head), BF16),
            shape((length, head), F32),
            shape((length, 1), F32),
        ],
        in_specs=[VMEM] * 3,
        out_specs=[VMEM] * 3,
        compiler_params=pltpu.CompilerParams(vmem_limit_bytes=32 << 20),
        cost_estimate=pl.CostEstimate(
            flops=2 * length * length * head,
            transcendentals=length * length // 2,
            bytes_accessed=8 * length * head,
        ),
        name="attention",
    )(queries, keys, values)


def attention_back_kernel(
    factor, q_ref, k_ref, v_ref, d_ref, sums_ref, delta_ref, dq_ref, dk_ref, dv_ref
):
    length, head = q_ref.shape
    block, count = blocks_of(length)
    rows = lax.broadcasted_iota(jnp.int32, (block, block), 0)
    cols = lax.broadcasted_iota(jnp.int32, (block, block), 1)
    dq_ref[...] = jnp.zeros_like(dq_ref)

    def outer(j, carry):
        there = pl.ds(pl.multiple_of(j * block, block), block)
        keys = k_ref[there, :]
        values = v_ref[there, :]

        def inner(i, state, masked):
            d_keys, d_values = state
            here = pl.ds(pl.multiple_of(i * block, block), block)
            part = q_ref[here, :]
            d_part = d_ref[here, :]
            scores = dot(keys, part, BY_LAST) * factor
            if masked:
                scores = jnp.where(rows <= cols, scores, NEG)
            probs = jnp.exp(scores - sums_ref[:, here])
            d_probs = dot(values, d_part, BY_LAST)
            d_scores = (probs * (d_probs - delta_ref[:, here])).astype(BF16)
            d_values = d_values + dot(probs.astype(BF16), d_part, MATMUL)
            d_keys = d_keys + dot(d_scores, part, MATMUL)
            dq_ref[here, :] += dot(d_scores, keys, BY_FIRST)
            return d_keys, d_values

        zero = jnp.zeros((block, head), F32)
        state = inner(j, (zero, zero), True)
        state = lax.fori_loop(j + 1, count, lambda i, s: inner(i, s, False), state)
        dk_ref[there, :] = state[0] * factor
        dv_ref[there, :] = state[1]
        return carry

    lax.fori_loop(0, count, outer, 0)
    dq_ref[...] = dq_ref[...] * factor


def attention_back(queries, keys, values, d_out, sums, delta, factor):
    length, head = queries.shape
    shape = jax.ShapeDtypeStruct((length, head), F32)
    return pl.pallas_call(
        partial(attention_back_kernel, factor),
        out_shape=[shape] * 3,
        in_specs=[VMEM] * 6,
        out_specs=[VMEM] * 3,
        compiler_params=pltpu.CompilerParams(vmem_limit_bytes=32 << 20),
        cost_estimate=pl.CostEstimate(
            flops=5 * length * length * head,
            transcendentals=length * length // 2,
            bytes_accessed=20 * length * head,
        ),
        name="attention_back",
    )(queries, keys, values, d_out, sums, delta)


def wide_store(target, slot, rows, left, right, dims):
    width = target.shape[-1]
    tile = min(512, width)
    for start in range(0, width, tile):
        cols = slice(start, start + tile)
        other = right[cols, :] if dims == BY_LAST else right[:, cols]
        target[slot, rows, cols] = dot(left, other, dims).astype(target.dtype)


def middle_kernel(n, f, *refs):
    attended, w_out, tokens, gain, router, routes = refs[:6]
    middle, hidden_all, probs_ref, weights_here = refs[6:10]
    hidden, outgoing = refs[10:12]
    buffers, scatter_sems = refs[12:17], refs[17:21]
    gather_sems = refs[21:26]
    send, recv, keep = refs[26:]
    ring = Ring(n, f)
    tok, width = tokens.shape
    half = tok // 2
    greet(ring, True, False)

    def part(chunk, way, target, slot):
        rows = pl.ds(way * half, half)
        wide_store(target, slot, rows, attended[chunk, rows, :], w_out, MATMUL)

    scatter = Scatter(ring, part, tok, width, buffers, scatter_sems)

    def finish(rows, value):
        value = tokens[rows, :].astype(F32) + value
        middle[rows, :] = value
        inverse = lax.rsqrt(jnp.mean(value * value, -1, keepdims=True) + EPS)
        hidden[rows, :] = (value * inverse * gain[...]).astype(BF16)

    scatter.run(finish)
    gather = Gather(ring, hidden, hidden_all, gather_sems)
    gather.begin()
    logits = dot(router[...], hidden[...], BY_LAST)
    expd = jnp.exp(logits - jnp.max(logits, 0, keepdims=True))
    probs = expd / jnp.sum(expd, 0, keepdims=True)
    probs_ref[...] = probs
    experts = lax.broadcasted_iota(jnp.int32, probs.shape, 0)
    named = jnp.zeros(probs.shape, F32)
    for k in range(routes.shape[0]):
        named = named + jnp.where(routes[k : k + 1, :] == experts, 1.0, 0.0)
    weights = probs * named
    for e in range(n):
        outgoing[e] = jnp.broadcast_to(weights[e : e + 1, :], (8, tok))

    def push(step):
        there = ring.peer(step)
        return remote(
            outgoing.at[there],
            weights_here.at[ring.me],
            send.at[step],
            recv.at[step],
            {"seq": there},
        )

    local = pltpu.make_async_copy(outgoing.at[ring.me], weights_here.at[ring.me], keep.at[0])
    for step in range(1, n):
        push(step).start()
    local.start()
    gather.run()
    scatter.close()
    gather.finish()
    for step in range(1, n):
        push(step).wait()
    local.wait()


def middle_stage(n, f, attended, w_out, tokens, gain, router, routes):
    tok, width = tokens.shape
    experts = router.shape[0]
    kind = pltpu.SemaphoreType.DMA
    shape = jax.ShapeDtypeStruct
    return pl.pallas_call(
        partial(middle_kernel, n, f),
        out_shape=[
            shape((tok, width), F32),
            shape((n, tok, width), BF16),
            shape((experts, tok), F32),
            shape((n, 8, tok), F32),
        ],
        in_specs=[VMEM] * 6,
        out_specs=[VMEM, ANY, VMEM, ANY],
        scratch_shapes=[pltpu.VMEM((tok, width), BF16), pltpu.VMEM((n, 8, tok), F32)]
        + Scatter.buffers(n, tok, width)
        + Scatter.semaphores(n)
        + Gather.semaphores(n)
        + [kind((n,)), kind((n,)), kind((1,))],
        compiler_params=pltpu.CompilerParams(
            collective_id=1, has_side_effects=True, vmem_limit_bytes=56 << 20
        ),
        name="middle_stage",
    )(attended, w_out, tokens, gain, router, routes)


def back_kernel(n, f, *refs):
    pick, d_rows, d_weight, probs, router, upstream, middle, gain = refs[:8]
    d_middle, d_attn_all, d_logits_all, gain_two = refs[8:12]
    d_attn, d_logits, arrived = refs[12:15]
    buffers, scatter_sems = refs[15:20], refs[20:24]
    gather_sems = refs[24:29]
    send, recv, keep = refs[29:]
    ring = Ring(n, f)
    tok, width = upstream.shape
    half = tok // 2
    greet(ring, True, False)

    def push(step):
        there = ring.peer(step)
        return remote(
            d_weight.at[there],
            arrived.at[ring.me],
            send.at[0, step],
            recv.at[0, step],
            {"seq": there},
        )

    local = pltpu.make_async_copy(d_weight.at[ring.me], arrived.at[ring.me], keep.at[0])
    for step in range(1, n):
        push(step).start()
    local.start()

    def part(chunk, way, target, slot):
        rows = pl.ds(way * half, half)
        wide_store(target, slot, rows, pick[chunk, rows, :], d_rows.at[chunk], MATMUL)

    scatter = Scatter(ring, part, tok, width, buffers, scatter_sems)

    def finish(rows, value):
        d_middle[rows, :] = value

    scatter.run(finish)
    for step in range(1, n):
        push(step).wait()
    local.wait()
    gate = probs[...]
    d_gate = jnp.concatenate([arrived[e, 0:1, :] for e in range(n)], 0)
    d_gate = gate * (d_gate - jnp.sum(gate * d_gate, 0, keepdims=True))
    d_logits[...] = d_gate.astype(BF16)
    d_hidden = d_middle[...] + dot(d_gate.astype(BF16), router[...], BY_FIRST)
    value = middle[...]
    inverse = lax.rsqrt(jnp.mean(value * value, -1, keepdims=True) + EPS)
    inner = jnp.mean(value * gain[...] * d_hidden, -1, keepdims=True)
    gain_two[...] = jnp.sum(value * inverse * d_hidden, 0, keepdims=True)
    d_value = inverse * gain[...] * d_hidden - value * (inverse * inverse * inverse) * inner
    d_value = upstream[...].astype(F32) + d_value
    d_middle[...] = d_value
    d_attn[...] = d_value.astype(BF16)
    gather = Gather(ring, d_attn, d_attn_all, gather_sems)
    gather.begin()

    def publish(step):
        return remote(
            d_logits,
            d_logits_all.at[ring.me],
            send.at[1, step],
            recv.at[1, step],
            {"seq": ring.peer(step)},
        )

    kept = pltpu.make_async_copy(d_logits, d_logits_all.at[ring.me], keep.at[1])
    for step in range(1, n):
        publish(step).start()
    kept.start()
    gather.run()
    scatter.close()
    gather.finish()
    for step in range(1, n):
        publish(step).wait()
    kept.wait()


def back_stage(n, f, pick, d_rows, d_weight, probs, router, upstream, middle, gain):
    tok, width = upstream.shape
    experts = router.shape[0]
    kind = pltpu.SemaphoreType.DMA
    shape = jax.ShapeDtypeStruct
    return pl.pallas_call(
        partial(back_kernel, n, f),
        out_shape=[
            shape((tok, width), F32),
            shape((n, tok, width), BF16),
            shape((n, experts, tok), BF16),
            shape((1, width), F32),
        ],
        in_specs=[VMEM] * 8,
        out_specs=[VMEM, ANY, ANY, VMEM],
        scratch_shapes=[
            pltpu.VMEM((tok, width), BF16),
            pltpu.VMEM((experts, tok), BF16),
            pltpu.VMEM((n, 8, tok), F32),
        ]
        + Scatter.buffers(n, tok, width)
        + Scatter.semaphores(n)
        + Gather.semaphores(n)
        + [kind((2, n)), kind((2, n)), kind((2,))],
        compiler_params=pltpu.CompilerParams(
            collective_id=2, has_side_effects=True, vmem_limit_bytes=60 << 20
        ),
        name="back_stage",
    )(pick, d_rows, d_weight, probs, router, upstream, middle, gain)


def result_kernel(n, f, *refs):
    pick, produced, weights, middle = refs[:4]
    result = refs[4]
    buffers, scatter_sems = refs[5:10], refs[10:14]
    ring = Ring(n, f)
    tok, width = middle.shape
    half = tok // 2
    greet(ring, False, False)

    def part(chunk, way, target, slot):
        rows = pl.ds(way * half, half)
        tile = min(512, width)
        for start in range(0, width, tile):
            cols = slice(start, start + tile)
            value = dot(pick[chunk, rows, :], produced[chunk, :, cols], MATMUL)
            target[slot, rows, cols] = (value * weights[chunk, rows, :]).astype(target.dtype)

    scatter = Scatter(ring, part, tok, width, buffers, scatter_sems)

    def finish(rows, value):
        result[rows, :] = (middle[rows, :] + value).astype(BF16)

    scatter.run(finish)
    scatter.close()


def result_stage(n, f, pick, produced, weights, middle):
    tok, width = middle.shape
    return pl.pallas_call(
        partial(result_kernel, n, f),
        out_shape=jax.ShapeDtypeStruct((tok, width), BF16),
        in_specs=[VMEM] * 4,
        out_specs=VMEM,
        scratch_shapes=Scatter.buffers(n, tok, width) + Scatter.semaphores(n),
        compiler_params=pltpu.CompilerParams(
            collective_id=3, has_side_effects=True, vmem_limit_bytes=56 << 20
        ),
        name="result_stage",
    )(pick, produced, weights, middle)


def last_kernel(n, f, *refs):
    d_mixed, w_head, qkv_part, tokens, gain, d_middle, gain_two, gain_head = refs[:8]
    d_inputs, qkv_rows, gains_out = refs[8:11]
    beside_rows, summed, gain_rows, gain_in, gain_side = refs[11:16]
    buffers, scatter_sems = refs[16:21], refs[21:25]
    side_send, side_recv, send, recv, keep = refs[25:]
    ring = Ring(n, f)
    tok, width = tokens.shape
    half = tok // 2
    slice_width = width // n
    greet(ring, True, True)

    def side(step):
        there = ring.beside(step)
        return remote(
            qkv_part.at[there],
            beside_rows.at[step - 1],
            side_send.at[0, step],
            side_recv.at[0, step],
            {"fsdp": there},
        )

    for step in range(1, f):
        side(step).start()

    def part(chunk, way, target, slot):
        rows = pl.ds(way * half, half)
        wide_store(target, slot, rows, d_mixed[chunk, rows, :], w_head, BY_LAST)

    scatter = Scatter(ring, part, tok, width, buffers, scatter_sems)

    def finish(rows, value):
        d_inputs[rows, :] = value

    def push(step):
        there = ring.peer(step)
        return remote(
            summed.at[there],
            qkv_rows.at[ring.me],
            send.at[0, step],
            recv.at[0, step],
            {"seq": there},
        )

    local = pltpu.make_async_copy(summed.at[ring.me], qkv_rows.at[ring.me], keep.at[0])
    for step in range(1, f):
        side(step).wait_recv()
    for block in range(n):
        value = qkv_part[ring.mine, block].astype(F32)
        for step in range(1, f):
            value = value + beside_rows[step - 1, block].astype(F32)
        summed[block] = value.astype(BF16)
    for step in range(1, n):
        push(step).start()
    local.start()
    scatter.run(finish)
    value = tokens[...].astype(F32)
    grad = d_inputs[...]
    inverse = lax.rsqrt(jnp.mean(value * value, -1, keepdims=True) + EPS)
    inner = jnp.mean(value * gain[...] * grad, -1, keepdims=True)
    gain_rows[...] = jnp.zeros_like(gain_rows)
    gain_rows[0:1, :] = jnp.sum(value * inverse * grad, 0, keepdims=True)
    gain_rows[1:2, :] = gain_two[...]

    def gains(step):
        there = ring.peer(step)
        cols = pl.ds(pl.multiple_of(there * slice_width, slice_width), slice_width)
        return remote(
            gain_rows.at[:, cols],
            gain_in.at[ring.me],
            send.at[1, step],
            recv.at[1, step],
            {"seq": there},
        )

    mine = pl.ds(pl.multiple_of(ring.me * slice_width, slice_width), slice_width)
    kept = pltpu.make_async_copy(gain_rows.at[:, mine], gain_in.at[ring.me], keep.at[1])
    for step in range(1, n):
        gains(step).start()
    kept.start()
    d_value = inverse * gain[...] * grad - value * (inverse * inverse * inverse) * inner
    d_inputs[...] = d_middle[...] + d_value
    for step in range(1, n):
        gains(step).wait()
    kept.wait()
    total = gain_head[...]
    for device in range(n):
        total = total + gain_in[device]
    gain_side[0] = total

    def sums(step):
        return remote(
            gain_side.at[0],
            gain_side.at[step],
            side_send.at[1, step],
            side_recv.at[1, step],
            {"fsdp": ring.beside(step)},
        )

    for step in range(1, f):
        sums(step).start()
    for step in range(1, f):
        sums(step).wait()
        total = total + gain_side[step]
    gains_out[...] = total
    scatter.close()
    for step in range(1, f):
        side(step).wait_send()
    for step in range(1, n):
        push(step).wait()
    local.wait()


def last_stage(n, f, d_mixed, w_head, qkv_part, tokens, gain, d_middle, gain_two, gain_head):
    tok, width = tokens.shape
    rows, across = qkv_part.shape[2:]
    kind = pltpu.SemaphoreType.DMA
    shape = jax.ShapeDtypeStruct
    return pl.pallas_call(
        partial(last_kernel, n, f),
        out_shape=[
            shape((tok, width), F32),
            shape((n, rows, across), BF16),
            shape((8, width // n), F32),
        ],
        in_specs=[VMEM] * 8,
        out_specs=[VMEM] * 3,
        scratch_shapes=[
            pltpu.VMEM((max(f - 1, 1), n, rows, across), BF16),
            pltpu.VMEM((n, rows, across), BF16),
            pltpu.VMEM((8, width), F32),
            pltpu.VMEM((n, 8, width // n), F32),
            pltpu.VMEM((f, 8, width // n), F32),
        ]
        + Scatter.buffers(n, tok, width)
        + Scatter.semaphores(n)
        + [kind((2, f)), kind((2, f)), kind((2, n)), kind((2, n)), kind((2,))],
        compiler_params=pltpu.CompilerParams(
            collective_id=4, has_side_effects=True, vmem_limit_bytes=60 << 20
        ),
        name="last_stage",
    )(d_mixed, w_head, qkv_part, tokens, gain, d_middle, gain_two, gain_head)


def angles_of(length, head_size):
    half = head_size // 2
    freqs = 10000.0 ** (-jnp.arange(half, dtype=F32) / half)
    angles = jnp.arange(length, dtype=jnp.int32).astype(F32)[:, None] * freqs[None, :]
    cosine = jnp.concatenate([jnp.cos(angles), jnp.cos(angles)], -1)
    sine = jnp.concatenate([jnp.sin(angles), jnp.sin(angles)], -1)
    return cosine, sine


def turn(values):
    half = values.shape[-1] // 2
    return jnp.concatenate([-values[..., half:], values[..., :half]], -1)


def turn_back(values):
    half = values.shape[-1] // 2
    return jnp.concatenate([values[..., half:], -values[..., :half]], -1)


def shift_fsdp(values, step, f):
    if step == 0:
        return values
    return lax.ppermute(values, "fsdp", [(i, (i + step) % f) for i in range(f)])


def shards(n, f, inputs, routes, w_qkv, w_out, w_router, norm_gains, w_gate, w_up, w_down, cotangent):
    tokens_low = inputs[0]
    upstream_low = cotangent[0]
    local_routes = routes[0].T
    me = lax.axis_index("seq")
    mine = lax.axis_index("fsdp")
    tok, width = tokens_low.shape
    length = tok * n
    head_size = width // HEADS
    across = 3 * head_size
    rows = w_qkv.shape[0]
    experts = n * w_gate.shape[0]
    capacity = min(tok, 5 * tok * TOPK // (4 * experts))
    factor = head_size ** (-0.5)

    by_head = w_qkv.reshape(rows, 3, HEADS, head_size).transpose(2, 0, 1, 3)
    by_head = by_head.reshape(HEADS, rows, across)
    small = jnp.concatenate([w_router, norm_gains], 1)
    small = jnp.pad(small, ((0, 0), (0, 128 - small.shape[1])))
    tokens_all, w_head, w_out_head, small_all, routes_all = first_gather(
        n, f, tokens_low, by_head, w_out, small, local_routes
    )
    gates = [shift_fsdp(w_gate[0], j, f) for j in range(f)]
    ups = [shift_fsdp(w_up[0], j, f) for j in range(f)]
    downs = [shift_fsdp(w_down[0], j, f) for j in range(f)]
    tokens_all = tokens_all.reshape(length, width)
    w_head = w_head.reshape(width, across)
    w_out_head = w_out_head.reshape(head_size, width)
    small_all = small_all.reshape(width, 128)
    router = small_all[:, :experts].T
    gains = small_all[:, experts : experts + 4].astype(F32).T
    upstream_low, _ = lax.optimization_barrier((upstream_low, tokens_all))
    upstream_all = lax.all_gather(upstream_low, "seq", axis=0, tiled=False)

    tokens_all32 = tokens_all.astype(F32)
    inverse_one = lax.rsqrt(jnp.mean(tokens_all32 * tokens_all32, -1, keepdims=True) + EPS)
    hidden_one = (tokens_all32 * inverse_one * gains[0:1]).astype(BF16)
    mixed = dot(hidden_one, w_head, MATMUL)
    raw_q = mixed[:, :head_size]
    raw_k = mixed[:, head_size : 2 * head_size]
    squares = jnp.stack([jnp.sum(raw_q * raw_q, -1), jnp.sum(raw_k * raw_k, -1)])
    squares = jnp.sum(spread(n, f, squares.reshape(-1, 128), 5), 0).reshape(2, length)
    inverses = lax.rsqrt(squares / width + EPS)
    inverse_q, inverse_k = inverses[0][:, None], inverses[1][:, None]
    own = lax.dynamic_slice_in_dim(gains, me * head_size, head_size, 1)
    gain_q, gain_k = own[1:2], own[2:3]
    cosine, sine = angles_of(length, head_size)
    normed_q = raw_q * inverse_q * gain_q
    normed_k = raw_k * inverse_k * gain_k
    queries = (normed_q * cosine + turn(normed_q) * sine).astype(BF16)
    keys = (normed_k * cosine + turn(normed_k) * sine).astype(BF16)
    values = mixed[:, 2 * head_size :].astype(BF16)
    attended, exact, sums = attention(queries, keys, values, factor)

    middle, hidden_all, gate_probs, weights_here = middle_stage(
        n,
        f,
        attended.reshape(n, tok, head_size),
        w_out_head,
        tokens_low,
        gains[3:4],
        router,
        local_routes,
    )

    weights_here = weights_here[:, 0, :]
    here = jnp.any(routes_all == me, 1)
    count = here.astype(jnp.int32)
    place = jnp.cumsum(count, 1) - count
    place = jnp.where(here, place, -1)
    slots = jnp.arange(capacity, dtype=jnp.int32)
    pick = slots[None, :, None] == place[:, None, :]
    pick_low = pick.astype(BF16)
    pick_back = (slots[None, None, :] == place[:, :, None]).astype(BF16)
    take = (((2,), (1,)), ((0,), (0,)))
    expert_rows = lax.dot_general(pick_low, hidden_all, take, preferred_element_type=F32)
    expert_rows = expert_rows.astype(BF16).reshape(n * capacity, width)
    upstream_rows = lax.dot_general(pick_low, upstream_all, take, preferred_element_type=F32)
    row_weight = jnp.sum(jnp.where(pick, weights_here[:, None, :], 0.0), -1)
    d_produced = (row_weight[..., None] * upstream_rows).astype(BF16).reshape(n * capacity, width)
    produced = 0.0
    inners, keeps = [], []
    for j in range(f):
        gate_act = dot(expert_rows, gates[j], MATMUL)
        up_act = dot(expert_rows, ups[j], MATMUL)
        sigma = jax.nn.sigmoid(gate_act)
        silu = gate_act * sigma
        inner = (silu * up_act).astype(BF16)
        produced = produced + dot(inner, downs[j], BY_LAST)
        inners.append(inner)
        keeps.append((gate_act, up_act, sigma, silu))
    produced = produced.astype(BF16).reshape(n, capacity, width)
    d_weight_rows = jnp.sum(produced.astype(F32) * upstream_rows, -1)
    d_weight_tok = jnp.sum(jnp.where(pick, d_weight_rows[..., None], 0.0), 1)
    d_weight_tok = jnp.broadcast_to(d_weight_tok[:, None, :], (n, 8, tok))
    d_rows = 0.0
    backs = []
    for j in range(f):
        gate_act, up_act, sigma, silu = keeps[j]
        d_inner = dot(d_produced, downs[j], MATMUL)
        d_gate = (d_inner * up_act * sigma * (1.0 + gate_act * (1.0 - sigma))).astype(BF16)
        d_up = (d_inner * silu).astype(BF16)
        d_rows = d_rows + dot(d_gate, gates[j], BY_LAST) + dot(d_up, ups[j], BY_LAST)
        backs.append((d_gate, d_up))
    d_rows = d_rows.astype(BF16).reshape(n, capacity, width)

    d_middle, d_attn_all, d_logits_all, gain_two = back_stage(
        n,
        f,
        pick_back,
        d_rows,
        d_weight_tok,
        gate_probs,
        router,
        upstream_low,
        middle,
        gains[3:4],
    )
    result = result_stage(n, f, pick_back, produced, weights_here[:, :, None], middle)

    grads = []
    for left, right in (
        (lambda j: expert_rows, lambda j: backs[j][0]),
        (lambda j: expert_rows, lambda j: backs[j][1]),
        (lambda j: d_produced, lambda j: inners[j]),
    ):
        total = dot(left(0), right(0), BY_FIRST)
        for j in range(1, f):
            part = dot(left(j), right(j), BY_FIRST).astype(BF16)
            total = total + shift_fsdp(part, f - j, f).astype(F32)
        grads.append(total[None])

    d_attn_all = d_attn_all.reshape(length, width)
    d_attended = dot(d_attn_all, w_out_head, BY_LAST).astype(BF16)
    delta = jnp.sum(d_attended.astype(F32) * exact, -1)[None, :]
    d_queries, d_keys, d_values = attention_back(
        queries, keys, values, d_attended, sums.reshape(1, length), delta, factor
    )
    d_q = d_queries.astype(BF16).astype(F32)
    d_k = d_keys.astype(BF16).astype(F32)
    d_q = d_q * cosine + turn_back(d_q * sine)
    d_k = d_k * cosine + turn_back(d_k * sine)
    inners = jnp.stack(
        [jnp.sum(raw_q * gain_q * d_q, -1), jnp.sum(raw_k * gain_k * d_k, -1)]
    )
    inners = jnp.sum(spread(n, f, inners.reshape(-1, 128), 6), 0).reshape(2, length) / width
    d_raw_q = inverse_q * gain_q * d_q - raw_q * (inverse_q**3) * inners[0][:, None]
    d_raw_k = inverse_k * gain_k * d_k - raw_k * (inverse_k**3) * inners[1][:, None]
    gain_query = jnp.sum(raw_q * inverse_q * d_q, 0)
    gain_key = jnp.sum(raw_k * inverse_k * d_k, 0)
    d_mixed = jnp.concatenate(
        [d_raw_q.astype(BF16), d_raw_k.astype(BF16), d_values.astype(BF16)], 1
    )
    qkv_part = dot(hidden_one, d_mixed, BY_FIRST).astype(BF16)
    qkv_part = qkv_part.reshape(n, f, rows, across).transpose(1, 0, 2, 3)
    zero = jnp.zeros((head_size,), F32)
    gain_head = jnp.stack([zero, zero, gain_query, gain_key, zero, zero, zero, zero])
    grad_inputs, qkv_rows, gains_own = last_stage(
        n,
        f,
        d_mixed.reshape(n, tok, across),
        w_head,
        qkv_part,
        tokens_low,
        gains[0:1],
        d_middle,
        gain_two,
        gain_head,
    )
    grad_qkv = (
        qkv_rows.reshape(HEADS, rows, 3, head_size)
        .transpose(1, 2, 0, 3)
        .reshape(rows, 3 * width)
        .astype(F32)
    )
    own_hidden = lax.dynamic_slice_in_dim(hidden_all, me * head_size, head_size, 2)
    proj_part = dot(attended, d_attn_all, BY_FIRST)
    router_part = jnp.einsum(
        "ntc,nkt->ck", own_hidden, d_logits_all, preferred_element_type=F32
    )
    both = jnp.concatenate([proj_part, router_part], 1).reshape(f, rows, width + experts)
    total = lax.dynamic_index_in_dim(both, mine, 0, keepdims=False)
    for j in range(1, f):
        part = lax.dynamic_index_in_dim(both, (mine + j) % f, 0, keepdims=False)
        total = total + shift_fsdp(part.astype(BF16), j, f).astype(F32)
    gains_out = jnp.stack([gains_own[0], gains_own[2], gains_own[3], gains_own[1]], 1)
    grad_gains = lax.dynamic_slice_in_dim(gains_out, mine * rows, rows, 0)
    return (
        result[None],
        grad_inputs[None],
        grad_qkv,
        total[:, :width],
        total[:, width:],
        grad_gains,
        *grads,
    )


def solution(mesh):
    tokens = P("fsdp", "seq", None)
    split = P(("seq", "fsdp"), None)
    expert = P("seq", None, "fsdp")
    return jax.shard_map(
        partial(shards, mesh.shape["seq"], mesh.shape["fsdp"]),
        mesh=mesh,
        in_specs=(tokens, tokens, split, split, split, split, expert, expert, expert, tokens),
        out_specs=(tokens, tokens, split, split, split, split, expert, expert, expert),
        check_vma=False,
    )
```

time: 1790 us -> 706 us (0.39)
  waiting for transfers between devices: 771 us -> 0.06 us
  Pallas kernels: 0 us -> 455 us
  blocking collectives: 226 us -> 0 us
  local copies, waits for them, and re-layouts: 254 us -> 30.8 us
  starting transfers between devices: 133 us -> 7.67 us
  other arithmetic: 146 us -> 41.5 us
  matrix products: 215 us -> 148 us
    pallas_call x0 -> x9, Pallas kernels: none -> 455 us  [the longest x1 101 us: middle_stage(): pl.pallas_call(partial(middle_kernel, n, f), out_shape=[shape((tok, width...]
    all_to_all x6 -> x0, waiting for transfers between devices: 310 us -> none  [the longest x1 185 us: shards(): lax.all_to_all(outgoing, 'seq', split_axis=1, concat_axis=3, tiled=True)]
    reduce_scatter x5 -> x0, waiting for transfers between devices: 189 us -> none  [the longest x1 52.9 us: shards(): lax.psum_scatter(up_part.astype(jnp.bfloat16), 'fsdp', scatter_dimension=...]
    all_gather x3 -> x0, blocking collectives: 163 us -> none  [the longest x1 72.3 us: shards(): lax.all_gather(norm_gains, ('seq', 'fsdp'), axis=0, tiled=True)]
    unnamed x16 -> x1, waiting for transfers between devices: 141 us -> 0.02 us
    all_to_all x6 -> x0, starting transfers between devices: 132 us -> none  [the longest x1 44.9 us: shards(): lax.all_to_all(produced[None], 'seq', split_axis=2, concat_axis=0, tiled=...]
    all_gather x7 -> x1, waiting for transfers between devices: 132 us -> 0.02 us  [shards(): upstream_all = lax.all_gather(upstream_low, 'seq', axis=0, tiled=False)]
    unnamed x11 -> x5, other arithmetic: 73.5 us -> 0.01 us
  transfers between devices with their start and end apart: 20 -> 8, of which waited for: 14 -> 0; matrix products, arithmetic and copies ran while one was open for 23% -> 23% of each run, Pallas kernels for 0% -> 54%
where the time goes in v1:
time: 706 us; the launch traced here: 698 us
  Pallas kernels  455 us (64%)
  matrix products  148 us (21%)
  other arithmetic  41.5 us (6%)
  local copies, waits for them, and re-layouts  30.8 us (4%)
  between operations  15.5 us (2%)
  starting transfers between devices  7.67 us (1%)
    dot_general x22, matrix products, dot(): return lax.dot_general(a, b, dims, preferred_element_type=F32)  134 us
    pallas_call x1, Pallas kernels, middle_stage(): pl.pallas_call(partial(middle_kernel, n, f), out_shape=[shape((tok, width...  101 us
    pallas_call x1, Pallas kernels, back_stage(): pl.pallas_call(partial(back_kernel, n, f), out_shape=[shape((tok, width),...  96.8 us
    pallas_call x1, Pallas kernels, last_stage(): pl.pallas_call(partial(last_kernel, n, f), out_shape=[shape((tok, width),...  93.4 us
    pallas_call x1, Pallas kernels, first_gather(): pl.pallas_call(partial(first_kernel, n, f), out_shape=[shape((n, tok, wid...  76.2 us
    pallas_call x1, Pallas kernels, result_stage(): pl.pallas_call(partial(result_kernel, n, f), out_shape=jax.ShapeDtypeStru...  50 us
    pallas_call x2, Pallas kernels, spread(): pl.pallas_call(partial(spread_kernel, n, f), out_shape=jax.ShapeDtypeStru...  20.2 us
    unnamed x125, local copies, waits for them, and re-layouts  17.8 us
  transfers between devices with their start and end apart: 8, of which 0 were waited for; matrix products, arithmetic and copies ran while one was open for 23% of the time, Pallas kernels for 54%

profile of v1, /device:TPU:0, one launch (start us, length us, event | category | flops | bytes accessed | tf_op | source)
XLA Modules:
  0.0 698.1 jit_solution(236104775155652466)
XLA Ops:
  11.6 76.2 %first_gather.1 = (bf16[16,128,2048]{2,1,0:T(8,128)(2,1)S(1)}, bf16[16,2,64,384]{3,2,1,0:T(8,128)(2,1)S(1)}, bf16[2,64,2048]{2,1,0:T(8,128)(2,1)S(1)}, bf16[16,2...) custom-call(bf16[128,2048]{1,0:T(8,128)(2,1)S(1)} %bitcast.153, bf16[16,64,384]{2,1,0:T(8,128)(2,1)S(1)} %reshape.184.refs_1_, ...), custom_call_target="tpu_custom_call" | custom-call | tf_op jit(solution)/shard_map/first_gather/pallas_call | solution.py:385
  87.8 3.2 copy-done
  91.9 1.6 collective-permute-start.2
  94.0 1.5 collective-permute-start
  97.0 5.4 fusion
  103.7 8.7 %fusion.2 = bf16[16,128,2048]{2,1,0:T(8,128)(2,1)} fusion(bf16[16,128,2048]{2,1,0:T(8,128)(2,1)} %copy-done, f32[2048]{0:T(1024)S(1)} %bitcast.209, f32[16,128]{1,0:T(8,128)S(1)} %get-tuple-element.136), kind=kLoop, calls=%fused_computation.4 | loop fusion | flops 16777216 | bytes 16793600 | tf_op jit(solution)/shard_map/convert_element_type | solution.py:1015
  112.4 6.9 fusion.41
  121.0 12.4 %spread.2 = f32[16,32,128]{2,1,0:T(8,128)S(1)} custom-call(f32[32,128]{1,0:T(8,128)S(1)} %reshape.187.block), custom_call_target="tpu_custom_call" | custom-call | tf_op jit(solution)/shard_map/spread/pallas_call | solution.py:426
  133.5 3.7 multiply_cosine_fusion
  137.2 2.7 multiply_multiply_fusion
  141.7 7.1 %attention.1 = (bf16[2048,128]{1,0:T(8,128)(2,1)S(1)}, f32[2048,128]{1,0:T(8,128)S(1)}, f32[2048,1]{1,0:T(8,128)S(1)}) custom-call(bf16[2048,128]{1,0:T(8,128)(2,1)S(1)} %get-tuple-element.112.q_ref, bf16[2048,128]{1,0:T(8,128)(2,1)S(1)} %get-tuple-element.111.k_ref, bf16[2048,128]{1,0:T(8,128)(2,1)S(1)} %slice.169.v_ref), custom_call_target="tpu_custom_call" | custom-call | flops 1073741824 | bytes 2097152 | tf_op jit(solution)/shard_map/attention/pallas_call | solution.py:486
  150.6 101.5 %middle_stage.1 = (f32[128,2048]{1,0:T(8,128)}, bf16[16,128,2048]{2,1,0:T(8,128)(2,1)}, f32[16,128]{1,0:T(8,128)}, f32[16,8,128]{2,1,0:T(8,128)}) custom-call(bf16[16,128,128]{2,1,0:T(8,128)(2,1)} %bitcast.154, bf16[128,2048]{1,0:T(8,128)(2,1)} %bitcast.159, bf16[128,2048]{1,0:T(8,128)(2,1)} %bitcast.151, f32[1,2048]{1,0:T(1,128)} %get-tuple-element.123.refs_3_.refs_7_, ...), custom_call_target="tpu_custom_call" | custom-call | tf_op jit(solution)/shard_map/middle_stage/pallas_call | solution.py:639
  252.2 5.0 convolution_convert_fusion
  257.2 2.9 fusion.32
  260.4 4.8 multiply_convert_fusion.10
  265.2 5.5 fusion.24
  274.5 6.0 fusion.42
  280.6 7.4 %multiply_convert_fusion.9 = (bf16[1280,512]{1,0:T(8,128)(2,1)S(1)}, f32[1280,512]{1,0:T(8,128)}) fusion(f32[1280,512]{1,0:T(8,128)S(1)} %fusion.42, bf16[1280,2048]{1,0:T(8,128)(2,1)S(1)} %bitcast.177, bf16[2048,512]{1,0:T(8,128)(2,1)} %collective-permute-done.1), kind=kOutput, calls=%fused_computation.25 | convolution fusion | flops 2688286720 | bytes 13893632 | tf_op jit(solution)/shard_map/dot_general | solution.py:26
  288.0 6.7 add_convert_fusion.1
  294.7 50.0 %result_stage.1 = bf16[128,2048]{1,0:T(8,128)(2,1)} custom-call(bf16[16,128,80]{2,1,0:T(8,128)(2,1)} %fusion.15.refs_0_, bf16[16,80,2048]{2,1,0:T(8,128)(2,1)} %bitcast.165, f32[16,128,1]{2,1,0:T(8,128)} %copy.71.refs_2_, f32[128,2048]{1,0:T(8,128)} %get-tuple-element.40.refs_3_.refs_6_), custom_call_target="tpu_custom_call" | custom-call | tf_op jit(solution)/shard_map/result_stage/pallas_call | solution.py:797
  344.7 7.5 %multiply_reduce_fusion = (f32[16,80]{1,0:T(8,128)S(1)}, f32[16,80,2048]{2,1,0:T(8,128)S(1)}) fusion(bf16[16,80,2048]{2,1,0:T(8,128)(2,1)} %bitcast.166, bf16[16,128,2048]{2,1,0:T(8,128)(2,1)} %bitcast.167, s32[16,128]{1,0:T(8,128)S(1)} %subtract_select_fusion), kind=kOutput, calls=%fused_computation.6 | convolution fusion | flops 679115520 | bytes 24130560 | tf_op jit(solution)/shard_map/dot_general | solution.py:1056
  352.8 2.9 multiply_convert_fusion.1
  355.7 7.3 %convolution_convert_fusion.1 = bf16[2048,512]{1,0:T(8,128)(2,1)} fusion(bf16[1280,2048]{1,0:T(8,128)(2,1)} %bitcast.190, bf16[1280,512]{1,0:T(8,128)(2,1)S(1)} %copy-done.35), kind=kOutput, calls=%fused_computation.17 | convolution fusion | flops 2685403136 | bytes 8650752 | tf_op jit(solution)/shard_map/dot_general | solution.py:26
  363.1 3.9 multiply_convert_fusion.7
  367.1 6.4 multiply_convert_fusion.6
  373.6 4.1 convolution_convert_fusion.3
  377.7 4.1 convolution_convert_fusion.2
  385.0 5.5 fusion.30
  390.5 5.5 fusion.26
  395.9 7.4 %fusion.43 = f32[1280,2048]{1,0:T(8,128)} fusion(bf16[1280,512]{1,0:T(8,128)(2,1)S(1)} %get-tuple-element.105, bf16[2048,512]{1,0:T(8,128)(2,1)} %collective-permute-done), kind=kOutput, calls=%fused_computation.129 | convolution fusion | flops 2684354560 | bytes 13893632 | tf_op jit(solution)/shard_map/dot_general | solution.py:26
  403.3 14.6 %add_convert_fusion = bf16[1280,2048]{1,0:T(8,128)(2,1)} fusion(f32[1280,2048]{1,0:T(8,128)} %fusion.43, f32[1280,2048]{1,0:T(8,128)} %fusion.30, f32[1280,2048]{1,0:T(8,128)} %fusion.26, bf16[1280,512]{1,0:T(8,128)(2,1)S(1)} %get-tuple-element.106, bf16[2048,512]{1,0:T(8,128)(2,1)} %collective-permute-done.1), kind=kOutput, calls=%fused_computation.7 | convolution fusion | flops 2694840320 | bytes 40108032 | tf_op jit(solution)/shard_map/dot_general | solution.py:26
  418.6 96.8 %back_stage.1 = (f32[128,2048]{1,0:T(8,128)}, bf16[16,128,2048]{2,1,0:T(8,128)(2,1)}, bf16[16,16,128]{2,1,0:T(8,128)(2,1)}, f32[1,2048]{1,0:T(1,128)}) custom-call(bf16[16,128,80]{2,1,0:T(8,128)(2,1)} %fusion.15.refs_0_, bf16[16,80,2048]{2,1,0:T(8,128)(2,1)} %bitcast.170, f32[16,8,128]{2,1,0:T(8,128)} %broadcast_in_dim.67.refs_2_, ...), custom_call_target="tpu_custom_call" | custom-call | tf_op jit(solution)/shard_map/back_stage/pallas_call | solution.py:743
  515.3 1.4 convolution_bitcast_fusion
  516.8 4.8 fusion.44
  521.6 1.4 copy-done.13
  523.0 2.5 multiply_reduce_fusion.5
  527.4 9.7 %attention_back.1 = (f32[2048,128]{1,0:T(8,128)S(1)}, f32[2048,128]{1,0:T(8,128)S(1)}, f32[2048,128]{1,0:T(8,128)S(1)}) custom-call(bf16[2048,128]{1,0:T(8,128)(2,1)S(1)} %get-tuple-element.112.q_ref, bf16[2048,128]{1,0:T(8,128)(2,1)S(1)} %get-tuple-element.111.k_ref, bf16[2048,128]{1,0:T(8,128)(2,1)S(1)} %slice.169.v_ref, ...), custom_call_target="tpu_custom_call" | custom-call | flops 2684354560 | bytes 5242880 | tf_op jit(solution)/shard_map/attention_back/pallas_call | solution.py:549
  539.1 1.5 copy-done.12
  540.9 3.1 multiply_reduce_fusion.2
  544.0 7.8 %spread.3 = f32[16,32,128]{2,1,0:T(8,128)S(1)} custom-call(f32[32,128]{1,0:T(8,128)S(1)} %reshape.197.block), custom_call_target="tpu_custom_call" | custom-call | tf_op jit(solution)/shard_map/spread/pallas_call | solution.py:426
  551.9 3.7 subtract_convert_fusion.1
  555.7 8.4 %fusion.6 = bf16[2048,384]{1,0:T(8,128)(2,1)S(1)} fusion(bf16[2048,2048]{1,0:T(8,128)(2,1)} %bitcast.150, f32[2048]{0:T(1024)S(1)} %bitcast.210, f32[2048]{0:T(1024)S(1)} %copy-done.27, bf16[2048,128]{1,0:T(8,128)(2,1)S(1)} %copy-done.23, bf16[2048,128]{1,0:T(8,128)(2,1)S(1)} %get-tuple-element.108, bf16[2048,128]{1,0:T(8,128)(2,1)S(1)} %get-tuple-element.107), kind=kOutput, calls=%fused_computation.20 | convolution fusion | flops 3243507712 | bytes 11550720 | tf_op jit(solution)/shard_map/dot_general | solution.py:26
  567.4 93.4 %last_stage.1 = (f32[128,2048]{1,0:T(8,128)}, bf16[16,64,384]{2,1,0:T(8,128)(2,1)}, f32[8,128]{1,0:T(8,128)}) custom-call(bf16[16,128,384]{2,1,0:T(8,128)(2,1)} %bitcast.188, bf16[2048,384]{1,0:T(8,128)(2,1)} %bitcast.158, bf16[2,16,64,384]{3,2,1,0:T(8,128)(2,1)} %bitcast.189, bf16[128,2048]{1,0:T(8,128)(2,1)} %bitcast.152, f32[1,2048]{1,0:T(1,128)} %copy-done.25, ...), custom_call_target="tpu_custom_call" | custom-call | tf_op jit(solution)/shard_map/last_stage/pallas_call | solution.py:928
  661.6 2.4 reshape.202
  664.9 1.6 copy.88
  669.8 7.5 %add_bitcast_fusion.1 = f32[1,2048,512]{2,1,0:T(8,128)} fusion(bf16[2048,512]{1,0:T(8,128)(2,1)} %collective-permute-done.5, bf16[1280,2048]{1,0:T(8,128)(2,1)} %bitcast.174, bf16[1280,512]{1,0:T(8,128)(2,1)S(1)} %copy-done.41), kind=kOutput, calls=%fused_computation.14 | convolution fusion | flops 2686451712 | bytes 12845056 | tf_op jit(solution)/shard_map/dot_general | solution.py:26
  677.4 5.9 add_bitcast_fusion.2
  683.3 5.8 add_bitcast_fusion
  (199 shorter events, 36.6 us)
Async XLA Ops:
  7.2 337.5 %all-gather.3.cloned.1.call-start = ((), (), s32[]{:S(2)}) async-start(), calls=%async_computation | async-start | bytes 8912896 | tf_op jit(solution)/shard_map/all_gather | solution.py:1011
  91.9 20.5 %copy-start.4 = (bf16[16,2,64,384]{3,2,1,0:T(8,128)(2,1)}, bf16[16,2,64,384]{3,2,1,0:T(8,128)(2,1)S(1)}, u32[]{:S(2)}) copy-start(bf16[16,2,64,384]{3,2,1,0:T(8,128)(2,1)S(1)} %get-tuple-element.35) | copy-start | bytes 4718596
  91.9 196.0 %collective-permute-start.2 = (bf16[2048,512]{1,0:T(8,128)(2,1)}, bf16[2048,512]{1,0:T(8,128)(2,1)}, u32[]{:S(2)}, u32[]{:S(2)}) collective-permute-start(bf16[2048,512]{1,0:T(8,128)(2,1)} %bitcast.219), channel_id=1, source_target_pairs={{0,1},{1,0},{2,3},{3,2},{4,5},{5,4},{6,7},{7,6},{8,9},{9,8},{10,11... | collective-permute-start | bytes 6291464 | tf_op jit(solution)/shard_map/ppermute | solution.py:976
  93.5 187.1 %collective-permute-start.1 = (bf16[2048,512]{1,0:T(8,128)(2,1)}, bf16[2048,512]{1,0:T(8,128)(2,1)}, u32[]{:S(2)}, u32[]{:S(2)}) collective-permute-start(bf16[2048,512]{1,0:T(8,128)(2,1)} %bitcast.221), channel_id=1, source_target_pairs={{0,1},{1,0},{2,3},{3,2},{4,5},{5,4},{6,7},{7,6},{8,9},{9,8},{10,11... | collective-permute-start | bytes 6291464 | tf_op jit(solution)/shard_map/ppermute | solution.py:976
  94.0 180.5 %collective-permute-start = (bf16[2048,512]{1,0:T(8,128)(2,1)}, bf16[2048,512]{1,0:T(8,128)(2,1)}, u32[]{:S(2)}, u32[]{:S(2)}) collective-permute-start(bf16[2048,512]{1,0:T(8,128)(2,1)} %bitcast.220), channel_id=1, source_target_pairs={{0,1},{1,0},{2,3},{3,2},{4,5},{5,4},{6,7},{7,6},{8,9},{9,8},{10,11... | collective-permute-start | bytes 6291464 | tf_op jit(solution)/shard_map/ppermute | solution.py:976
  103.7 8.7 %copy-start.25 = (f32[1,2048]{1,0:T(1,128)}, f32[1,2048]{1,0:T(1,128)S(1)}, u32[]{:S(2)}) copy-start(f32[1,2048]{1,0:T(1,128)S(1)} %get-tuple-element.124.refs_4_) | copy-start | bytes 24580
  252.1 5.1 copy-start.30
  260.4 4.8 copy-start.42
  260.4 4.8 copy-start.28
  265.2 5.5 copy-start.36
  273.4 7.2 %slice-start = ((s8[5242880]{0:T(1024)(128)(4,1)}), s8[4194304]{0:T(1024)(128)(4,1)S(1)}, s32[]{:S(2)}) async-start(s8[5242880]{0:T(1024)(128)(4,1)} %bitcast.175), calls=%async_computation.1 | async-start | bytes 8388608
  274.5 6.0 slice-start.1
  274.5 13.4 %slice-start.8 = ((s8[10485760]{0:T(1024)(128)(4,1)}), s8[4194304]{0:T(1024)(128)(4,1)S(1)}, s32[]{:S(2)}) async-start(s8[10485760]{0:T(1024)(128)(4,1)} %bitcast.222), calls=%async_computation.9 | async-start | bytes 8388608
  274.5 13.4 %slice-start.9 = ((s8[10485760]{0:T(1024)(128)(4,1)}), s8[4194304]{0:T(1024)(128)(4,1)S(1)}, s32[]{:S(2)}) async-start(s8[10485760]{0:T(1024)(128)(4,1)} %bitcast.222), calls=%async_computation.10 | async-start | bytes 8388608
  280.5 7.4 %copy-start.44 = (f32[1280,512]{1,0:T(8,128)}, f32[1280,512]{1,0:T(8,128)S(1)}, u32[]{:S(2)}) copy-start(f32[1280,512]{1,0:T(8,128)S(1)} %fusion.42) | copy-start | bytes 7864324
  280.5 7.4 %slice-start.10 = ((s8[10485760]{0:T(1024)(128)(4,1)}), s8[2097152]{0:T(1024)(128)(4,1)S(1)}, s32[]{:S(2)}) async-start(s8[10485760]{0:T(1024)(128)(4,1)} %bitcast.222), calls=%async_computation.11 | async-start | bytes 4194304
  287.9 6.8 copy-start.34
  355.7 7.3 %copy-start.19 = (bf16[16,80,2048]{2,1,0:T(8,128)(2,1)S(1)}, bf16[16,80,2048]{2,1,0:T(8,128)(2,1)}, u32[]{:S(2)}) copy-start(bf16[16,80,2048]{2,1,0:T(8,128)(2,1)} %multiply_convert_fusion.1) | copy-start | bytes 15728644
  355.7 7.3 %copy-start.29 = (bf16[1,2048,512]{2,1,0:T(8,128)(2,1)S(1)}, bf16[1,2048,512]{2,1,0:T(8,128)(2,1)}, u32[]{:S(2)}) copy-start(bf16[1,2048,512]{2,1,0:T(8,128)(2,1)} %param.18) | copy-start | bytes 6291460
  355.7 7.3 %copy-start.43 = (f32[1280,512]{1,0:T(8,128)S(1)}, f32[1280,512]{1,0:T(8,128)}, u32[]{:S(2)}) copy-start(f32[1280,512]{1,0:T(8,128)} %copy-done.42) | copy-start | bytes 7864324
  355.7 7.3 %copy-start.46 = (f32[1280,512]{1,0:T(8,128)S(1)}, f32[1280,512]{1,0:T(8,128)}, u32[]{:S(2)}) copy-start(f32[1280,512]{1,0:T(8,128)} %get-tuple-element.144) | copy-start | bytes 7864324
  363.1 4.0 copy-start.45
  363.1 4.0 copy-start.47
  363.1 10.4 %slice-start.2 = ((s8[5242880]{0:T(1024)(128)(4,1)}), s8[4194304]{0:T(1024)(128)(4,1)S(1)}, s32[]{:S(2)}) async-start(s8[5242880]{0:T(1024)(128)(4,1)} %bitcast.178), calls=%async_computation.3 | async-start | bytes 8388608
  367.0 18.0 %copy-start.38 = (bf16[1280,512]{1,0:T(8,128)(2,1)}, bf16[1280,512]{1,0:T(8,128)(2,1)S(1)}, u32[]{:S(2)}) copy-start(bf16[1280,512]{1,0:T(8,128)(2,1)S(1)} %get-tuple-element.104) | copy-start | bytes 3932164
  367.0 23.5 %copy-start.40 = (bf16[1280,512]{1,0:T(8,128)(2,1)}, bf16[1280,512]{1,0:T(8,128)(2,1)S(1)}, u32[]{:S(2)}) copy-start(bf16[1280,512]{1,0:T(8,128)(2,1)S(1)} %get-tuple-element.103) | copy-start | bytes 3932164
  367.1 6.5 slice-start.3
  377.7 7.3 %copy-start.31 = (bf16[1,2048,512]{2,1,0:T(8,128)(2,1)S(1)}, bf16[1,2048,512]{2,1,0:T(8,128)(2,1)}, u32[]{:S(2)}) copy-start(bf16[1,2048,512]{2,1,0:T(8,128)(2,1)} %param.16) | copy-start | bytes 6291460
  381.8 288.0 %collective-permute-start.5 = (bf16[2048,512]{1,0:T(8,128)(2,1)}, bf16[2048,512]{1,0:T(8,128)(2,1)}, u32[]{:S(2)}, u32[]{:S(2)}) collective-permute-start(bf16[2048,512]{1,0:T(8,128)(2,1)} %convolution_convert_fusion.2), channel_id=1, source_target_pairs={{0,1},{1,0},{2,3},{3,2},{4,5},{5,4},{6,7},{7,6},{8,9},{9,8},{10,11... | collective-permute-start | bytes 6291464 | tf_op jit(solution)/shard_map/ppermute | solution.py:976
  382.9 294.4 %collective-permute-start.4 = (bf16[2048,512]{1,0:T(8,128)(2,1)}, bf16[2048,512]{1,0:T(8,128)(2,1)}, u32[]{:S(2)}, u32[]{:S(2)}) collective-permute-start(bf16[2048,512]{1,0:T(8,128)(2,1)} %convolution_convert_fusion.3), channel_id=1, source_target_pairs={{0,1},{1,0},{2,3},{3,2},{4,5},{5,4},{6,7},{7,6},{8,9},{9,8},{10,11... | collective-permute-start | bytes 6291464 | tf_op jit(solution)/shard_map/ppermute | solution.py:976
  383.8 299.4 %collective-permute-start.6 = (bf16[2048,512]{1,0:T(8,128)(2,1)}, bf16[2048,512]{1,0:T(8,128)(2,1)}, u32[]{:S(2)}, u32[]{:S(2)}) collective-permute-start(bf16[2048,512]{1,0:T(8,128)(2,1)} %convolution_convert_fusion.1), channel_id=1, source_target_pairs={{0,1},{1,0},{2,3},{3,2},{4,5},{5,4},{6,7},{7,6},{8,9},{9,8},{10,11... | collective-permute-start | bytes 6291464 | tf_op jit(solution)/shard_map/ppermute | solution.py:976
  385.0 5.5 copy-start.33
  418.6 98.2 %copy-start.3 = (bf16[2048,128]{1,0:T(8,128)(2,1)S(1)}, bf16[2048,128]{1,0:T(8,128)(2,1)}, u32[]{:S(2)}) copy-start(bf16[2048,128]{1,0:T(8,128)(2,1)} %copy-done.2) | copy-start | bytes 1572868
  516.7 4.9 copy-start.6
  516.8 4.9 copy-start.10
  516.8 6.3 copy-start.13
  526.5 140.7 %collective-permute-start.3 = (bf16[64,2064]{1,0:T(8,128)(2,1)}, bf16[64,2064]{1,0:T(8,128)(2,1)}, u32[]{:S(2)}, u32[]{:S(2)}) collective-permute-start(bf16[64,2064]{1,0:T(8,128)(2,1)} %fusion.20), channel_id=1, source_target_pairs={{0,1},{1,0},{2,3},{3,2},{4,5},{5,4},{6,7},{7,6},{8,9},{9,8},{10,11... | collective-permute-start | bytes 792584 | tf_op jit(solution)/shard_map/ppermute | solution.py:976
  527.4 10.6 %copy-start.18 = (f32[2048,64]{1,0:T(8,128)S(1)}, f32[2048,64]{1,0:T(8,128)}, u32[]{:S(2)}) copy-start(f32[2048,64]{1,0:T(8,128)} %copy-done.17) | copy-start | bytes 1572868
  551.9 3.8 copy-start.23
  664.9 4.8 copy-start.41
  669.1 8.2 %slice-start.4 = ((s8[5242880]{0:T(1024)(128)(4,1)}), s8[1048576]{0:T(1024)(128)(4,1)S(1)}, s32[]{:S(2)}) async-start(s8[5242880]{0:T(1024)(128)(4,1)} %bitcast.182), calls=%async_computation.5 | async-start | bytes 2097152
  669.8 7.6 %slice-start.5 = ((s8[5242880]{0:T(1024)(128)(4,1)}), s8[4194304]{0:T(1024)(128)(4,1)S(1)}, s32[]{:S(2)}) async-start(s8[5242880]{0:T(1024)(128)(4,1)} %bitcast.182), calls=%async_computation.6 | async-start | bytes 8388608
  669.8 7.6 %copy-start.39 = (bf16[1280,512]{1,0:T(8,128)(2,1)S(1)}, bf16[1280,512]{1,0:T(8,128)(2,1)}, u32[]{:S(2)}) copy-start(bf16[1280,512]{1,0:T(8,128)(2,1)} %copy-done.38) | copy-start | bytes 3932164
  669.8 13.5 %slice-start.6 = ((s8[5242880]{0:T(1024)(128)(4,1)}), s8[4194304]{0:T(1024)(128)(4,1)S(1)}, s32[]{:S(2)}) async-start(s8[5242880]{0:T(1024)(128)(4,1)} %bitcast.193), calls=%async_computation.7 | async-start | bytes 8388608
  677.3 5.9 slice-start.7
  677.3 5.9 copy-start.37
  683.2 5.8 copy-start.22
  683.2 6.6 copy-start.24
  (19 other events, 46.0 us)
Sparse Core Ops, SparseCore 0:
  92.0 77.8 all-gather.2

commit v2 on v1

v2 whole, which is shorter than its diff:
```python
from functools import partial

import jax
import jax.numpy as jnp
from jax import lax
from jax.experimental import pallas as pl
from jax.experimental.pallas import tpu as pltpu
from jax.sharding import PartitionSpec as P


HEADS = 16
TOPK = 8
EPS = 1e-05
NEG = -1e30
F32 = jnp.float32
BF16 = jnp.bfloat16
MESH = pl.DeviceIdType.MESH
PIECES = 2
ANY = pl.BlockSpec(memory_space=pl.ANY)
VMEM = pl.BlockSpec(memory_space=pltpu.VMEM)
MATMUL = (((1,), (0,)), ((), ()))
BY_LAST = (((1,), (1,)), ((), ()))
BY_FIRST = (((0,), (0,)), ((), ()))


def dot(a, b, dims):
    return lax.dot_general(a, b, dims, preferred_element_type=F32)


class Ring:
    def __init__(self, n, f):
        self.n, self.f = n, f
        self.chips = n // 2
        self.half = self.chips // 2
        self.pairs_minor = f == 2
        self.me = lax.axis_index("seq")
        self.mine = lax.axis_index("fsdp")
        chip = self.me // 2
        self.core = self.me % 2
        if self.pairs_minor:
            along, side = chip // 2, chip % 2
        else:
            along, side = chip % self.half, chip // self.half
        self.pos = along + side * (self.chips - 1 - 2 * along)
        self.right = self.at(self.pos + 1)
        self.left = self.at(self.pos + self.chips - 1)
        self.mate = self.me + 1 - 2 * self.core
        self.sign = 1 - 2 * self.core
        self.onward = self.at(self.pos + self.sign + self.chips)

    def at(self, place, other=False):
        place = lax.rem(place + self.chips, self.chips)
        side = place // self.half
        along = place + side * (self.chips - 1 - 2 * place)
        chip = along * 2 + side if self.pairs_minor else side * self.half + along
        core = 1 - self.core if other else self.core
        return chip * 2 + core

    def peer(self, step):
        return lax.rem(self.me + step, self.n)

    def beside(self, step):
        return lax.rem(self.mine + step, self.f)


def greet(ring, everyone, beside):
    barrier = pltpu.get_barrier_semaphore()
    count = 0
    if everyone:
        for step in range(1, ring.n):
            pl.semaphore_signal(
                barrier, inc=1, device_id={"seq": ring.peer(step)}, device_id_type=MESH
            )
        count += ring.n - 1
    else:
        for other in (ring.right, ring.left, ring.mate):
            pl.semaphore_signal(barrier, inc=1, device_id={"seq": other}, device_id_type=MESH)
        count += 3
    if beside:
        for step in range(1, ring.f):
            pl.semaphore_signal(
                barrier, inc=1, device_id={"fsdp": ring.beside(step)}, device_id_type=MESH
            )
        count += ring.f - 1
    pl.semaphore_wait(barrier, count)


def remote(src, dst, send, recv, where):
    return pltpu.make_async_remote_copy(
        src_ref=src,
        dst_ref=dst,
        send_sem=send,
        recv_sem=recv,
        device_id=where,
        device_id_type=MESH,
    )


class Gather:
    def __init__(self, ring, own, out, sems):
        self.ring, self.own, self.out = ring, own, out
        self.send, self.recv, self.mate_send, self.mate_recv, self.keep = sems
        self.piece = own.shape[0] // (2 * PIECES)
        self.last = ring.chips - 1

    @staticmethod
    def semaphores(n):
        hops = n // 2 - 1
        kind = pltpu.SemaphoreType.DMA
        return [
            kind((2, hops, PIECES)),
            kind((2, hops, PIECES)),
            kind((2, hops + 1, PIECES)),
            kind((2, hops + 1, PIECES)),
            kind((1,)),
        ]

    def rows(self, way, s):
        return pl.ds((way * PIECES + s) * self.piece, self.piece)

    def hop(self, way, step, s, first):
        ring = self.ring
        chunk = ring.at(ring.pos - step if way == 0 else ring.pos + step)
        rows = self.rows(way, s)
        there = self.out.at[chunk, rows]
        return remote(
            self.own.at[rows] if first else there,
            there,
            self.send.at[way, step, s],
            self.recv.at[way, step, s],
            {"seq": ring.right if way == 0 else ring.left},
        )

    def share(self, way, step, s, first):
        ring = self.ring
        chunk = ring.at(ring.pos - step if way == 0 else ring.pos + step)
        rows = self.rows(way, s)
        there = self.out.at[chunk, rows]
        return remote(
            self.own.at[rows] if first else there,
            there,
            self.mate_send.at[way, step, s],
            self.mate_recv.at[way, step, s],
            {"seq": ring.mate},
        )

    def local(self):
        return pltpu.make_async_copy(self.own, self.out.at[self.ring.me], self.keep.at[0])

    def begin(self):
        for s in range(PIECES):
            for way in (0, 1):
                self.hop(way, 0, s, True).start()
        for s in range(PIECES):
            for way in (0, 1):
                self.share(way, 0, s, True).start()
        self.local().start()

    def pass_on(self, i):
        for s in range(PIECES):
            for way in (0, 1):
                self.hop(way, i, s, False).wait_recv()

                @pl.when(i + 1 < self.ring.chips - 1)
                def _():
                    self.hop(way, i + 1, s, False).start()

                self.share(way, i + 1, s, False).start()

    def run(self):
        def body(step, carry):
            self.pass_on(step)
            return carry

        lax.fori_loop(0, self.ring.chips - 1, body, 0)

    def finish(self):
        hops = self.ring.chips - 1

        def body(step, carry):
            for s in range(PIECES):
                for way in (0, 1):
                    self.hop(way, step, s, False).wait_send()
                    self.share(way, step, s, False).wait()
            return carry

        lax.fori_loop(0, hops, body, 0)
        for s in range(PIECES):
            for way in (0, 1):
                self.share(way, hops, s, False).wait()
        self.local().wait()


class Scatter:
    def __init__(self, ring, part, tok, width, buffers, sems):
        self.ring, self.part, self.tok, self.width = ring, part, tok, width
        self.mate_out, self.mate_in, self.own, self.going, self.coming = buffers
        self.send, self.recv, self.mate_send, self.mate_recv = sems
        self.piece = tok // (2 * PIECES)

    @staticmethod
    def buffers(n, tok, width):
        chips = n // 2
        return [
            pltpu.VMEM((chips, tok, width), BF16),
            pltpu.VMEM((chips, tok, width), BF16),
            pltpu.VMEM((2, tok, width), F32),
            pltpu.VMEM((chips - 1, tok, width), BF16),
            pltpu.VMEM((chips - 1, tok, width), BF16),
        ]

    @staticmethod
    def semaphores(n):
        chips = n // 2
        kind = pltpu.SemaphoreType.DMA
        return [
            kind((2, chips - 1, PIECES)),
            kind((2, chips - 1, PIECES)),
            kind((chips,)),
            kind((chips,)),
        ]

    def rows(self, way, s):
        return pl.ds((way * PIECES + s) * self.piece, self.piece)

    def exchange(self, i):
        return remote(
            self.mate_out.at[i],
            self.mate_in.at[i],
            self.mate_send.at[i],
            self.mate_recv.at[i],
            {"seq": self.ring.mate},
        )

    def hop(self, way, i, s):
        ring = self.ring
        rows = self.rows(way, s)
        return remote(
            self.going.at[i, rows],
            self.coming.at[i, rows],
            self.send.at[way, i, s],
            self.recv.at[way, i, s],
            {"seq": ring.right if way == 0 else ring.left},
        )

    def produce(self, i):
        ring = self.ring
        half = self.tok // 2
        places = (ring.pos - 1 - i, ring.pos + 1 + i)
        for way in (0, 1):
            chunk = ring.at(places[way] + ring.chips, True)
            self.part(chunk, way, self.mate_out, i)
        self.exchange(i).start()
        slot = lax.rem(i, 2)
        for way in (0, 1):
            chunk = ring.at(places[way] + ring.chips)
            self.part(chunk, way, self.own, slot)

    def step(self, i, first):
        self.exchange(i).wait_recv()
        slot = lax.rem(i, 2)
        for s in range(PIECES):
            for way in (0, 1):
                rows = self.rows(way, s)
                value = self.own[slot, rows] + self.mate_in[i, rows].astype(F32)
                if not first:
                    self.hop(way, i - 1, s).wait_recv()
                    value = value + self.coming[i - 1, rows].astype(F32)
                self.going[i, rows] = value.astype(BF16)
                self.hop(way, i, s).start()

    def run(self, finish, between=None):
        last = self.ring.chips - 1
        self.produce(0)
        self.produce(1)
        self.step(0, True)

        def body(i, carry):
            self.produce(i + 1)
            self.step(i, False)
            return carry

        if between is None:
            lax.fori_loop(1, last, body, 0)
        else:
            lax.fori_loop(1, last // 2 + 1, body, 0)
            between()
            lax.fori_loop(last // 2 + 1, last, body, 0)
        self.exchange(last).wait_recv()
        slot = last % 2
        for s in range(PIECES):
            for way in (0, 1):
                rows = self.rows(way, s)
                self.hop(way, last - 1, s).wait_recv()
                value = self.own[slot, rows] + self.mate_in[last, rows].astype(F32)
                value = value + self.coming[last - 1, rows].astype(F32)
                finish(rows, value)

    def close(self):
        last = self.ring.chips - 1

        def body(i, carry):
            self.exchange(i).wait_send()
            for s in range(PIECES):
                for way in (0, 1):
                    self.hop(way, i, s).wait_send()
            return carry

        lax.fori_loop(0, last, body, 0)
        self.exchange(last).wait_send()


class Walk:
    def __init__(self, ring, own, out, sems):
        self.ring, self.own, self.out = ring, own, out
        self.send, self.recv, self.share_send, self.share_recv, self.keep = sems
        self.piece = own.shape[0] // PIECES
        self.last = ring.chips - 1

    @staticmethod
    def semaphores(n):
        kind = pltpu.SemaphoreType.DMA
        return [kind((n // 2, PIECES)) for _ in range(4)] + [kind((1,))]

    def block(self, i):
        ring = self.ring
        return ring.at(ring.pos - ring.sign * i + 2 * ring.chips)

    def hop(self, i, s, first=False):
        rows = pl.ds(s * self.piece, self.piece)
        there = self.out.at[self.block(i), rows]
        return remote(
            self.own.at[rows] if first else there,
            there,
            self.send.at[i, s],
            self.recv.at[i, s],
            {"seq": self.ring.onward},
        )

    def share(self, i, s, first=False):
        rows = pl.ds(s * self.piece, self.piece)
        there = self.out.at[self.block(i), rows]
        return remote(
            self.own.at[rows] if first else there,
            there,
            self.share_send.at[i, s],
            self.share_recv.at[i, s],
            {"seq": self.ring.mate},
        )

    def local(self):
        return pltpu.make_async_copy(self.own, self.out.at[self.ring.me], self.keep.at[0])

    def begin(self):
        for s in range(PIECES):
            self.hop(0, s, True).start()
        for s in range(PIECES):
            self.share(0, s, True).start()
        self.local().start()

    def pass_on(self, i):
        for s in range(PIECES):
            self.hop(i, s).wait_recv()

            @pl.when(i + 1 < self.last)
            def _():
                self.hop(i + 1, s).start()

            self.share(i + 1, s).start()

    def finish(self):
        def body(i, carry):
            for s in range(PIECES):
                self.hop(i, s).wait_send()
                self.share(i, s).wait()
            return carry

        lax.fori_loop(0, self.last, body, 0)
        for s in range(PIECES):
            self.share(self.last, s).wait()
        self.local().wait()


class Fold:
    def __init__(self, ring, part, buffers, sems):
        self.ring, self.part = ring, part
        self.mate_out, self.mate_in, self.own, self.going, self.coming = buffers
        self.swap_send, self.swap_recv, self.send, self.recv = sems
        self.piece = self.own.shape[0] // PIECES
        self.last = ring.chips - 1

    @staticmethod
    def buffers(n, tok, width):
        chips = n // 2
        return [
            pltpu.VMEM((2, tok, width), BF16),
            pltpu.VMEM((chips, tok, width), BF16),
            pltpu.VMEM((tok, width), F32),
            pltpu.VMEM((2, tok, width), BF16),
            pltpu.VMEM((chips - 1, tok, width), BF16),
        ]

    @staticmethod
    def semaphores(n):
        chips = n // 2
        kind = pltpu.SemaphoreType.DMA
        return [kind((chips,)), kind((chips,)), kind((chips, PIECES)), kind((chips, PIECES))]

    def swap(self, i):
        return remote(
            self.mate_out.at[lax.rem(i, 2)],
            self.mate_in.at[i],
            self.swap_send.at[i],
            self.swap_recv.at[i],
            {"seq": self.ring.mate},
        )

    def hop(self, i, s):
        rows = pl.ds(s * self.piece, self.piece)
        return remote(
            self.going.at[lax.rem(i, 2), rows],
            self.coming.at[i, rows],
            self.send.at[i, s],
            self.recv.at[i, s],
            {"seq": self.ring.onward},
        )

    def produce(self, i):
        ring = self.ring

        @pl.when(i >= 2)
        def _():
            self.swap(i - 2).wait_send()

        slot = lax.rem(i, 2)
        there = ring.at(ring.pos + ring.sign * (1 + i) + 2 * ring.chips, True)
        self.part(there, self.mate_out.at[slot])
        self.swap(i).start()
        here = ring.at(ring.pos - ring.sign * (1 + i) + 2 * ring.chips)
        self.part(here, self.own)

    def step(self, i):
        self.swap(i).wait_recv()

        @pl.when(i >= 2)
        def _():
            for s in range(PIECES):
                self.hop(i - 2, s).wait_send()

        for s in range(PIECES):
            rows = pl.ds(s * self.piece, self.piece)

            @pl.when(i > 0)
            def _():
                self.hop(i - 1, s).wait_recv()
                self.own[rows, :] = self.own[rows, :] + self.coming[i - 1, rows].astype(F32)

            value = self.own[rows, :] + self.mate_in[i, rows].astype(F32)
            self.going[lax.rem(i, 2), rows] = value.astype(BF16)
            self.hop(i, s).start()

    def run(self, finish, filler, after):
        last = self.last

        def body(i, carry):
            self.produce(i)
            self.step(i)
            after(i)
            filler(i)
            return carry

        lax.fori_loop(1, last, body, 0)
        self.produce(last)
        filler(last)
        self.swap(last).wait_recv()
        for s in range(PIECES):
            rows = pl.ds(s * self.piece, self.piece)
            self.hop(last - 1, s).wait_recv()
            value = self.own[rows, :] + self.mate_in[last, rows].astype(F32)
            finish(rows, value + self.coming[last - 1, rows].astype(F32))

    def close(self):
        last = self.last
        for s in range(PIECES):
            self.hop(last - 2, s).wait_send()
            self.hop(last - 1, s).wait_send()
        self.swap(last - 1).wait_send()
        self.swap(last).wait_send()


class Stored:
    def __init__(self, ring, parts, buffers, sems):
        self.ring, self.parts = ring, parts
        self.near, self.mate_in, self.going, self.coming = buffers
        self.swap_send, self.swap_recv, self.send, self.recv, self.load_sem = sems
        self.piece = self.near.shape[1] // PIECES
        self.last = ring.chips - 1

    @staticmethod
    def buffers(n, tok, width):
        chips = n // 2
        return [
            pltpu.VMEM((2, tok, width), BF16),
            pltpu.VMEM((chips, tok, width), BF16),
            pltpu.VMEM((2, tok, width), BF16),
            pltpu.VMEM((chips - 1, tok, width), BF16),
        ]

    @staticmethod
    def semaphores(n):
        chips = n // 2
        kind = pltpu.SemaphoreType.DMA
        return [
            kind((chips,)),
            kind((chips,)),
            kind((chips, PIECES)),
            kind((chips, PIECES)),
            kind((2,)),
        ]

    def swap(self, i):
        ring = self.ring
        there = ring.at(ring.pos + ring.sign * (1 + i) + 2 * ring.chips, True)
        return remote(
            self.parts.at[there],
            self.mate_in.at[i],
            self.swap_send.at[i],
            self.swap_recv.at[i],
            {"seq": ring.mate},
        )

    def load(self, i):
        ring = self.ring
        here = ring.at(ring.pos - ring.sign * (1 + i) + 2 * ring.chips)
        slot = lax.rem(i, 2)
        return pltpu.make_async_copy(
            self.parts.at[here], self.near.at[slot], self.load_sem.at[slot]
        )

    def hop(self, i, s):
        rows = pl.ds(s * self.piece, self.piece)
        return remote(
            self.going.at[lax.rem(i, 2), rows],
            self.coming.at[i, rows],
            self.send.at[i, s],
            self.recv.at[i, s],
            {"seq": self.ring.onward},
        )

    def begin(self):
        self.load(0).start()

        def body(i, carry):
            self.swap(i).start()
            return carry

        lax.fori_loop(0, self.last + 1, body, 0)

    def step(self, i):
        self.load(i).wait()
        self.load(i + 1).start()
        self.swap(i).wait_recv()
        slot = lax.rem(i, 2)

        @pl.when(i >= 2)
        def _():
            for s in range(PIECES):
                self.hop(i - 2, s).wait_send()

        for s in range(PIECES):
            rows = pl.ds(s * self.piece, self.piece)
            value = self.near[slot, rows].astype(F32) + self.mate_in[i, rows].astype(F32)
            self.going[slot, rows] = value.astype(BF16)

            @pl.when(i > 0)
            def _():
                self.hop(i - 1, s).wait_recv()
                total = self.near[slot, rows].astype(F32) + self.mate_in[i, rows].astype(F32)
                total = total + self.coming[i - 1, rows].astype(F32)
                self.going[slot, rows] = total.astype(BF16)

            self.hop(i, s).start()

    def close(self, finish):
        last = self.last
        self.load(last).wait()
        self.swap(last).wait_recv()
        for s in range(PIECES):
            rows = pl.ds(s * self.piece, self.piece)
            self.hop(last - 1, s).wait_recv()
            value = self.near[last % 2, rows].astype(F32) + self.mate_in[last, rows].astype(F32)
            finish(rows, value + self.coming[last - 1, rows].astype(F32))
            self.hop(last - 2, s).wait_send()
            self.hop(last - 1, s).wait_send()

        def body(i, carry):
            self.swap(i).wait_send()
            return carry

        lax.fori_loop(0, last + 1, body, 0)


def first_kernel(n, f, *refs):
    own, by_head, small, routes, w_out, w_gate, w_up = refs[:7]
    hidden_all, mixed, w_head, router, gains, routes_all, gate_near, up_near, out_all = refs[7:16]
    near, small_all, out_rows = refs[16:19]
    sems, out_sems = refs[19:24], refs[24:29]
    send, recv, beside_send, beside_recv, keep = refs[29:34]
    wide_send, wide_recv, row_send, row_recv, out_sem = refs[34:]
    ring = Ring(n, f)
    experts = router.shape[0]
    tok, width = own.shape
    rows = small.shape[0]
    hops = ring.chips - 1
    piece = width // ring.chips
    greet(ring, True, True)
    gather = Gather(ring, own, near, sems)
    gather_out = Gather(ring, out_rows, out_all, out_sems)
    out_mine = pl.ds(pl.multiple_of(ring.mine * rows, rows), rows)

    def push(kind, step):
        there = ring.peer(step)
        source, target = [
            (by_head.at[there], w_head.at[ring.me, ring.mine]),
            (small, small_all.at[ring.me, ring.mine]),
            (routes, routes_all.at[ring.me]),
        ][kind]
        return remote(
            source, target, send.at[kind, step], recv.at[kind, step], {"seq": there}
        )

    def aside(kind, step, over, first):
        origin = lax.rem(ring.me + n - step, n)
        block = [w_head, small_all][kind].at[origin, ring.mine]
        source = [by_head.at[ring.me], small][kind] if first else block
        return remote(
            source,
            block,
            beside_send.at[kind, step, over],
            beside_recv.at[kind, step, over],
            {"fsdp": ring.beside(over)},
        )

    def row(over):
        return remote(
            w_out,
            out_rows.at[out_mine],
            row_send.at[over],
            row_recv.at[over],
            {"fsdp": ring.beside(over)},
        )

    def wide(kind, part, over):
        these = pl.ds(part * piece, piece)
        return remote(
            [w_gate, w_up][kind].at[these],
            [gate_near, up_near][kind].at[over - 1, these],
            wide_send.at[kind, part, over],
            wide_recv.at[kind, part, over],
            {"fsdp": ring.beside(over)},
        )

    gather.begin()
    for over in range(1, f):
        row(over).start()
    copies = [
        pltpu.make_async_copy(by_head.at[ring.me], w_head.at[ring.me, ring.mine], keep.at[0]),
        pltpu.make_async_copy(small, small_all.at[ring.me, ring.mine], keep.at[1]),
        pltpu.make_async_copy(routes, routes_all.at[ring.me], keep.at[2]),
        pltpu.make_async_copy(w_out, out_rows.at[out_mine], keep.at[3]),
    ]
    for copy in copies:
        copy.start()
    for step in range(1, n):
        for kind in (1, 0, 2):
            push(kind, step).start()
    for over in range(1, f):
        aside(1, 0, over, True).start()
        aside(0, 0, over, True).start()
        for kind in (0, 1):
            wide(kind, 0, over).start()
    copies[3].wait()
    for over in range(1, f):
        row(over).wait_recv()
    gather_out.begin()
    each = -(-(n - 1) // (hops - 1))
    for i in range(hops):
        gather.pass_on(i)
        gather_out.pass_on(i)
        if i:
            for step in range((i - 1) * each + 1, min(i * each, n - 1) + 1):
                for kind in (1, 0):
                    push(kind, step).wait_recv()
                    for over in range(1, f):
                        aside(kind, step, over, False).start()
        for over in range(1, f):
            for kind in (0, 1):
                wide(kind, i + 1, over).start()
    gather.finish()
    for copy in copies[:3]:
        copy.wait()
    for step in range(1, n):
        push(2, step).wait_recv()
        for kind in (0, 1, 2):
            push(kind, step).wait_send()
    for step in range(n):
        for kind in (0, 1):
            for over in range(1, f):
                aside(kind, step, over, False).wait()

    lanes = lax.broadcasted_iota(jnp.int32, (32, small.shape[1]), 1)
    places = lax.broadcasted_iota(jnp.int32, (32, small.shape[1]), 0)
    chosen = jnp.where(lanes == places, 1.0, 0.0).astype(BF16)
    for c in range(n):
        for x in range(f):
            start = (c * f + x) * rows
            flipped = dot(chosen, small_all[c, x], BY_LAST)
            router[:, start : start + rows] = flipped[0:experts, :].astype(BF16)
            gains[:, start : start + rows] = flipped[experts : experts + 8, :]

    def out(c):
        return pltpu.make_async_copy(near.at[c], hidden_all.at[c], out_sem.at[c])

    def project(c, carry):
        value = near[c].astype(F32)
        inverse = lax.rsqrt(jnp.mean(value * value, -1, keepdims=True) + EPS)
        near[c] = (value * inverse * gains[0:1, :]).astype(BF16)
        out(c).start()
        here = pl.ds(pl.multiple_of(c * tok, tok), tok)
        total = jnp.zeros((tok, w_head.shape[3]), F32)
        for k in range(n):
            for x in range(f):
                start = (k * f + x) * rows
                if (k * f + x) % (256 // rows):
                    continue
                wide_rows = 256 // rows
                if wide_rows <= f:
                    right = w_head[k, x : x + wide_rows]
                else:
                    right = w_head[k : k + wide_rows // f]
                right = right.reshape(256, w_head.shape[3])
                total = total + dot(near[c, :, start : start + 256], right, MATMUL)
        mixed[here, :] = total
        return carry

    lax.fori_loop(0, n, project, 0)
    for c in range(n):
        out(c).wait()
    gather_out.finish()
    for over in range(1, f):
        row(over).wait_send()
        for kind in (0, 1):
            for part in range(ring.chips):
                wide(kind, part, over).wait()


def first_gather(n, f, own, by_head, small, routes, w_out, w_gate, w_up):
    tok, width = own.shape
    experts = by_head.shape[0]
    kind = pltpu.SemaphoreType.DMA
    shape = jax.ShapeDtypeStruct
    return pl.pallas_call(
        partial(first_kernel, n, f),
        out_shape=[
            shape((n, tok, width), BF16),
            shape((n * tok, by_head.shape[2]), F32),
            shape((n, f) + by_head.shape[1:], BF16),
            shape((experts, width), BF16),
            shape((8, width), F32),
            shape((n,) + routes.shape, jnp.int32),
            shape((max(f - 1, 1),) + w_up.shape, BF16),
            shape((max(f - 1, 1),) + w_up.shape, BF16),
            shape((n, f * w_out.shape[0], w_out.shape[1]), BF16),
        ],
        in_specs=[VMEM] * 5 + [ANY] * 2,
        out_specs=[ANY] + [VMEM] * 4 + [ANY] * 4,
        scratch_shapes=[
            pltpu.VMEM((n, tok, width), BF16),
            pltpu.VMEM((n, f) + small.shape, BF16),
            pltpu.VMEM((f * w_out.shape[0], w_out.shape[1]), BF16),
        ]
        + Gather.semaphores(n)
        + Gather.semaphores(n)
        + [kind((3, n)), kind((3, n)), kind((2, n, f)), kind((2, n, f)), kind((4,))]
        + [kind((2, n // 2, f)), kind((2, n // 2, f)), kind((f,)), kind((f,)), kind((n,))],
        compiler_params=pltpu.CompilerParams(
            collective_id=0, has_side_effects=True, vmem_limit_bytes=56 << 20
        ),
        name="first_gather",
    )(own, by_head, small, routes, w_out, w_gate, w_up)


def blocks_of(length):
    block = min(512, length)
    return block, length // block


def across_lanes(value):
    ones = jnp.ones((8, value.shape[1]), F32)
    total = lax.dot_general(
        ones, value, BY_LAST, precision=lax.Precision.HIGHEST, preferred_element_type=F32
    )
    return total[0:1, :]


def to_column(table, index, lanes):
    rows = lax.broadcasted_iota(jnp.int32, (table.shape[0], lanes), 0)
    chosen = jnp.where(rows == index, 1.0, 0.0)
    return lax.dot_general(
        table, chosen, BY_FIRST, precision=lax.Precision.HIGHEST, preferred_element_type=F32
    )


def half_turn(value, first_sign):
    half = value.shape[1] // 2
    lanes = lax.broadcasted_iota(jnp.int32, value.shape, 1)
    sign = jnp.where(lanes < half, first_sign, -first_sign)
    return pltpu.roll(value, half, 1) * sign


class Spread:
    def __init__(self, ring, block, out, sems):
        self.ring, self.block, self.out = ring, block, out
        self.send, self.recv, self.keep = sems

    @staticmethod
    def semaphores(n):
        kind = pltpu.SemaphoreType.DMA
        return [kind((n,)), kind((n,)), kind((1,))]

    def push(self, step):
        return remote(
            self.block,
            self.out.at[self.ring.me],
            self.send.at[step],
            self.recv.at[step],
            {"seq": self.ring.peer(step)},
        )

    def local(self):
        return pltpu.make_async_copy(self.block, self.out.at[self.ring.me], self.keep.at[0])

    def begin(self):
        for step in range(1, self.ring.n):
            self.push(step).start()
        self.local().start()

    def finish(self):
        for step in range(1, self.ring.n):
            self.push(step).wait()
        self.local().wait()

    def total(self):
        total = self.out[0]
        for device in range(1, self.ring.n):
            total = total + self.out[device]
        return total


def attention_kernel(n, f, factor, *refs):
    mixed, tables, starts, gains, upstream = refs[:5]
    q_ref, k_ref, v_ref, out_ref, exact_ref, sums_ref, squares = refs[5:12]
    cosine, sine, upstream_all = refs[12:15]
    partial_sums, arrived = refs[15:17]
    sems, walk_sems = refs[17:20], refs[20:]
    ring = Ring(n, f)
    length, head = q_ref.shape
    width = head * n
    block, count = blocks_of(length)
    greet(ring, True, False)
    walk = Gather(ring, upstream, upstream_all, walk_sems)
    walk.begin()
    last = walk.last
    tok = tables.shape[1]

    def measure(b, carry):
        here = pl.ds(pl.multiple_of(b * block, block), block)
        for kind in (0, 1):
            raw = mixed[here, kind * head : (kind + 1) * head]
            partial_sums[pl.ds(kind * count + b, 1), :] = across_lanes(raw * raw)
        v_ref[here, :] = mixed[here, 2 * head :].astype(BF16)
        return carry

    lax.fori_loop(0, count, measure, 0)
    spread = Spread(ring, partial_sums, arrived, sems)
    spread.begin()

    def angles(c, carry):
        here = pl.ds(pl.multiple_of(c * tok, tok), tok)
        cosine[here, :] = starts[0, c] * tables[0] - starts[1, c] * tables[1]
        sine[here, :] = starts[1, c] * tables[0] + starts[0, c] * tables[1]
        return carry

    lax.fori_loop(0, n, angles, 0)
    spread.finish()
    squares[...] = spread.total()
    walk.pass_on(0)

    def prepare(b, carry):
        here = pl.ds(pl.multiple_of(b * block, block), block)
        for kind, target in ((0, q_ref), (1, k_ref)):
            inverse = lax.rsqrt(to_column(squares[...], kind * count + b, head) / width + EPS)
            raw = mixed[here, kind * head : (kind + 1) * head]
            normed = raw * inverse * gains[kind + 1 : kind + 2, :]
            turned = half_turn(normed, -1.0)
            target[here, :] = (normed * cosine[here, :] + turned * sine[here, :]).astype(BF16)
        return carry

    lax.fori_loop(0, count, prepare, 0)
    rows = lax.broadcasted_iota(jnp.int32, (block, block), 0)
    cols = lax.broadcasted_iota(jnp.int32, (block, block), 1)

    def outer(i, carry):
        here = pl.ds(pl.multiple_of(i * block, block), block)
        part = q_ref[here, :]

        def inner(j, state, masked):
            top, total, acc = state
            there = pl.ds(pl.multiple_of(j * block, block), block)
            scores = dot(part, k_ref[there, :], BY_LAST) * factor
            if masked:
                scores = jnp.where(cols <= rows, scores, NEG)
            new = jnp.maximum(top, jnp.max(scores, -1, keepdims=True))
            scale = jnp.exp(top - new)
            expd = jnp.exp(scores - new)
            total = total * scale + jnp.sum(expd, -1, keepdims=True)
            acc = acc * scale + dot(expd.astype(BF16), v_ref[there, :], MATMUL)
            return new, total, acc

        state = (
            jnp.full((block, 1), NEG, F32),
            jnp.zeros((block, 1), F32),
            jnp.zeros((block, head), F32),
        )
        state = lax.fori_loop(0, i, lambda j, s: inner(j, s, False), state)
        top, total, acc = inner(i, state, True)
        exact = acc / total
        exact_ref[here, :] = exact
        out_ref[here, :] = exact.astype(BF16)
        column = jnp.broadcast_to(top + jnp.log(total), (block, 128))
        sums_ref[:, here] = jnp.transpose(column)[0:8, :]

        @pl.when((i > 0) & (i < last))
        def _():
            walk.pass_on(i)

        return carry

    lax.fori_loop(0, count, outer, 0)
    for i in range(count, last):
        walk.pass_on(i)
    walk.finish()


def attention(n, f, mixed, tables, starts, gains, upstream, factor):
    length, head = mixed.shape[0], mixed.shape[1] // 3
    block, count = blocks_of(length)
    shape = jax.ShapeDtypeStruct
    return pl.pallas_call(
        partial(attention_kernel, n, f, factor),
        out_shape=[
            shape((length, head), BF16),
            shape((length, head), BF16),
            shape((length, head), BF16),
            shape((length, head), BF16),
            shape((length, head), F32),
            shape((8, length), F32),
            shape((2 * count, block), F32),
            shape((length, head), F32),
            shape((length, head), F32),
            shape((n,) + upstream.shape, BF16),
        ],
        in_specs=[VMEM] * 5,
        out_specs=[VMEM] * 9 + [ANY],
        scratch_shapes=[
            pltpu.VMEM((2 * count, block), F32),
            pltpu.VMEM((n, 2 * count, block), F32),
        ]
        + Spread.semaphores(n)
        + Gather.semaphores(n),
        compiler_params=pltpu.CompilerParams(
            collective_id=5, has_side_effects=True, vmem_limit_bytes=40 << 20
        ),
        cost_estimate=pl.CostEstimate(
            flops=2 * length * length * head,
            transcendentals=length * length // 2,
            bytes_accessed=8 * length * head,
        ),
        name="attention",
    )(mixed, tables, starts, gains, upstream)


def attention_back_kernel(n, f, factor, *refs):
    q_ref, k_ref, v_ref, d_ref, sums_ref, exact, mixed, cosine, sine, gains, squares = refs[:11]
    d_attn = refs[11]
    far = refs[12:15]
    d_mixed, gain_head, d_attn_all, third, qkv_part = refs[15:20]
    dq_ref, dk_ref, dv_ref, delta, partial_sums, arrived = refs[20:26]
    near = refs[26:29]
    d_in, inner_in, hidden = near
    walk_sems, spread_sems, load_sem = refs[29:34], refs[34:37], refs[37]
    ring = Ring(n, f)
    length, head = q_ref.shape
    width = head * n
    block, count = blocks_of(length)
    greet(ring, True, False)
    walk = Gather(ring, d_attn, d_attn_all, walk_sems)
    walk.begin()
    last = walk.last
    loads = [
        pltpu.make_async_copy(source, target, load_sem.at[k])
        for k, (source, target) in enumerate(zip(far, near))
    ]
    for load in loads:
        load.start()
    dq_ref[...] = jnp.zeros_like(dq_ref)

    def measure(b, carry):
        here = pl.ds(pl.multiple_of(b * block, block), block)
        value = across_lanes(d_ref[here, :].astype(F32) * exact[here, :])
        delta[:, here] = jnp.broadcast_to(value, (8, block))
        return carry

    lax.fori_loop(0, count, measure, 0)
    rows = lax.broadcasted_iota(jnp.int32, (block, block), 0)
    cols = lax.broadcasted_iota(jnp.int32, (block, block), 1)

    def outer(j, carry):
        there = pl.ds(pl.multiple_of(j * block, block), block)
        keys = k_ref[there, :]
        values = v_ref[there, :]

        def inner(i, state, masked):
            d_keys, d_values = state
            here = pl.ds(pl.multiple_of(i * block, block), block)
            part = q_ref[here, :]
            d_part = d_ref[here, :]
            scores = dot(keys, part, BY_LAST) * factor
            if masked:
                scores = jnp.where(rows <= cols, scores, NEG)
            probs = jnp.exp(scores - sums_ref[0:1, here])
            d_probs = dot(values, d_part, BY_LAST)
            d_scores = (probs * (d_probs - delta[0:1, here])).astype(BF16)
            d_values = d_values + dot(probs.astype(BF16), d_part, MATMUL)
            d_keys = d_keys + dot(d_scores, part, MATMUL)
            dq_ref[here, :] += dot(d_scores, keys, BY_FIRST)
            return d_keys, d_values

        zero = jnp.zeros((block, head), F32)
        state = inner(j, (zero, zero), True)
        state = lax.fori_loop(j + 1, count, lambda i, s: inner(i, s, False), state)
        dk_ref[there, :] = state[0]
        dv_ref[there, :] = state[1]

        @pl.when((j >= 1) & (j < last + 1))
        def _():
            walk.pass_on(j - 1)

        return carry

    lax.fori_loop(0, count, outer, 0)

    def unturn(b, carry):
        here = pl.ds(pl.multiple_of(b * block, block), block)
        for kind, source in ((0, dq_ref), (1, dk_ref)):
            grad = (source[here, :] * factor).astype(BF16).astype(F32)
            grad = grad * cosine[here, :] + half_turn(grad * sine[here, :], 1.0)
            source[here, :] = grad
            raw = mixed[here, kind * head : (kind + 1) * head]
            partial_sums[pl.ds(kind * count + b, 1), :] = across_lanes(
                raw * gains[kind + 1 : kind + 2, :] * grad
            )
        return carry

    lax.fori_loop(0, count, unturn, 0)
    spread = Spread(ring, partial_sums, arrived, spread_sems)
    spread.begin()
    walk.pass_on(count - 1)
    units = third.shape[2]
    for load in loads:
        load.wait()

    def products(tile, tiles):
        size = d_in.shape[1] // tiles
        these = pl.ds(pl.multiple_of(tile * size, size), size)
        for j in range(1, f):
            part = slice(j * units, (j + 1) * units)
            third[j - 1, these, :] = dot(d_in[:, these], inner_in[:, part], BY_FIRST).astype(BF16)

    def some(tile, carry):
        products(tile, 8)
        return carry

    spread.finish()
    total = spread.total()
    gain_head[...] = jnp.zeros_like(gain_head)

    def close(b, carry):
        here = pl.ds(pl.multiple_of(b * block, block), block)
        for kind, source in ((0, dq_ref), (1, dk_ref)):
            index = kind * count + b
            inverse = lax.rsqrt(to_column(squares[...], index, head) / width + EPS)
            inner = to_column(total, index, head) / width
            raw = mixed[here, kind * head : (kind + 1) * head]
            grad = source[here, :]
            value = inverse * gains[kind + 1 : kind + 2, :] * grad
            value = value - raw * (inverse * inverse * inverse) * inner
            d_mixed[here, kind * head : (kind + 1) * head] = value.astype(BF16)
            gain_head[kind + 2 : kind + 3, :] += jnp.sum(raw * inverse * grad, 0, keepdims=True)
        d_mixed[here, 2 * head :] = dv_ref[here, :].astype(BF16)
        return carry

    lax.fori_loop(0, count, close, 0)
    walk.pass_on(count)
    chunks, beside, rows_each = qkv_part.shape[1], qkv_part.shape[0], qkv_part.shape[2]
    span = width // chunks

    def weigh(c, carry):
        these = pl.ds(pl.multiple_of(c * span, span), span)
        value = dot(hidden[:, these], d_mixed[...], BY_FIRST).astype(BF16)
        for x in range(beside):
            qkv_part[x, c] = value[x * rows_each : (x + 1) * rows_each]
        return carry

    lax.fori_loop(0, chunks, weigh, 0)
    for i in range(count + 1, last):
        walk.pass_on(i)
        if i == count + 1:
            lax.fori_loop(0, 8, some, 0)
    walk.finish()


def attention_back(
    n, f, queries, keys, values, d_out, sums, exact, mixed, cosine, sine, gains, squares,
    d_attn, d_in, inner_in, hidden, rows, factor
):
    length, head = queries.shape
    tok, width = d_attn.shape
    block, count = blocks_of(length)
    shape = jax.ShapeDtypeStruct
    units = inner_in.shape[1] // f
    grad = shape((max(f - 1, 1), width, units), BF16)
    return pl.pallas_call(
        partial(attention_back_kernel, n, f, factor),
        out_shape=[
            shape((length, 3 * head), BF16),
            shape((8, head), F32),
            shape((n, tok, width), BF16),
            grad,
            shape((f, n, rows, 3 * head), BF16),
        ],
        in_specs=[VMEM] * 12 + [ANY] * 3,
        out_specs=[VMEM, VMEM, ANY] + [VMEM] * 2,
        scratch_shapes=[pltpu.VMEM((length, head), F32)] * 3
        + [
            pltpu.VMEM((8, length), F32),
            pltpu.VMEM((2 * count, block), F32),
            pltpu.VMEM((n, 2 * count, block), F32),
            pltpu.VMEM(d_in.shape, BF16),
            pltpu.VMEM(inner_in.shape, BF16),
            pltpu.VMEM(hidden.shape, BF16),
        ]
        + Gather.semaphores(n)
        + Spread.semaphores(n)
        + [pltpu.SemaphoreType.DMA((3,))],
        compiler_params=pltpu.CompilerParams(
            collective_id=6, has_side_effects=True, vmem_limit_bytes=64 << 20
        ),
        name="attention_back",
    )(
        queries, keys, values, d_out, sums, exact, mixed, cosine, sine, gains, squares,
        d_attn, d_in, inner_in, hidden
    )


def core_kernel(n, f, *refs):
    attended, w_out, tokens, upstream, gain, router, routes, routes_all, upstream_all = refs[:9]
    shards_in = refs[9 : 9 + 3 * f]
    refs = refs[9 + 3 * f :]
    d_middle, middle, d_attn, d_attended, d_logits_all, gain_two = refs[:6]
    own_hidden, rows_out, d_out, inner_out, d_gate_out, d_up_out, moe_out = refs[6:13]
    refs = refs[13:]
    w_near, w_gate, w_up, w_down, by_token, d_logits, arrived, outgoing, weights_in = refs[:9]
    refs = refs[9:]
    ring_in, mate_near, d_mate_in, coming, going, d_mate_out, own, lift = refs[:8]
    refs = refs[8:]
    rows_now, lifted, d_now, inner_now, d_gate_now, d_up_now, moe_now, d_weight, places = refs[:9]
    refs = refs[9:]
    hop_send, hop_recv, share_send, share_recv, swap_send, swap_recv = refs[:6]
    sum_send, sum_recv, send, recv, keep, load_sem, lift_sem, stage_sem, own_sem = refs[6:]
    ring = Ring(n, f)
    tok, width = tokens.shape
    head = width // n
    chips = ring.chips
    last = chips - 1
    capacity = rows_now.shape[1] // 2
    hidden_units = w_gate.shape[1]
    piece = tok // PIECES
    sign = 1 - 2 * ring.core
    onward = ring.at(ring.pos + sign + chips)
    local_units = hidden_units // f

    loads = [pltpu.make_async_copy(w_out, w_near, keep.at[0])]
    for kind, target in enumerate((w_gate, w_up, w_down)):
        for j in range(f):
            cols = slice(j * local_units, (j + 1) * local_units)
            loads.append(
                pltpu.make_async_copy(
                    shards_in[kind * f + j], target.at[:, cols], load_sem.at[kind, j]
                )
            )
    for load in loads:
        load.start()

    def chunk_of(i, other):
        return ring.at(
            ring.pos + (sign * (1 + i) if other else -sign * (1 + i)) + 2 * chips, other
        )

    def lift_copy(i, other):
        slot = lax.rem(i, 2)
        return pltpu.make_async_copy(
            upstream_all.at[chunk_of(i, other)],
            lift.at[slot, other],
            lift_sem.at[slot, other],
        )

    lift_copy(0, 0).start()
    lift_copy(0, 1).start()
    greet(ring, True, False)

    def deal(step):
        cols = pl.ds(pl.multiple_of(ring.me * head, head), head)
        there = ring.peer(step)
        return remote(
            attended.at[there],
            by_token.at[:, cols],
            send.at[0, step],
            recv.at[0, step],
            {"seq": there},
        )

    for step in range(1, n):
        deal(step).start()
    mine = pl.ds(pl.multiple_of(ring.me * head, head), head)
    by_token[:, mine] = attended[ring.me]

    before = lax.broadcasted_iota(jnp.int32, (tok, tok), 0)
    after = lax.broadcasted_iota(jnp.int32, (tok, tok), 1)
    earlier = jnp.where(before < after, 1.0, 0.0).astype(BF16)
    for c in range(n):
        here = jnp.where(routes_all[c] == ring.me, 1.0, 0.0)
        here = jnp.sum(here, 0, keepdims=True)
        count = dot(jnp.broadcast_to(here, (8, tok)).astype(BF16), earlier, MATMUL)
        places[c] = jnp.where(jnp.broadcast_to(here, (8, tok)) > 0.5, count, -1.0)

    loads[0].wait()
    for step in range(1, n):
        deal(step).wait()
    tile = min(512, width)
    squares = jnp.zeros((tok, 1), F32)
    for start in range(0, width, tile):
        cols = slice(start, start + tile)
        value = tokens[:, cols].astype(F32) + dot(by_token[...], w_near[:, cols], MATMUL)
        middle[:, cols] = value
        squares = squares + jnp.sum(value * value, -1, keepdims=True)
    inverse = lax.rsqrt(squares / width + EPS)
    ring_in[last] = (middle[...] * inverse * gain[...]).astype(BF16)

    def hop(i, s):
        rows = pl.ds(s * piece, piece)
        source = lax.rem(i + last, chips)
        return remote(
            ring_in.at[source, rows],
            ring_in.at[i, rows],
            hop_send.at[i, s],
            hop_recv.at[i, s],
            {"seq": onward},
        )

    def share(i, s):
        rows = pl.ds(s * piece, piece)
        return remote(
            ring_in.at[i, rows],
            mate_near.at[i, rows],
            share_send.at[i, s],
            share_recv.at[i, s],
            {"seq": ring.mate},
        )

    for s in range(PIECES):
        hop(0, s).start()
    for s in range(PIECES):
        share(last, s).start()

    logits = dot(router[...], ring_in[last], BY_LAST)
    expd = jnp.exp(logits - jnp.max(logits, 0, keepdims=True))
    gate = expd / jnp.sum(expd, 0, keepdims=True)
    experts = lax.broadcasted_iota(jnp.int32, gate.shape, 0)
    named = jnp.zeros(gate.shape, F32)
    for k in range(routes.shape[0]):
        named = named + jnp.where(routes[k : k + 1, :] == experts, 1.0, 0.0)
    weights = gate * named
    for e in range(n):
        outgoing[e] = jnp.broadcast_to(weights[e : e + 1, :], (8, tok))

    def push(there):
        return remote(
            outgoing.at[there],
            weights_in.at[ring.me],
            send.at[1, there],
            recv.at[1, ring.me],
            {"seq": there},
        )

    def pushed(origin):
        return remote(
            outgoing.at[origin],
            weights_in.at[origin],
            send.at[1, origin],
            recv.at[1, origin],
            {"seq": origin},
        )

    for step in range(1, n):
        push(ring.peer(step)).start()
    weights_in[ring.me] = outgoing[ring.me]
    for load in loads[1:]:
        load.wait()

    def swap(i):
        return remote(
            d_mate_out.at[lax.rem(i, 2)],
            d_mate_in.at[i],
            swap_send.at[i],
            swap_recv.at[i],
            {"seq": ring.mate},
        )

    def sum_hop(i, s):
        rows = pl.ds(s * piece, piece)
        return remote(
            going.at[lax.rem(i, 2), rows],
            coming.at[i, rows],
            sum_send.at[i, s],
            sum_recv.at[i, s],
            {"seq": onward},
        )

    def sum_step(i):
        swap(i).wait_recv()

        @pl.when(i >= 2)
        def _():
            for s in range(PIECES):
                sum_hop(i - 2, s).wait_send()

        for s in range(PIECES):
            rows = pl.ds(s * piece, piece)

            @pl.when(i > 0)
            def _():
                sum_hop(i - 1, s).wait_recv()
                own[rows, :] = own[rows, :] + coming[i - 1, rows].astype(F32)

            value = own[rows, :] + d_mate_in[i, rows].astype(F32)
            going[lax.rem(i, 2), rows] = value.astype(BF16)
            sum_hop(i, s).start()

    def give(kind, target, other, slot):
        chunk = target
        source, sink = [
            (rows_now, rows_out),
            (d_now, d_out),
            (inner_now, inner_out),
            (d_gate_now, d_gate_out),
            (d_up_now, d_up_out),
            (moe_now, moe_out),
        ][kind]
        size = tok if kind == 5 else capacity
        return pltpu.make_async_copy(
            source.at[slot, pl.ds(other * size, size)],
            sink.at[chunk],
            stage_sem.at[slot, kind, other],
        )

    def keep_hidden(i, other):
        return pltpu.make_async_copy(
            (mate_near if other else ring_in).at[i, :, mine],
            own_hidden.at[chunk_of(i, other)],
            own_sem.at[other, i],
        )

    def report(there, slot, other):
        return remote(
            d_weight.at[slot, other],
            arrived.at[ring.me],
            send.at[2, there],
            recv.at[2, ring.me],
            {"seq": there},
        )

    def reported(origin):
        return remote(
            d_weight.at[0, 0],
            arrived.at[origin],
            send.at[2, origin],
            recv.at[2, origin],
            {"seq": origin},
        )

    def pass_on(i):
        for s in range(PIECES):
            hop(i, s).wait_recv()

            @pl.when(i < last - 1)
            def _():
                hop(i + 1, s).start()

            share(i, s).start()

    def work(i):
        slot = lax.rem(i, 2)
        chunks = (chunk_of(i, 0), chunk_of(i, 1))
        for s in range(PIECES):
            share(i, s).wait_recv()
        keep_hidden(i, 0).start()
        keep_hidden(i, 1).start()
        for other in (0, 1):
            lift_copy(i, other).wait()

        @pl.when(i < last)
        def _():
            lift_copy(i + 1, 0).start()
            lift_copy(i + 1, 1).start()
            pushed(chunks[0]).wait_recv()

        pushed(chunks[1]).wait_recv()

        @pl.when(i >= 2)
        def _():
            for kind in range(6):
                for other in (0, 1):
                    give(kind, chunks[other], other, slot).wait()
            swap(i - 2).wait_send()
            for other in (0, 1):
                report(chunk_of(i - 2, other), slot, other).wait_send()

        slots = lax.broadcasted_iota(jnp.int32, (capacity, tok), 0).astype(F32)
        picks, rates = [], []
        for other in (0, 1):
            rows = slice(other * capacity, (other + 1) * capacity)
            where = slots == jnp.broadcast_to(places[chunks[other], 0:1, :], (capacity, tok))
            pick = jnp.where(where, 1.0, 0.0)
            low = pick.astype(BF16)
            source = mate_near.at[i] if other else ring_in.at[i]
            share_of = weights_in[chunks[other], 0:1, :]
            rate = jnp.sum(jnp.where(where, share_of, 0.0), -1, keepdims=True)
            for start in range(0, width, tile):
                cols = slice(start, start + tile)
                rows_now[slot, rows, cols] = dot(low, source[:, cols], MATMUL).astype(BF16)
                picked = dot(low, lift[slot, other, :, cols], MATMUL)
                lifted[rows, cols] = picked.astype(BF16)
                d_now[slot, rows, cols] = (rate * picked).astype(BF16)
            picks.append((low, where))
            rates.append(rate)
        rate = jnp.concatenate(rates, 0)
        unit = min(256, hidden_units)
        for start in range(0, hidden_units, unit):
            cols = slice(start, start + unit)
            gate_act = dot(rows_now[slot], w_gate[:, cols], MATMUL)
            up_act = dot(rows_now[slot], w_up[:, cols], MATMUL)
            d_inner = dot(d_now[slot], w_down[:, cols], MATMUL)
            sigma = 1.0 / (1.0 + jnp.exp(-gate_act))
            silu = gate_act * sigma
            inner_now[slot, :, cols] = (silu * up_act).astype(BF16)
            d_gate_now[slot, :, cols] = (
                d_inner * up_act * sigma * (1.0 + gate_act * (1.0 - sigma))
            ).astype(BF16)
            d_up_now[slot, :, cols] = (d_inner * silu).astype(BF16)
        inner_product = jnp.zeros((2 * capacity, 1), F32)
        for start in range(0, width, tile):
            cols = slice(start, start + tile)
            produced = dot(inner_now[slot], w_down[cols, :], BY_LAST)
            produced = produced.astype(BF16).astype(F32)
            inner_product = inner_product + jnp.sum(
                produced * lifted[:, cols].astype(F32), -1, keepdims=True
            )
            scaled = (rate * produced).astype(BF16)
            d_rows = dot(d_gate_now[slot], w_gate[cols, :], BY_LAST)
            d_rows = (d_rows + dot(d_up_now[slot], w_up[cols, :], BY_LAST)).astype(BF16)
            for other in (0, 1):
                rows = slice(other * capacity, (other + 1) * capacity)
                low = picks[other][0]
                moe_now[slot, other * tok : (other + 1) * tok, cols] = dot(
                    low, scaled[rows], BY_FIRST
                ).astype(BF16)
                spread_rows = dot(low, d_rows[rows], BY_FIRST)
                if other:
                    d_mate_out[slot, :, cols] = spread_rows.astype(BF16)
                else:
                    own[:, cols] = spread_rows
        swap(i).start()
        for kind in range(6):
            for other in (0, 1):
                give(kind, chunks[other], other, slot).start()
        for other in (0, 1):
            rows = slice(other * capacity, (other + 1) * capacity)
            value = jnp.sum(
                jnp.where(picks[other][1], inner_product[rows], 0.0), 0, keepdims=True
            )
            d_weight[slot, other] = jnp.broadcast_to(value, (8, tok))
        report(chunks[1], slot, 1).start()

        @pl.when(i < last)
        def _():
            report(chunks[0], slot, 0).start()

    pass_on(0)
    work(0)

    def body(i, carry):
        @pl.when(i < last)
        def _():
            pass_on(i)

        sum_step(i - 1)
        work(i)
        return carry

    lax.fori_loop(1, chips, body, 0)
    arrived[ring.me] = d_weight[last % 2, 0]
    for step in range(1, n):
        reported(ring.peer(step)).wait_recv()
    gate_back = jnp.concatenate([arrived[e, 0:1, :] for e in range(n)], 0)
    gate_back = gate * (gate_back - jnp.sum(gate * gate_back, 0, keepdims=True))
    d_logits[...] = gate_back.astype(BF16)

    def publish(step):
        return remote(
            d_logits,
            d_logits_all.at[ring.me],
            send.at[4, step],
            recv.at[4, step],
            {"seq": ring.peer(step)},
        )

    kept = pltpu.make_async_copy(d_logits, d_logits_all.at[ring.me], keep.at[1])
    swap(last).wait_recv()
    for s in range(PIECES):
        rows = pl.ds(s * piece, piece)
        sum_hop(last - 1, s).wait_recv()
        value = own[rows, :] + d_mate_in[last, rows].astype(F32)
        own[rows, :] = value + coming[last - 1, rows].astype(F32)
    d_hidden = own[...] + dot(gate_back.astype(BF16), router[...], BY_FIRST)
    value = middle[...]
    inner = jnp.mean(value * gain[...] * d_hidden, -1, keepdims=True)
    gain_two[...] = jnp.sum(value * inverse * d_hidden, 0, keepdims=True)
    d_value = inverse * gain[...] * d_hidden - value * (inverse * inverse * inverse) * inner
    d_value = upstream[...].astype(F32) + d_value
    d_middle[...] = d_value
    d_attn[...] = d_value.astype(BF16)
    for start in range(0, width, tile):
        cols = slice(start, start + tile)
        by_token[:, cols] = dot(d_attn[...], w_near[cols, :], BY_LAST).astype(BF16)

    def deal_back(step):
        there = ring.peer(step)
        cols = pl.ds(pl.multiple_of(there * head, head), head)
        return remote(
            by_token.at[:, cols],
            d_attended.at[ring.me],
            send.at[3, step],
            recv.at[3, step],
            {"seq": there},
        )

    for step in range(1, n):
        deal_back(step).start()
    d_attended[ring.me] = by_token[:, mine]
    for step in range(1, n):
        publish(step).start()
    kept.start()

    for s in range(PIECES):
        share(last, s).wait_send()

    def settle(i, carry):
        for s in range(PIECES):
            hop(i, s).wait_send()
            share(i, s).wait_send()
        for other in (0, 1):
            keep_hidden(i, other).wait()
        return carry

    lax.fori_loop(0, last, settle, 0)
    for other in (0, 1):
        keep_hidden(last, other).wait()
    for s in range(PIECES):
        sum_hop(last - 2, s).wait_send()
        sum_hop(last - 1, s).wait_send()
    for i in (last - 1, last):
        swap(i).wait_send()
        for other in (0, 1):
            for kind in range(6):
                give(kind, chunk_of(i, other), other, i % 2).wait()
            if other or i < last:
                report(chunk_of(i, other), i % 2, other).wait_send()
    for step in range(1, n):
        push(ring.peer(step)).wait_send()
    for step in range(1, n):
        deal_back(step).wait()
        publish(step).wait()
    kept.wait()


def core_stage(
    n, f, attended, w_out, tokens, upstream, gain, router, routes, routes_all, upstream_all, halves
):
    tok, width = tokens.shape
    experts = router.shape[0]
    units = f * halves[0].shape[1]
    capacity = min(tok, 5 * tok * TOPK // (4 * experts))
    chips = n // 2
    kind = pltpu.SemaphoreType.DMA
    shape = jax.ShapeDtypeStruct
    rows = 2 * capacity
    return pl.pallas_call(
        partial(core_kernel, n, f),
        out_shape=[
            shape((tok, width), F32),
            shape((tok, width), F32),
            shape((tok, width), BF16),
            shape((n, tok, width // n), BF16),
            shape((n, experts, tok), BF16),
            shape((1, width), F32),
            shape((n, tok, width // n), BF16),
            shape((n, capacity, width), BF16),
            shape((n, capacity, width), BF16),
            shape((n, capacity, units), BF16),
            shape((n, capacity, units), BF16),
            shape((n, capacity, units), BF16),
            shape((n, tok, width), BF16),
        ],
        in_specs=[VMEM, ANY] + [VMEM] * 6 + [ANY] * (1 + 3 * f),
        out_specs=[VMEM] * 4 + [ANY, VMEM] + [ANY] * 7,
        scratch_shapes=[
            pltpu.VMEM((width, width), BF16),
            pltpu.VMEM((width, units), BF16),
            pltpu.VMEM((width, units), BF16),
            pltpu.VMEM((width, units), BF16),
            pltpu.VMEM((tok, width), BF16),
            pltpu.VMEM((experts, tok), BF16),
            pltpu.VMEM((n, 8, tok), F32),
            pltpu.VMEM((n, 8, tok), F32),
            pltpu.VMEM((n, 8, tok), F32),
            pltpu.VMEM((chips, tok, width), BF16),
            pltpu.VMEM((chips, tok, width), BF16),
            pltpu.VMEM((chips, tok, width), BF16),
            pltpu.VMEM((chips - 1, tok, width), BF16),
            pltpu.VMEM((2, tok, width), BF16),
            pltpu.VMEM((2, tok, width), BF16),
            pltpu.VMEM((tok, width), F32),
            pltpu.VMEM((2, 2, tok, width), BF16),
            pltpu.VMEM((2, rows, width), BF16),
            pltpu.VMEM((rows, width), BF16),
            pltpu.VMEM((2, rows, width), BF16),
            pltpu.VMEM((2, rows, units), BF16),
            pltpu.VMEM((2, rows, units), BF16),
            pltpu.VMEM((2, rows, units), BF16),
            pltpu.VMEM((2, 2 * tok, width), BF16),
            pltpu.VMEM((2, 2, 8, tok), F32),
            pltpu.VMEM((n, 8, tok), F32),
            kind((chips, PIECES)),
            kind((chips, PIECES)),
            kind((chips, PIECES)),
            kind((chips, PIECES)),
            kind((chips,)),
            kind((chips,)),
            kind((chips, PIECES)),
            kind((chips, PIECES)),
            kind((5, n)),
            kind((5, n)),
            kind((2,)),
            kind((3, f)),
            kind((2, 2)),
            kind((2, 6, 2)),
            kind((2, chips)),
        ],
        compiler_params=pltpu.CompilerParams(
            collective_id=1, has_side_effects=True, vmem_limit_bytes=67_000_000
        ),
        name="core_stage",
    )(attended, w_out, tokens, upstream, gain, router, routes, routes_all, upstream_all, *halves)


def last_kernel(n, f, *refs):
    d_mixed, w_head, qkv_part, tokens, gain, d_middle, gain_two, gain_head = refs[:8]
    middle, third, moe_part = refs[8:11]
    far_refs = refs[11:16]
    d_inputs, qkv_rows, gains_out, third_in, grads_out, result = refs[16:22]
    beside_rows, summed, gain_rows, gain_in, gain_side, stage = refs[22:28]
    near_refs = refs[28:33]
    rows_in, d_in, d_gate, d_up, inner_in = near_refs
    buffers, fold_sems = refs[33:38], refs[38:42]
    stored_buffers, stored_sems = refs[42:46], refs[46:51]
    side_send, side_recv, send, recv, keep, stage_sem, load_sem = refs[51:]
    ring = Ring(n, f)
    _, width = tokens.shape
    slice_width = width // n
    units = grads_out.shape[2]
    chips = ring.chips
    size = width // chips
    loads = [
        pltpu.make_async_copy(source if k < 2 else source.at[:, :units], target, load_sem.at[k])
        for k, (source, target) in enumerate(zip(far_refs, near_refs))
    ]
    greet(ring, True, True)

    def side(step):
        there = ring.beside(step)
        return remote(
            qkv_part.at[there],
            beside_rows.at[step - 1],
            side_send.at[0, step],
            side_recv.at[0, step],
            {"fsdp": there},
        )

    for step in range(1, f):
        side(step).start()

    def part(chunk, target):
        tile = min(512, width)
        for start in range(0, width, tile):
            cols = slice(start, start + tile)
            target[:, cols] = dot(d_mixed[chunk], w_head[cols, :], BY_LAST).astype(target.dtype)

    fold = Fold(ring, part, buffers, fold_sems)

    def finish(rows, value):
        d_inputs[rows, :] = value

    def store(i, which):
        these = pl.ds(pl.multiple_of(i * size, size), size)
        slot = lax.rem(i, 2)
        return pltpu.make_async_copy(
            stage.at[slot, which], grads_out.at[which, these], stage_sem.at[slot, which]
        )

    def filler(i):
        these = pl.ds(pl.multiple_of(i * size, size), size)
        slot = lax.rem(i, 2)
        pairs = ((rows_in, d_gate), (rows_in, d_up), (d_in, inner_in))
        for which, (left, right) in enumerate(pairs):

            @pl.when(i >= 2)
            def _():
                store(i - 2, which).wait()

            stage[slot, which] = dot(left[:, these], right[...], BY_FIRST)
            store(i, which).start()

    def push(step):
        there = ring.peer(step)
        return remote(
            summed.at[there],
            qkv_rows.at[ring.me],
            send.at[0, step],
            recv.at[0, step],
            {"seq": there},
        )

    local = pltpu.make_async_copy(summed.at[ring.me], qkv_rows.at[ring.me], keep.at[0])

    def far(step):
        return remote(
            third.at[step - 1],
            third_in.at[step - 1],
            side_send.at[2, step],
            side_recv.at[2, step],
            {"fsdp": ring.beside(f - step)},
        )

    for step in range(1, f):
        far(step).start()
    stored = Stored(ring, moe_part, stored_buffers, stored_sems)
    fold.produce(0)
    stored.begin()
    for load in loads:
        load.start()
    fold.step(0)
    stored.step(0)
    for load in loads:
        load.wait()
    filler(0)
    fold.run(finish, filler, stored.step)

    def settle(rows, value):
        result[rows, :] = (middle[rows, :] + value).astype(BF16)

    stored.close(settle)
    value = tokens[...].astype(F32)
    grad = d_inputs[...]
    inverse = lax.rsqrt(jnp.mean(value * value, -1, keepdims=True) + EPS)
    inner = jnp.mean(value * gain[...] * grad, -1, keepdims=True)
    gain_rows[...] = jnp.zeros_like(gain_rows)
    gain_rows[0:1, :] = jnp.sum(value * inverse * grad, 0, keepdims=True)
    gain_rows[1:2, :] = gain_two[...]

    def gains(step):
        there = ring.peer(step)
        cols = pl.ds(pl.multiple_of(there * slice_width, slice_width), slice_width)
        return remote(
            gain_rows.at[:, cols],
            gain_in.at[ring.me],
            send.at[1, step],
            recv.at[1, step],
            {"seq": there},
        )

    mine = pl.ds(pl.multiple_of(ring.me * slice_width, slice_width), slice_width)
    kept = pltpu.make_async_copy(gain_rows.at[:, mine], gain_in.at[ring.me], keep.at[1])
    for step in range(1, n):
        gains(step).start()
    kept.start()
    d_value = inverse * gain[...] * grad - value * (inverse * inverse * inverse) * inner
    d_inputs[...] = d_middle[...] + d_value
    for step in range(1, f):
        side(step).wait_recv()

    def add(block, carry):
        value = qkv_part[ring.mine, block].astype(F32)
        for step in range(1, f):
            value = value + beside_rows[step - 1, block].astype(F32)
        summed[block] = value.astype(BF16)
        return carry

    lax.fori_loop(0, n, add, 0)
    for step in range(1, n):
        push(step).start()
    local.start()
    for step in range(1, n):
        gains(step).wait()
    kept.wait()
    total = gain_head[...]
    for device in range(n):
        total = total + gain_in[device]
    gain_side[0] = total

    def sums(step):
        return remote(
            gain_side.at[0],
            gain_side.at[step],
            side_send.at[1, step],
            side_recv.at[1, step],
            {"fsdp": ring.beside(step)},
        )

    for step in range(1, f):
        sums(step).start()
    fold.close()
    for i in (chips - 2, chips - 1):
        for which in range(3):
            store(i, which).wait()
    for step in range(1, f):
        side(step).wait_send()
    for step in range(1, n):
        push(step).wait()
    local.wait()
    for step in range(1, f):
        sums(step).wait()
        total = total + gain_side[step]
    gains_out[...] = total
    for step in range(1, f):
        far(step).wait()


def last_stage(
    n, f, d_mixed, w_head, qkv_part, tokens, gain, d_middle, gain_two, gain_head,
    middle, third, moe_part, rows_in, d_in, d_gate, d_up, inner_in
):
    tok, width = tokens.shape
    rows, across = qkv_part.shape[2:]
    units = third.shape[2]
    kind = pltpu.SemaphoreType.DMA
    shape = jax.ShapeDtypeStruct
    return pl.pallas_call(
        partial(last_kernel, n, f),
        out_shape=[
            shape((tok, width), F32),
            shape((n, rows, across), BF16),
            shape((8, width // n), F32),
            shape(third.shape, BF16),
            shape((3, width, units), F32),
            shape((tok, width), BF16),
        ],
        in_specs=[VMEM] * 9 + [ANY] * 7,
        out_specs=[VMEM] * 3 + [ANY] * 2 + [VMEM],
        scratch_shapes=[
            pltpu.VMEM((max(f - 1, 1), n, rows, across), BF16),
            pltpu.VMEM((n, rows, across), BF16),
            pltpu.VMEM((8, width), F32),
            pltpu.VMEM((n, 8, width // n), F32),
            pltpu.VMEM((f, 8, width // n), F32),
            pltpu.VMEM((2, 3, 2 * width // n, units), F32),
            pltpu.VMEM(rows_in.shape, BF16),
            pltpu.VMEM(rows_in.shape, BF16),
            pltpu.VMEM((rows_in.shape[0], units), BF16),
            pltpu.VMEM((rows_in.shape[0], units), BF16),
            pltpu.VMEM((rows_in.shape[0], units), BF16),
        ]
        + Fold.buffers(n, tok, width)
        + Fold.semaphores(n)
        + Stored.buffers(n, tok, width)
        + Stored.semaphores(n)
        + [kind((3, f)), kind((3, f)), kind((2, n)), kind((2, n)), kind((2,)), kind((2, 3))]
        + [kind((5,))],
        compiler_params=pltpu.CompilerParams(
            collective_id=4, has_side_effects=True, vmem_limit_bytes=67_000_000
        ),
        name="last_stage",
    )(
        d_mixed, w_head, qkv_part, tokens, gain, d_middle, gain_two, gain_head,
        middle, third, moe_part, rows_in, d_in, d_gate, d_up, inner_in
    )


def angles_of(n, tok, head_size):
    half = head_size // 2
    freqs = 10000.0 ** (-jnp.arange(half, dtype=F32) / half)
    inside = jnp.arange(tok, dtype=jnp.int32)
    starts = jnp.arange(n, dtype=jnp.int32) * tok
    angles = jnp.concatenate([inside, starts]).astype(F32)[:, None] * freqs[None, :]
    both = jnp.stack([jnp.cos(angles), jnp.sin(angles)])
    both = jnp.concatenate([both, both], -1)
    return both[:, :tok], both[:, tok:, None, :]


def shift_fsdp(values, step, f):
    if step == 0:
        return values
    return lax.ppermute(values, "fsdp", [(i, (i + step) % f) for i in range(f)])


def shards(n, f, inputs, routes, w_qkv, w_out, w_router, norm_gains, w_gate, w_up, w_down, cotangent):
    tokens_low = inputs[0]
    upstream_low = cotangent[0]
    local_routes = routes[0].T
    me = lax.axis_index("seq")
    mine = lax.axis_index("fsdp")
    tok, width = tokens_low.shape
    length = tok * n
    head_size = width // HEADS
    across = 3 * head_size
    rows = w_qkv.shape[0]
    experts = n * w_gate.shape[0]
    capacity = min(tok, 5 * tok * TOPK // (4 * experts))
    factor = head_size ** (-0.5)

    by_head = w_qkv.reshape(rows, 3, HEADS, head_size).transpose(2, 0, 1, 3)
    by_head = by_head.reshape(HEADS, rows, across)
    small = jnp.concatenate([w_router, norm_gains], 1)
    small = jnp.pad(small, ((0, 0), (0, 128 - small.shape[1])))
    (
        hidden_one,
        mixed,
        w_head,
        router,
        gains,
        routes_all,
        gate_near,
        up_near,
        w_out_all,
    ) = first_gather(n, f, tokens_low, by_head, small, local_routes, w_out, w_gate[0], w_up[0])
    w_out_all = w_out_all.reshape(width, width)
    gates = [w_gate[0]] + [gate_near[j] for j in range(f - 1)]
    ups = [w_up[0]] + [up_near[j] for j in range(f - 1)]
    w_low, _ = lax.optimization_barrier((w_down[0], mixed))
    downs = [shift_fsdp(w_low, j, f) for j in range(f)]
    hidden_one = hidden_one.reshape(length, width)
    w_head = w_head.reshape(width, across)
    own = lax.dynamic_slice_in_dim(gains, me * head_size, head_size, 1)
    tables, starts = angles_of(n, tok, head_size)
    queries, keys, values, attended, exact, sums, squares, cosine, sine, upstream_all = attention(
        n, f, mixed, tables, starts, own, upstream_low, factor
    )

    (
        d_middle,
        middle,
        d_attn,
        d_attended,
        d_logits_all,
        gain_two,
        own_hidden,
        expert_rows,
        d_produced,
        inner,
        d_gate,
        d_up,
        moe_part,
    ) = core_stage(
        n,
        f,
        attended.reshape(n, tok, head_size),
        w_out_all,
        tokens_low,
        upstream_low,
        gains[3:4],
        router,
        local_routes,
        routes_all,
        upstream_all,
        gates + ups + downs,
    )
    flat = n * capacity
    units = w_gate.shape[2]
    expert_rows = expert_rows.reshape(flat, width)
    d_produced = d_produced.reshape(flat, width)
    inner, d_gate, d_up = (v.reshape(flat, f * units) for v in (inner, d_gate, d_up))
    pairs = ((expert_rows, d_gate), (expert_rows, d_up), (d_produced, inner))

    def others(which):
        left, right = pairs[which]
        return [
            dot(left, right[:, j * units : (j + 1) * units], BY_FIRST).astype(BF16)
            for j in range(1, f)
        ]

    first, second = others(0), others(1)
    d_attended, first, second = lax.optimization_barrier((d_attended, first, second))
    first = [shift_fsdp(v, f - 1 - j, f) for j, v in enumerate(first)]
    second = [shift_fsdp(v, f - 1 - j, f) for j, v in enumerate(second)]
    d_mixed, gain_head, d_attn_all, third, qkv_part = attention_back(
        n,
        f,
        queries,
        keys,
        values,
        d_attended.reshape(length, head_size),
        sums,
        exact,
        mixed,
        cosine,
        sine,
        own,
        squares,
        d_attn,
        d_produced,
        inner,
        hidden_one,
        rows,
        factor,
    )
    d_attn_all = d_attn_all.reshape(length, width)
    proj_part = dot(attended, d_attn_all, BY_FIRST)
    router_part = jnp.einsum(
        "ntc,nkt->ck", own_hidden, d_logits_all, preferred_element_type=F32
    )
    both = jnp.concatenate([proj_part, router_part], 1).reshape(f, rows, width + experts)
    d_mixed, both = lax.optimization_barrier((d_mixed, both))
    proj = lax.dynamic_index_in_dim(both, mine, 0, keepdims=False)
    for j in range(1, f):
        part = lax.dynamic_index_in_dim(both, (mine + j) % f, 0, keepdims=False)
        proj = proj + shift_fsdp(part.astype(BF16), j, f).astype(F32)
    grad_inputs, qkv_rows, gains_own, third, grads_own, result = last_stage(
        n,
        f,
        d_mixed.reshape(n, tok, across),
        w_head,
        qkv_part,
        tokens_low,
        gains[0:1],
        d_middle,
        gain_two,
        gain_head,
        middle,
        third,
        moe_part,
        expert_rows,
        d_produced,
        d_gate,
        d_up,
        inner,
    )
    grads = []
    for which, arrived in enumerate((first, second, [third[j] for j in range(f - 1)])):
        total = grads_own[which]
        for part in arrived:
            total = total + part.astype(F32)
        grads.append(total[None])
    grad_qkv = (
        qkv_rows.reshape(HEADS, rows, 3, head_size)
        .transpose(1, 2, 0, 3)
        .reshape(rows, 3 * width)
        .astype(F32)
    )
    gains_out = jnp.stack([gains_own[0], gains_own[2], gains_own[3], gains_own[1]], 1)
    grad_gains = lax.dynamic_slice_in_dim(gains_out, mine * rows, rows, 0)
    return (
        result[None],
        grad_inputs[None],
        grad_qkv,
        proj[:, :width],
        proj[:, width:],
        grad_gains,
        *grads,
    )


def solution(mesh):
    tokens = P("fsdp", "seq", None)
    split = P(("seq", "fsdp"), None)
    expert = P("seq", None, "fsdp")
    return jax.shard_map(
        partial(shards, mesh.shape["seq"], mesh.shape["fsdp"]),
        mesh=mesh,
        in_specs=(tokens, tokens, split, split, split, split, expert, expert, expert, tokens),
        out_specs=(tokens, tokens, split, split, split, split, expert, expert, expert),
        check_vma=False,
    )
```

time: 706 us -> 638 us (0.904)
  matrix products: 148 us -> 16.9 us
  Pallas kernels: 455 us -> 569 us
  other arithmetic: 41.5 us -> 16.9 us
  between operations: 15.5 us -> 1.16 us
  local copies, waits for them, and re-layouts: 30.8 us -> 23.4 us
    dot_general x22 -> x3, matrix products: 134 us -> 16.5 us  [dot(): return lax.dot_general(a, b, dims, preferred_element_type=F32)]
    pallas_call x1, Pallas kernels: 76.2 us -> 147 us  [first_gather(): pl.pallas_call(partial(first_kernel, n, f), out_shape=[shape((n, tok, wid...]
    pallas_call x1, Pallas kernels: 93.4 us -> 160 us  [last_stage(): pl.pallas_call(partial(last_kernel, n, f), out_shape=[shape((tok, width),...]
    pallas_call x7 -> x3, Pallas kernels: 285 us -> 262 us  [the longest x1 138 us: core_stage(): pl.pallas_call(partial(core_kernel, n, f), out_shape=[shape((tok, width),...]
    convert_element_type x9 -> x1, other arithmetic: 18.5 us -> 0.01 us  [angles_of(): jnp.concatenate([inside, starts]).astype(F32)[:, None] * freqs[None, :]]
    dot_general x2 -> x0, matrix products: 12.6 us -> none  [the longest x1 7.51 us: shards(): lax.dot_general(pick_low, upstream_all, take, preferred_element_type=F32)]
    reduce_sum x6 -> x0, other arithmetic: 9.68 us -> none  [the longest x1 5.41 us: shards(): jnp.mean(tokens_all32 * tokens_all32, -1, keepdims=True) + EPS]
    broadcast_in_dim x0 -> x1, other arithmetic: none -> 9.63 us  [shards(): grads.append(total[None])]
  transfers between devices with their start and end apart: 8 -> 4, of which waited for: 0 -> 0; matrix products, arithmetic and copies ran while one was open for 23% -> 2% of each run, Pallas kernels for 54% -> 35%
where the time goes in v2:
time: 638 us; the launch traced here: 632 us
  Pallas kernels  569 us (89%)
  local copies, waits for them, and re-layouts  23.4 us (4%)
  other arithmetic  16.9 us (3%)
  matrix products  16.9 us (3%)
    pallas_call x1, Pallas kernels, last_stage(): pl.pallas_call(partial(last_kernel, n, f), out_shape=[shape((tok, width),...  160 us
    pallas_call x1, Pallas kernels, first_gather(): pl.pallas_call(partial(first_kernel, n, f), out_shape=[shape((n, tok, wid...  147 us
    pallas_call x1, Pallas kernels, core_stage(): pl.pallas_call(partial(core_kernel, n, f), out_shape=[shape((tok, width),...  138 us
    pallas_call x1, Pallas kernels, attention_back(): pl.pallas_call(partial(attention_back_kernel, n, f, factor), out_shape=[s...  65.3 us
    pallas_call x1, Pallas kernels, attention(): pl.pallas_call(partial(attention_kernel, n, f, factor), out_shape=[shape(...  59 us
    dot_general x3, matrix products, dot(): return lax.dot_general(a, b, dims, preferred_element_type=F32)  16.5 us
    unnamed x55, local copies, waits for them, and re-layouts  14.6 us
  transfers between devices with their start and end apart: 4, of which 0 were waited for; matrix products, arithmetic and copies ran while one was open for 2% of the time, Pallas kernels for 35%

profile of v2, /device:TPU:0, one launch (start us, length us, event | category | flops | bytes accessed | tf_op | source)
XLA Modules:
  0.0 631.6 jit_solution(2218863941655423280)
XLA Ops:
  0.7 1.3 copy.49
  1.9 0.5 copy.54
  2.4 1.4 reshape.177.refs_1_
  3.9 0.1 copy.43
  4.0 0.6 pad.4.refs_2_
  4.6 147.5 %first_gather.1 = (bf16[16,128,2048]{2,1,0:T(8,128)(2,1)}, f32[2048,384]{1,0:T(8,128)}, bf16[16,2,64,384]{3,2,1,0:T(8,128)(2,1)}, bf16[16,2048]{1,0:T(8,128)(2,1...) custom-call(bf16[128,2048]{1,0:T(8,128)(2,1)} %bitcast.90, ...), custom_call_target="tpu_custom_call" | custom-call | tf_op jit(solution)/shard_map/first_gather/pallas_call | solution.py:762
  152.1 0.6 collective-permute-start
  152.8 0.3 multiply_cosine_fusion
  153.1 0.1 maximum_maximum_fusion
  153.2 0.7 constant_dynamic-slice_fusion.1.refs_3_.refs_9_
  153.9 0.1 maximum_maximum_fusion.1
  154.0 1.9 copy-done.1
  155.9 59.0 %attention.1 = (bf16[2048,128]{1,0:T(8,128)(2,1)S(1)}, bf16[2048,128]{1,0:T(8,128)(2,1)S(1)}, bf16[2048,128]{1,0:T(8,128)(2,1)S(1)}, bf16[2048,128]{1,0:T(8,128)...) custom-call(f32[2048,384]{1,0:T(8,128)S(1)} %copy-done.1, ...), custom_call_target="tpu_custom_call" | custom-call | flops 1073741824 | bytes 2097152 | tf_op jit(solution)/shard_map/attention/pallas_call | solution.py:959
  214.9 0.8 copy-done
  215.7 1.0 copy-done.2
  216.7 1.0 copy-done.3
  217.6 1.0 copy-done.4
  218.6 0.8 copy-done.6
  219.4 0.8 copy-done.7
  220.2 0.8 copy-done.8
  221.0 0.6 copy-done.9
  221.6 0.6 copy-done.10
  222.2 1.5 fusion.5
  223.7 0.0 collective-permute-done.refs_14_
  223.7 137.5 %core_stage.1 = (f32[128,2048]{1,0:T(8,128)}, f32[128,2048]{1,0:T(8,128)}, bf16[128,2048]{1,0:T(8,128)(2,1)}, bf16[16,128,128]{2,1,0:T(8,128)(2,1)}, bf16[16,16,...) custom-call(bf16[16,128,128]{2,1,0:T(8,128)(2,1)} %bitcast.70, ...), custom_call_target="tpu_custom_call" | custom-call | tf_op jit(solution)/shard_map/core_stage/pallas_call | solution.py:1628
  361.3 7.3 %convolution_convert_fusion = bf16[2048,512]{1,0:T(8,128)(2,1)} fusion(bf16[1280,2048]{1,0:T(8,128)(2,1)} %bitcast.87, bf16[1280,1024]{1,0:T(8,128)(2,1)} %bitcast.99), kind=kOutput, calls=%fused_computation.5 | convolution fusion | flops 2685403136 | bytes 8650752 | tf_op jit(solution)/shard_map/dot_general | solution.py:27
  368.6 4.4 convolution_convert_fusion.1
  372.9 65.3 %attention_back.1 = (bf16[2048,384]{1,0:T(8,128)(2,1)}, f32[8,128]{1,0:T(8,128)}, bf16[16,128,2048]{2,1,0:T(8,128)(2,1)}, bf16[1,2048,512]{2,1,0:T(8,128)(2,1)}, bf16[2,16,64,384]{3,2,1,0:T(8,128)(2,1)}) custom-call(bf16[2048,128]{1,0:T(8,128)(2,1)} %copy-done.6, bf16[2048,128]{1,0:T(8,128)(2,1)} %copy-done.7, bf16[2048,128]{1,0:T(8,128)(2,1)} %copy-done.8, ...), custom_call_target="tpu_custom_call" | custom-call | tf_op jit(solution)/shard_map/attention_back/pallas_call | solution.py:1143
  438.3 4.9 fusion.6
  443.2 0.3 convolution_bitcast_fusion
  443.6 0.1 pad_maximum_fusion
  443.7 1.6 collective-permute-start.2
  445.2 0.5 collective-permute-start.3
  445.8 0.7 fusion.4
  446.5 1.5 collective-permute-start.1
  448.0 159.7 %last_stage.1 = (f32[128,2048]{1,0:T(8,128)}, bf16[16,64,384]{2,1,0:T(8,128)(2,1)}, f32[8,128]{1,0:T(8,128)}, bf16[1,2048,512]{2,1,0:T(8,128)(2,1)}, f32[3,2048,512]{2,1,0:T(8,128)}, /*index=5*/bf16[128,2048]{1,0:T(8,128)(2,1)}) custom-call(bf16[16,128,384]{2,1,0:T(8,128)(2,1)} %bitcast.106, bf16[2048,384]{1,0:T(8,128)(2,1)} %bitcast.105, ...), custom_call_target="tpu_custom_call" | custom-call | tf_op jit(solution)/shard_map/last_stage/pallas_call | solution.py:1888
  607.8 5.6 convert_add_fusion
  613.4 0.8 reshape.192
  614.2 0.9 copy.45
  615.1 1.6 copy.53
  616.8 0.7 constant_dynamic-slice_fusion
  617.4 0.0 collective-permute-done.1
  617.4 1.0 bitcast_add_fusion.2
  618.4 0.8 slice.63
  619.3 0.7 copy.46
  620.0 9.6 %fusion = (f32[1,2048,512]{2,1,0:T(8,128)}, f32[1,2048,512]{2,1,0:T(8,128)}) fusion(bf16[2048,512]{1,0:T(8,128)(2,1)} %collective-permute-done.3, f32[3,2048,512]{2,1,0:T(8,128)} %get-tuple-element.103, bf16[2048,512]{1,0:T(8,128)(2,1)} %collective-permute-done.2), kind=kLoop, calls=%fused_computation.1 | loop fusion | flops 4194304 | bytes 20971520 | tf_op jit(solution)/shard_map/broadcast_in_dim | solution.py:2092
  629.6 0.8 copy.57
  630.4 1.0 copy.58
  (51 shorter events, 0.1 us)
Async XLA Ops:
  0.6 3.2 copy-start.22
  0.7 3.2 copy-start.24
  4.6 147.5 %copy-start.16 = (bf16[1,2048,512]{2,1,0:T(8,128)(2,1)S(1)}, bf16[1,2048,512]{2,1,0:T(8,128)(2,1)}, u32[]{:S(2)}) copy-start(bf16[1,2048,512]{2,1,0:T(8,128)(2,1)} %param.18) | copy-start | bytes 6291460
  4.6 149.4 %copy-start.5 = (bf16[1,128,2048]{2,1,0:T(8,128)(2,1)S(1)}, bf16[1,128,2048]{2,1,0:T(8,128)(2,1)}, u32[]{:S(2)}) copy-start(bf16[1,128,2048]{2,1,0:T(8,128)(2,1)} %param.19) | copy-start | bytes 1572868
  152.1 71.6 %collective-permute-start = (bf16[2048,512]{1,0:T(8,128)(2,1)S(1)}, bf16[2048,512]{1,0:T(8,128)(2,1)}, u32[]{:S(2)}, u32[]{:S(2)}) collective-permute-start(bf16[2048,512]{1,0:T(8,128)(2,1)S(1)} %bitcast.102), channel_id=1, source_target_pairs={{0,1},{1,0},{2,3},{3,2},{4,5},{5,4},{6,7},{7,6},{8,9},{9,8},{10,11... | collective-permute-start | bytes 6291464 | tf_op jit(solution)/shard_map/ppermute | solution.py:1943
  153.9 60.9 %copy-start.11 = (f32[8,128]{1,0:T(8,128)}, f32[8,128]{1,0:T(8,128)S(1)}, u32[]{:S(2)}) copy-start(f32[8,128]{1,0:T(8,128)S(1)} %constant_dynamic-slice_fusion.1.refs_3_.refs_9_) | copy-start | bytes 12292
  154.0 1.9 copy-start.1
  214.9 0.8 copy-start
  215.7 1.0 copy-start.2
  216.7 1.0 copy-start.3
  217.6 1.0 copy-start.4
  218.6 0.8 copy-start.6
  219.4 0.8 copy-start.7
  220.2 0.8 copy-start.8
  221.0 0.6 copy-start.9
  221.6 0.6 copy-start.10
  361.3 7.3 %copy-start.12 = (bf16[16,80,2048]{2,1,0:T(8,128)(2,1)S(1)}, bf16[16,80,2048]{2,1,0:T(8,128)(2,1)}, u32[]{:S(2)}) copy-start(bf16[16,80,2048]{2,1,0:T(8,128)(2,1)} %get-tuple-element.72) | copy-start | bytes 15728644
  361.3 7.3 %copy-start.15 = (bf16[16,80,1024]{2,1,0:T(8,128)(2,1)S(1)}, bf16[16,80,1024]{2,1,0:T(8,128)(2,1)}, u32[]{:S(2)}) copy-start(bf16[16,80,1024]{2,1,0:T(8,128)(2,1)} %get-tuple-element.73) | copy-start | bytes 7864324
  438.3 4.9 copy-start.19
  438.3 4.9 copy-start.21
  443.7 2.1 copy-start.13
  443.7 176.3 %collective-permute-start.2 = (bf16[2048,512]{1,0:T(8,128)(2,1)}, bf16[2048,512]{1,0:T(8,128)(2,1)}, u32[]{:S(2)}, u32[]{:S(2)}) collective-permute-start(bf16[2048,512]{1,0:T(8,128)(2,1)} %convolution_convert_fusion.1), channel_id=1, source_target_pairs={{0,1},{1,0},{2,3},{3,2},{4,5},{5,4},{6,7},{7,6},{8,9},{9,8},{10,11... | collective-permute-start | bytes 6291464 | tf_op jit(solution)/shard_map/ppermute | solution.py:1943
  445.2 174.7 %collective-permute-start.3 = (bf16[2048,512]{1,0:T(8,128)(2,1)}, bf16[2048,512]{1,0:T(8,128)(2,1)}, u32[]{:S(2)}, u32[]{:S(2)}) collective-permute-start(bf16[2048,512]{1,0:T(8,128)(2,1)} %convolution_convert_fusion), channel_id=1, source_target_pairs={{0,1},{1,0},{2,3},{3,2},{4,5},{5,4},{6,7},{7,6},{8,9},{9,8},{10,11... | collective-permute-start | bytes 6291464 | tf_op jit(solution)/shard_map/ppermute | solution.py:1943
  446.5 170.9 %collective-permute-start.1 = (bf16[64,2064]{1,0:T(8,128)(2,1)}, bf16[64,2064]{1,0:T(8,128)(2,1)}, u32[]{:S(2)}, u32[]{:S(2)}) collective-permute-start(bf16[64,2064]{1,0:T(8,128)(2,1)} %fusion.4), channel_id=1, source_target_pairs={{0,1},{1,0},{2,3},{3,2},{4,5},{5,4},{6,7},{7,6},{8,9},{9,8},{10,11... | collective-permute-start | bytes 792584 | tf_op jit(solution)/shard_map/ppermute | solution.py:1943
  607.7 5.6 copy-start.23
  607.8 5.6 copy-start.18
  614.2 3.2 copy-start.14
  619.9 9.6 %copy-start.20 = (bf16[128,2048]{1,0:T(8,128)(2,1)S(1)}, bf16[128,2048]{1,0:T(8,128)(2,1)}, u32[]{:S(2)}) copy-start(bf16[128,2048]{1,0:T(8,128)(2,1)} %get-tuple-element.98) | copy-start | bytes 1572868
  619.9 10.4 %copy-start.17 = (f32[128,2048]{1,0:T(8,128)S(1)}, f32[128,2048]{1,0:T(8,128)}, u32[]{:S(2)}) copy-start(f32[128,2048]{1,0:T(8,128)} %get-tuple-element.99) | copy-start | bytes 3145732

commit v3 on v2

--- a/solution.py
+++ b/solution.py
@@ -16,6 +16,7 @@
 BF16 = jnp.bfloat16
 MESH = pl.DeviceIdType.MESH
 PIECES = 2
+EARLY = 3
 ANY = pl.BlockSpec(memory_space=pl.ANY)
 VMEM = pl.BlockSpec(memory_space=pltpu.VMEM)
 MATMUL = (((1,), (0,)), ((), ()))
@@ -601,18 +602,23 @@
 
 
 def first_kernel(n, f, *refs):
-    own, by_head, small, routes, w_out, w_gate, w_up = refs[:7]
+    own, w_qkv, small, routes, w_out, w_gate, w_up = refs[:7]
     hidden_all, mixed, w_head, router, gains, routes_all, gate_near, up_near, out_all = refs[7:16]
-    near, small_all, out_rows = refs[16:19]
-    sems, out_sems = refs[19:24], refs[24:29]
-    send, recv, beside_send, beside_recv, keep = refs[29:34]
-    wide_send, wide_recv, row_send, row_recv, out_sem = refs[34:]
+    near, small_all, out_rows, by_head = refs[16:20]
+    sems, out_sems = refs[20:25], refs[25:30]
+    send, recv, beside_send, beside_recv, keep = refs[30:35]
+    wide_send, wide_recv, row_send, row_recv, out_sem = refs[35:]
     ring = Ring(n, f)
     experts = router.shape[0]
     tok, width = own.shape
     rows = small.shape[0]
     hops = ring.chips - 1
     piece = width // ring.chips
+    head = width // n
+    for h in range(n):
+        for k in range(3):
+            start = k * width + h * head
+            by_head[h, :, k * head : (k + 1) * head] = w_qkv[:, start : start + head]
     greet(ring, True, True)
     gather = Gather(ring, own, near, sems)
     gather_out = Gather(ring, out_rows, out_all, out_sems)
@@ -650,7 +656,8 @@
             {"fsdp": ring.beside(over)},
         )
 
-    def wide(kind, part, over):
+    def wide(part, over):
+        kind, part = divmod(part, ring.chips)
         these = pl.ds(part * piece, piece)
         return remote(
             [w_gate, w_up][kind].at[these],
@@ -659,6 +666,8 @@
             wide_recv.at[kind, part, over],
             {"fsdp": ring.beside(over)},
         )
+
+    half_parts = ring.chips + ring.chips // 2
 
     gather.begin()
     for over in range(1, f):
@@ -677,25 +686,31 @@
     for over in range(1, f):
         aside(1, 0, over, True).start()
         aside(0, 0, over, True).start()
-        for kind in (0, 1):
-            wide(kind, 0, over).start()
-    copies[3].wait()
-    for over in range(1, f):
-        row(over).wait_recv()
-    gather_out.begin()
-    each = -(-(n - 1) // (hops - 1))
+        wide(0, over).start()
+    each = -(-(n - 1) // 3)
+    parts = 1
+
+    def widen(parts):
+        if parts < half_parts:
+            for over in range(1, f):
+                wide(parts, over).start()
+        return parts + 1
+
     for i in range(hops):
         gather.pass_on(i)
-        gather_out.pass_on(i)
-        if i:
-            for step in range((i - 1) * each + 1, min(i * each, n - 1) + 1):
+        if 2 <= i < 5:
+            for step in range((i - 2) * each + 1, min((i - 1) * each, n - 1) + 1):
                 for kind in (1, 0):
                     push(kind, step).wait_recv()
                     for over in range(1, f):
                         aside(kind, step, over, False).start()
-        for over in range(1, f):
-            for kind in (0, 1):
-                wide(kind, i + 1, over).start()
+        else:
+            parts = widen(parts)
+        if i == hops - 2:
+            copies[3].wait()
+            for over in range(1, f):
+                row(over).wait_recv()
+            gather_out.begin()
     gather.finish()
     for copy in copies[:3]:
         copy.wait()
@@ -743,20 +758,28 @@
         mixed[here, :] = total
         return carry
 
-    lax.fori_loop(0, n, project, 0)
+    done = 0
+    for i in range(hops):
+        parts = widen(parts)
+        upto = min(n, -(-n * (i + 1) // hops))
+        lax.fori_loop(done, upto, project, 0)
+        done = upto
+        gather_out.pass_on(i)
+    while parts < half_parts:
+        parts = widen(parts)
     for c in range(n):
         out(c).wait()
     gather_out.finish()
     for over in range(1, f):
         row(over).wait_send()
-        for kind in (0, 1):
-            for part in range(ring.chips):
-                wide(kind, part, over).wait()
-
-
-def first_gather(n, f, own, by_head, small, routes, w_out, w_gate, w_up):
+        for part in range(half_parts):
+            wide(part, over).wait()
+
+
+def first_gather(n, f, own, w_qkv, small, routes, w_out, w_gate, w_up):
     tok, width = own.shape
-    experts = by_head.shape[0]
+    experts = n
+    by_head = jax.ShapeDtypeStruct((n, w_qkv.shape[0], 3 * width // n), BF16)
     kind = pltpu.SemaphoreType.DMA
     shape = jax.ShapeDtypeStruct
     return pl.pallas_call(
@@ -768,8 +791,8 @@
             shape((experts, width), BF16),
             shape((8, width), F32),
             shape((n,) + routes.shape, jnp.int32),
-            shape((max(f - 1, 1),) + w_up.shape, BF16),
-            shape((max(f - 1, 1),) + w_up.shape, BF16),
+            shape((max(f - 1, 1),) + w_gate.shape, BF16),
+            shape((max(f - 1, 1), w_up.shape[0] // 2, w_up.shape[1]), BF16),
             shape((n, f * w_out.shape[0], w_out.shape[1]), BF16),
         ],
         in_specs=[VMEM] * 5 + [ANY] * 2,
@@ -778,16 +801,17 @@
             pltpu.VMEM((n, tok, width), BF16),
             pltpu.VMEM((n, f) + small.shape, BF16),
             pltpu.VMEM((f * w_out.shape[0], w_out.shape[1]), BF16),
+            pltpu.VMEM(by_head.shape, BF16),
         ]
         + Gather.semaphores(n)
         + Gather.semaphores(n)
         + [kind((3, n)), kind((3, n)), kind((2, n, f)), kind((2, n, f)), kind((4,))]
         + [kind((2, n // 2, f)), kind((2, n // 2, f)), kind((f,)), kind((f,)), kind((n,))],
         compiler_params=pltpu.CompilerParams(
-            collective_id=0, has_side_effects=True, vmem_limit_bytes=56 << 20
+            collective_id=0, has_side_effects=True, vmem_limit_bytes=67_000_000
         ),
         name="first_gather",
-    )(own, by_head, small, routes, w_out, w_gate, w_up)
+    )(own, w_qkv, small, routes, w_out, w_gate, w_up)
 
 
 def blocks_of(length):
@@ -818,6 +842,18 @@
     return pltpu.roll(value, half, 1) * sign
 
 
+def set_angles(n, tables, starts, cosine, sine):
+    tok = tables.shape[1]
+
+    def angles(c, carry):
+        here = pl.ds(pl.multiple_of(c * tok, tok), tok)
+        cosine[here, :] = starts[0, c] * tables[0] - starts[1, c] * tables[1]
+        sine[here, :] = starts[1, c] * tables[0] + starts[0, c] * tables[1]
+        return carry
+
+    lax.fori_loop(0, n, angles, 0)
+
+
 class Spread:
     def __init__(self, ring, block, out, sems):
         self.ring, self.block, self.out = ring, block, out
@@ -860,17 +896,38 @@
 def attention_kernel(n, f, factor, *refs):
     mixed, tables, starts, gains, upstream = refs[:5]
     q_ref, k_ref, v_ref, out_ref, exact_ref, sums_ref, squares = refs[5:12]
-    cosine, sine, upstream_all = refs[12:15]
-    partial_sums, arrived = refs[15:17]
-    sems, walk_sems = refs[17:20], refs[20:]
+    upstream_all, by_token = refs[12:14]
+    partial_sums, arrived, cosine, sine = refs[14:18]
+    sems, walk_sems = refs[18:21], refs[21:26]
+    deal_send, deal_recv, deal_keep = refs[26:]
     ring = Ring(n, f)
     length, head = q_ref.shape
     width = head * n
     block, count = blocks_of(length)
     greet(ring, True, False)
     walk = Gather(ring, upstream, upstream_all, walk_sems)
-    walk.begin()
     last = walk.last
+    mine = pl.ds(pl.multiple_of(ring.me * head, head), head)
+
+    def deal(there):
+        these = pl.ds(pl.multiple_of(there * tok, tok), tok)
+        return remote(
+            out_ref.at[these],
+            by_token.at[:, mine],
+            deal_send.at[there],
+            deal_recv.at[ring.me],
+            {"seq": there},
+        )
+
+    def dealt(origin):
+        return remote(
+            out_ref.at[pl.ds(0, tok)],
+            by_token.at[:, pl.ds(pl.multiple_of(origin * head, head), head)],
+            deal_send.at[origin],
+            deal_recv.at[origin],
+            {"seq": origin},
+        )
+
     tok = tables.shape[1]
 
     def measure(b, carry):
@@ -884,14 +941,9 @@
     lax.fori_loop(0, count, measure, 0)
     spread = Spread(ring, partial_sums, arrived, sems)
     spread.begin()
-
-    def angles(c, carry):
-        here = pl.ds(pl.multiple_of(c * tok, tok), tok)
-        cosine[here, :] = starts[0, c] * tables[0] - starts[1, c] * tables[1]
-        sine[here, :] = starts[1, c] * tables[0] + starts[0, c] * tables[1]
-        return carry
-
-    lax.fori_loop(0, n, angles, 0)
+    walk.begin()
+
+    set_angles(n, tables, starts, cosine, sine)
     spread.finish()
     squares[...] = spread.total()
     walk.pass_on(0)
@@ -901,7 +953,7 @@
         for kind, target in ((0, q_ref), (1, k_ref)):
             inverse = lax.rsqrt(to_column(squares[...], kind * count + b, head) / width + EPS)
             raw = mixed[here, kind * head : (kind + 1) * head]
-            normed = raw * inverse * gains[kind + 1 : kind + 2, :]
+            normed = raw * inverse * gains[kind + 1 : kind + 2, mine]
             turned = half_turn(normed, -1.0)
             target[here, :] = (normed * cosine[here, :] + turned * sine[here, :]).astype(BF16)
         return carry
@@ -940,6 +992,13 @@
         column = jnp.broadcast_to(top + jnp.log(total), (block, 128))
         sums_ref[:, here] = jnp.transpose(column)[0:8, :]
 
+        for r in range(block // tok):
+            there = i * (block // tok) + r
+
+            @pl.when(there != ring.me)
+            def _():
+                deal(there).start()
+
         @pl.when((i > 0) & (i < last))
         def _():
             walk.pass_on(i)
@@ -947,9 +1006,16 @@
         return carry
 
     lax.fori_loop(0, count, outer, 0)
+    these = pl.ds(pl.multiple_of(ring.me * tok, tok), tok)
+    local = pltpu.make_async_copy(out_ref.at[these], by_token.at[:, mine], deal_keep.at[0])
+    local.start()
     for i in range(count, last):
         walk.pass_on(i)
     walk.finish()
+    for step in range(1, n):
+        deal(ring.peer(step)).wait_send()
+        dealt(ring.peer(step)).wait_recv()
+    local.wait()
 
 
 def attention(n, f, mixed, tables, starts, gains, upstream, factor):
@@ -966,20 +1032,23 @@
             shape((length, head), F32),
             shape((8, length), F32),
             shape((2 * count, block), F32),
-            shape((length, head), F32),
-            shape((length, head), F32),
             shape((n,) + upstream.shape, BF16),
+            shape((length // n, head * n), BF16),
         ],
         in_specs=[VMEM] * 5,
-        out_specs=[VMEM] * 9 + [ANY],
+        out_specs=[VMEM] * 7 + [ANY, VMEM],
         scratch_shapes=[
             pltpu.VMEM((2 * count, block), F32),
             pltpu.VMEM((n, 2 * count, block), F32),
+            pltpu.VMEM((length, head), F32),
+            pltpu.VMEM((length, head), F32),
         ]
         + Spread.semaphores(n)
-        + Gather.semaphores(n),
+        + Gather.semaphores(n)
+        + [pltpu.SemaphoreType.DMA((n,)), pltpu.SemaphoreType.DMA((n,))]
+        + [pltpu.SemaphoreType.DMA((1,))],
         compiler_params=pltpu.CompilerParams(
-            collective_id=5, has_side_effects=True, vmem_limit_bytes=40 << 20
+            collective_id=5, has_side_effects=True, vmem_limit_bytes=67_000_000
         ),
         cost_estimate=pl.CostEstimate(
             flops=2 * length * length * head,
@@ -991,28 +1060,83 @@
 
 
 def attention_back_kernel(n, f, factor, *refs):
-    q_ref, k_ref, v_ref, d_ref, sums_ref, exact, mixed, cosine, sine, gains, squares = refs[:11]
-    d_attn = refs[11]
-    far = refs[12:15]
-    d_mixed, gain_head, d_attn_all, third, qkv_part = refs[15:20]
-    dq_ref, dk_ref, dv_ref, delta, partial_sums, arrived = refs[20:26]
-    near = refs[26:29]
-    d_in, inner_in, hidden = near
-    walk_sems, spread_sems, load_sem = refs[29:34], refs[34:37], refs[37]
+    q_ref, k_ref, v_ref, by_token, sums_ref, exact, mixed, tables, starts, gains, squares = refs[:11]
+    d_attn, attended, own_hidden, d_logits = refs[11:15]
+    far = refs[15:19]
+    d_mixed, gain_head, qkv_part, proj, router, first_in, second_in = refs[19:26]
+    dq_ref, dk_ref, dv_ref, delta, partial_sums, arrived, d_attn_all, first, d_ref = refs[26:35]
+    cosine, sine = refs[35:37]
+    near = refs[37:41]
+    rows_in, d_gate, d_up, hidden = near
+    walk_sems, spread_sems = refs[41:46], refs[46:49]
+    load_sem, first_send, first_recv, deal_send, deal_recv, deal_keep = refs[49:]
     ring = Ring(n, f)
     length, head = q_ref.shape
     width = head * n
+    units = first_in.shape[2]
     block, count = blocks_of(length)
-    greet(ring, True, False)
-    walk = Gather(ring, d_attn, d_attn_all, walk_sems)
-    walk.begin()
-    last = walk.last
     loads = [
-        pltpu.make_async_copy(source, target, load_sem.at[k])
+        pltpu.make_async_copy(
+            source.at[:, units:] if k in (1, 2) else source, target, load_sem.at[k]
+        )
         for k, (source, target) in enumerate(zip(far, near))
     ]
     for load in loads:
         load.start()
+    greet(ring, True, True)
+    tok = d_attn.shape[0]
+    here_rows = pl.ds(pl.multiple_of(ring.me * tok, tok), tok)
+    mine = pl.ds(pl.multiple_of(ring.me * head, head), head)
+
+    def deal(step):
+        there = ring.peer(step)
+        return remote(
+            by_token.at[:, pl.ds(pl.multiple_of(there * head, head), head)],
+            d_ref.at[here_rows],
+            deal_send.at[step],
+            deal_recv.at[step],
+            {"seq": there},
+        )
+
+    local = pltpu.make_async_copy(
+        by_token.at[:, pl.ds(pl.multiple_of(ring.me * head, head), head)],
+        d_ref.at[here_rows],
+        deal_keep.at[0],
+    )
+    for step in range(1, n):
+        deal(step).start()
+    local.start()
+    walk = Gather(ring, d_attn, d_attn_all, walk_sems)
+    walk.begin()
+    last = walk.last
+    tiles = ring.chips
+    size = width // tiles
+
+    def send_first(tile, j):
+        kind, at = divmod(tile, tiles)
+        these = pl.ds(at * size, size)
+        return remote(
+            first.at[tile, j],
+            [first_in, second_in][kind].at[j, these],
+            first_send.at[tile, j],
+            first_recv.at[tile, j],
+            {"fsdp": ring.beside(f - 1 - j)},
+        )
+
+    set_angles(n, tables, starts, cosine, sine)
+    for load in loads[:3]:
+        load.wait()
+    for tile in range(tiles + EARLY):
+        kind, at = divmod(tile, tiles)
+        for j in range(f - 1):
+            part = slice(j * units, (j + 1) * units)
+            right = [d_gate, d_up][kind]
+            value = dot(rows_in[:, at * size : (at + 1) * size], right[:, part], BY_FIRST)
+            first[tile, j] = value.astype(BF16)
+            send_first(tile, j).start()
+    for step in range(1, n):
+        deal(step).wait()
+    local.wait()
     dq_ref[...] = jnp.zeros_like(dq_ref)
 
     def measure(b, carry):
@@ -1068,7 +1192,7 @@
             source[here, :] = grad
             raw = mixed[here, kind * head : (kind + 1) * head]
             partial_sums[pl.ds(kind * count + b, 1), :] = across_lanes(
-                raw * gains[kind + 1 : kind + 2, :] * grad
+                raw * gains[kind + 1 : kind + 2, mine] * grad
             )
         return carry
 
@@ -1076,21 +1200,7 @@
     spread = Spread(ring, partial_sums, arrived, spread_sems)
     spread.begin()
     walk.pass_on(count - 1)
-    units = third.shape[2]
-    for load in loads:
-        load.wait()
-
-    def products(tile, tiles):
-        size = d_in.shape[1] // tiles
-        these = pl.ds(pl.multiple_of(tile * size, size), size)
-        for j in range(1, f):
-            part = slice(j * units, (j + 1) * units)
-            third[j - 1, these, :] = dot(d_in[:, these], inner_in[:, part], BY_FIRST).astype(BF16)
-
-    def some(tile, carry):
-        products(tile, 8)
-        return carry
-
+    loads[3].wait()
     spread.finish()
     total = spread.total()
     gain_head[...] = jnp.zeros_like(gain_head)
@@ -1103,7 +1213,7 @@
             inner = to_column(total, index, head) / width
             raw = mixed[here, kind * head : (kind + 1) * head]
             grad = source[here, :]
-            value = inverse * gains[kind + 1 : kind + 2, :] * grad
+            value = inverse * gains[kind + 1 : kind + 2, mine] * grad
             value = value - raw * (inverse * inverse * inverse) * inner
             d_mixed[here, kind * head : (kind + 1) * head] = value.astype(BF16)
             gain_head[kind + 2 : kind + 3, :] += jnp.sum(raw * inverse * grad, 0, keepdims=True)
@@ -1125,63 +1235,106 @@
     lax.fori_loop(0, chunks, weigh, 0)
     for i in range(count + 1, last):
         walk.pass_on(i)
-        if i == count + 1:
-            lax.fori_loop(0, 8, some, 0)
+    router[...] = jnp.zeros_like(router)
+
+    def route(c, carry):
+        router[...] += dot(d_logits[c], own_hidden[c], MATMUL)
+        return carry
+
+    lax.fori_loop(0, n, route, 0)
     walk.finish()
+    group = block // tok
+    tile = min(512, width)
+
+    def project(c, carry):
+        left = attended[pl.ds(pl.multiple_of(c * block, block), block), :]
+        for start in range(0, width, tile):
+            cols = slice(start, start + tile)
+            right = d_attn_all[pl.ds(c * group, group), :, cols].reshape(block, tile)
+            value = dot(left, right, BY_FIRST)
+
+            @pl.when(c == 0)
+            def _():
+                proj[:, cols] = value
+
+            @pl.when(c > 0)
+            def _():
+                proj[:, cols] = proj[:, cols] + value
+
+        return carry
+
+    lax.fori_loop(0, count, project, 0)
+    for at in range(tiles + EARLY):
+        for j in range(f - 1):
+            send_first(at, j).wait()
 
 
 def attention_back(
-    n, f, queries, keys, values, d_out, sums, exact, mixed, cosine, sine, gains, squares,
-    d_attn, d_in, inner_in, hidden, rows, factor
+    n, f, queries, keys, values, by_token, sums, exact, mixed, tables, starts, gains, squares,
+    d_attn, attended, own_hidden, d_logits, rows_in, d_gate, d_up, hidden, rows, factor
 ):
     length, head = queries.shape
     tok, width = d_attn.shape
     block, count = blocks_of(length)
+    experts = d_logits.shape[1]
     shape = jax.ShapeDtypeStruct
-    units = inner_in.shape[1] // f
+    kind = pltpu.SemaphoreType.DMA
+    flat, every = d_gate.shape
+    units = every // f
+    tiles = n // 2
     grad = shape((max(f - 1, 1), width, units), BF16)
     return pl.pallas_call(
         partial(attention_back_kernel, n, f, factor),
         out_shape=[
             shape((length, 3 * head), BF16),
             shape((8, head), F32),
-            shape((n, tok, width), BF16),
+            shape((f, n, rows, 3 * head), BF16),
+            shape((head, width), F32),
+            shape((experts, head), F32),
             grad,
-            shape((f, n, rows, 3 * head), BF16),
+            grad,
         ],
-        in_specs=[VMEM] * 12 + [ANY] * 3,
-        out_specs=[VMEM, VMEM, ANY] + [VMEM] * 2,
+        in_specs=[VMEM] * 15 + [ANY] * 4,
+        out_specs=[VMEM] * 5 + [ANY] * 2,
         scratch_shapes=[pltpu.VMEM((length, head), F32)] * 3
         + [
             pltpu.VMEM((8, length), F32),
             pltpu.VMEM((2 * count, block), F32),
             pltpu.VMEM((n, 2 * count, block), F32),
-            pltpu.VMEM(d_in.shape, BF16),
-            pltpu.VMEM(inner_in.shape, BF16),
+            pltpu.VMEM((n, tok, width), BF16),
+            pltpu.VMEM((tiles + EARLY, max(f - 1, 1), width // tiles, units), BF16),
+            pltpu.VMEM((length, head), BF16),
+            pltpu.VMEM((length, head), F32),
+            pltpu.VMEM((length, head), F32),
+            pltpu.VMEM(rows_in.shape, BF16),
+            pltpu.VMEM((flat, every - units), BF16),
+            pltpu.VMEM((flat, every - units), BF16),
             pltpu.VMEM(hidden.shape, BF16),
         ]
         + Gather.semaphores(n)
         + Spread.semaphores(n)
-        + [pltpu.SemaphoreType.DMA((3,))],
+        + [kind((4,))]
+        + [kind((tiles + EARLY, max(f - 1, 1))), kind((tiles + EARLY, max(f - 1, 1)))]
+        + [kind((n,)), kind((n,)), kind((1,))],
         compiler_params=pltpu.CompilerParams(
-            collective_id=6, has_side_effects=True, vmem_limit_bytes=64 << 20
+            collective_id=6, has_side_effects=True, vmem_limit_bytes=67_000_000
         ),
         name="attention_back",
     )(
-        queries, keys, values, d_out, sums, exact, mixed, cosine, sine, gains, squares,
-        d_attn, d_in, inner_in, hidden
+        queries, keys, values, by_token, sums, exact, mixed, tables, starts, gains, squares,
+        d_attn, attended, own_hidden, d_logits, rows_in, d_gate, d_up, hidden
     )
 
 
 def core_kernel(n, f, *refs):
-    attended, w_out, tokens, upstream, gain, router, routes, routes_all, upstream_all = refs[:9]
-    shards_in = refs[9 : 9 + 3 * f]
-    refs = refs[9 + 3 * f :]
-    d_middle, middle, d_attn, d_attended, d_logits_all, gain_two = refs[:6]
+    by_token, w_out, tokens, upstream, gain, router, routes, routes_all, upstream_all = refs[:9]
+    shards_in = refs[9 : 8 + 4 * f]
+    refs = refs[8 + 4 * f :]
+    d_middle, middle, d_attn, d_by_token, d_logits_all, gain_two = refs[:6]
     own_hidden, rows_out, d_out, inner_out, d_gate_out, d_up_out, moe_out = refs[6:13]
     refs = refs[13:]
-    w_near, w_gate, w_up, w_down, by_token, d_logits, arrived, outgoing, weights_in = refs[:9]
-    refs = refs[9:]
+    w_near, w_gate, w_up, w_down, d_logits, arrived, outgoing, weights_in = refs[:8]
+    refs = refs[8:]
     ring_in, mate_near, d_mate_in, coming, going, d_mate_out, own, lift = refs[:8]
     refs = refs[8:]
     rows_now, lifted, d_now, inner_now, d_gate_now, d_up_now, moe_now, d_weight, places = refs[:9]
@@ -1201,14 +1354,19 @@
     local_units = hidden_units // f
 
     loads = [pltpu.make_async_copy(w_out, w_near, keep.at[0])]
-    for kind, target in enumerate((w_gate, w_up, w_down)):
-        for j in range(f):
-            cols = slice(j * local_units, (j + 1) * local_units)
-            loads.append(
-                pltpu.make_async_copy(
-                    shards_in[kind * f + j], target.at[:, cols], load_sem.at[kind, j]
-                )
-            )
+    half_width = width // 2
+    sources = []
+    for j in range(f):
+        cols = slice(j * local_units, (j + 1) * local_units)
+        sources.append((w_gate.at[:, cols], 0, j))
+        sources.append((w_down.at[:, cols], 2, j))
+        if j:
+            sources.append((w_up.at[pl.ds(0, half_width), cols], 1, j))
+            sources.append((w_up.at[pl.ds(half_width, half_width), cols], 3, j))
+        else:
+            sources.append((w_up.at[:, cols], 1, j))
+    for source, (target, kind, j) in zip(shards_in, sources):
+        loads.append(pltpu.make_async_copy(source, target, load_sem.at[kind, j]))
     for load in loads:
         load.start()
 
@@ -1229,21 +1387,7 @@
     lift_copy(0, 1).start()
     greet(ring, True, False)
 
-    def deal(step):
-        cols = pl.ds(pl.multiple_of(ring.me * head, head), head)
-        there = ring.peer(step)
-        return remote(
-            attended.at[there],
-            by_token.at[:, cols],
-            send.at[0, step],
-            recv.at[0, step],
-            {"seq": there},
-        )
-
-    for step in range(1, n):
-        deal(step).start()
     mine = pl.ds(pl.multiple_of(ring.me * head, head), head)
-    by_token[:, mine] = attended[ring.me]
 
     before = lax.broadcasted_iota(jnp.int32, (tok, tok), 0)
     after = lax.broadcasted_iota(jnp.int32, (tok, tok), 1)
@@ -1255,8 +1399,6 @@
         places[c] = jnp.where(jnp.broadcast_to(here, (8, tok)) > 0.5, count, -1.0)
 
     loads[0].wait()
-    for step in range(1, n):
-        deal(step).wait()
     tile = min(512, width)
     squares = jnp.zeros((tok, 1), F32)
     for start in range(0, width, tile):
@@ -1562,22 +1704,7 @@
     d_attn[...] = d_value.astype(BF16)
     for start in range(0, width, tile):
         cols = slice(start, start + tile)
-        by_token[:, cols] = dot(d_attn[...], w_near[cols, :], BY_LAST).astype(BF16)
-
-    def deal_back(step):
-        there = ring.peer(step)
-        cols = pl.ds(pl.multiple_of(there * head, head), head)
-        return remote(
-            by_token.at[:, cols],
-            d_attended.at[ring.me],
-            send.at[3, step],
-            recv.at[3, step],
-            {"seq": there},
-        )
-
-    for step in range(1, n):
-        deal_back(step).start()
-    d_attended[ring.me] = by_token[:, mine]
+        d_by_token[:, cols] = dot(d_attn[...], w_near[cols, :], BY_LAST).astype(BF16)
     for step in range(1, n):
         publish(step).start()
     kept.start()
@@ -1609,13 +1736,12 @@
     for step in range(1, n):
         push(ring.peer(step)).wait_send()
     for step in range(1, n):
-        deal_back(step).wait()
         publish(step).wait()
     kept.wait()
 
 
 def core_stage(
-    n, f, attended, w_out, tokens, upstream, gain, router, routes, routes_all, upstream_all, halves
+    n, f, by_token, w_out, tokens, upstream, gain, router, routes, routes_all, upstream_all, halves
 ):
     tok, width = tokens.shape
     experts = router.shape[0]
@@ -1631,7 +1757,7 @@
             shape((tok, width), F32),
             shape((tok, width), F32),
             shape((tok, width), BF16),
-            shape((n, tok, width // n), BF16),
+            shape((tok, width), BF16),
             shape((n, experts, tok), BF16),
             shape((1, width), F32),
             shape((n, tok, width // n), BF16),
@@ -1642,14 +1768,13 @@
             shape((n, capacity, units), BF16),
             shape((n, tok, width), BF16),
         ],
-        in_specs=[VMEM, ANY] + [VMEM] * 6 + [ANY] * (1 + 3 * f),
+        in_specs=[VMEM, ANY] + [VMEM] * 6 + [ANY] * (4 * f),
         out_specs=[VMEM] * 4 + [ANY, VMEM] + [ANY] * 7,
         scratch_shapes=[
             pltpu.VMEM((width, width), BF16),
             pltpu.VMEM((width, units), BF16),
             pltpu.VMEM((width, units), BF16),
             pltpu.VMEM((width, units), BF16),
-            pltpu.VMEM((tok, width), BF16),
             pltpu.VMEM((experts, tok), BF16),
             pltpu.VMEM((n, 8, tok), F32),
             pltpu.VMEM((n, 8, tok), F32),
@@ -1682,7 +1807,7 @@
             kind((5, n)),
             kind((5, n)),
             kind((2,)),
-            kind((3, f)),
+            kind((4, f)),
             kind((2, 2)),
             kind((2, 6, 2)),
             kind((2, chips)),
@@ -1691,20 +1816,22 @@
             collective_id=1, has_side_effects=True, vmem_limit_bytes=67_000_000
         ),
         name="core_stage",
-    )(attended, w_out, tokens, upstream, gain, router, routes, routes_all, upstream_all, *halves)
+    )(by_token, w_out, tokens, upstream, gain, router, routes, routes_all, upstream_all, *halves)
 
 
 def last_kernel(n, f, *refs):
     d_mixed, w_head, qkv_part, tokens, gain, d_middle, gain_two, gain_head = refs[:8]
-    middle, third, moe_part = refs[8:11]
-    far_refs = refs[11:16]
-    d_inputs, qkv_rows, gains_out, third_in, grads_out, result = refs[16:22]
-    beside_rows, summed, gain_rows, gain_in, gain_side, stage = refs[22:28]
-    near_refs = refs[28:33]
+    middle, proj, router, moe_part = refs[8:12]
+    far_refs = refs[12:17]
+    d_inputs, qkv_out, gains_out, second_in, third_in, grads_out, result = refs[17:24]
+    proj_out, router_out = refs[24:26]
+    beside_rows, summed, qkv_rows, gain_rows, gain_in, gain_side, stage, far_stage = refs[26:34]
+    proj_low, proj_in, router_low = refs[34:37]
+    near_refs = refs[37:42]
     rows_in, d_in, d_gate, d_up, inner_in = near_refs
-    buffers, fold_sems = refs[33:38], refs[38:42]
-    stored_buffers, stored_sems = refs[42:46], refs[46:51]
-    side_send, side_recv, send, recv, keep, stage_sem, load_sem = refs[51:]
+    buffers, fold_sems = refs[42:47], refs[47:51]
+    stored_buffers, stored_sems = refs[51:55], refs[55:60]
+    side_send, side_recv, send, recv, keep, stage_sem, load_sem, far_send, far_recv = refs[60:]
     ring = Ring(n, f)
     _, width = tokens.shape
     slice_width = width // n
@@ -1712,7 +1839,7 @@
     chips = ring.chips
     size = width // chips
     loads = [
-        pltpu.make_async_copy(source if k < 2 else source.at[:, :units], target, load_sem.at[k])
+        pltpu.make_async_copy(source.at[:, :units] if k == 2 else source, target, load_sem.at[k])
         for k, (source, target) in enumerate(zip(far_refs, near_refs))
     ]
     greet(ring, True, True)
@@ -1730,6 +1857,32 @@
     for step in range(1, f):
         side(step).start()
 
+    def proj_side(step):
+        there = ring.beside(step)
+        return remote(
+            proj_low.at[there],
+            proj_in.at[step - 1],
+            side_send.at[3, step],
+            side_recv.at[3, step],
+            {"fsdp": there},
+        )
+
+    def router_side(step):
+        return remote(
+            router_low.at[0],
+            router_low.at[step],
+            side_send.at[4, step],
+            side_recv.at[4, step],
+            {"fsdp": ring.beside(step)},
+        )
+
+    for x in range(f):
+        proj_low[x] = proj[x].astype(BF16)
+    router_low[0] = router[...].astype(BF16)
+    for step in range(1, f):
+        proj_side(step).start()
+        router_side(step).start()
+
     def part(chunk, target):
         tile = min(512, width)
         for start in range(0, width, tile):
@@ -1758,8 +1911,40 @@
             def _():
                 store(i - 2, which).wait()
 
-            stage[slot, which] = dot(left[:, these], right[...], BY_FIRST)
+            stage[slot, which] = dot(left[:, these], right[:, :units], BY_FIRST).astype(BF16)
             store(i, which).start()
+        afar(i)
+
+    def far(kind, i, j):
+        these = pl.ds(pl.multiple_of(i * size, size), size)
+        return remote(
+            far_stage.at[lax.rem(i, 2), kind, j],
+            [second_in, third_in][kind].at[j, these],
+            far_send.at[kind, i, j],
+            far_recv.at[kind, i, j],
+            {"fsdp": ring.beside(f - 1 - j)},
+        )
+
+    def afar(i):
+        these = pl.ds(pl.multiple_of(i * size, size), size)
+        slot = lax.rem(i, 2)
+
+        def make(kind, first_tile, left, right):
+            @pl.when(i >= first_tile + 2)
+            def _():
+                for j in range(f - 1):
+                    far(kind, i - 2, j).wait_send()
+
+            @pl.when(i >= first_tile)
+            def _():
+                for j in range(f - 1):
+                    part = slice((j + 1) * units, (j + 2) * units)
+                    value = dot(left[:, these], right[:, part], BY_FIRST)
+                    far_stage[slot, kind, j] = value.astype(BF16)
+                    far(kind, i, j).start()
+
+        make(0, EARLY, rows_in, d_up)
+        make(1, 0, d_in, inner_in)
 
     def push(step):
         there = ring.peer(step)
@@ -1773,17 +1958,6 @@
 
     local = pltpu.make_async_copy(summed.at[ring.me], qkv_rows.at[ring.me], keep.at[0])
 
-    def far(step):
-        return remote(
-            third.at[step - 1],
-            third_in.at[step - 1],
-            side_send.at[2, step],
-            side_recv.at[2, step],
-            {"fsdp": ring.beside(f - step)},
-        )
-
-    for step in range(1, f):
-        far(step).start()
     stored = Stored(ring, moe_part, stored_buffers, stored_sems)
     fold.produce(0)
     stored.begin()
@@ -1859,6 +2033,15 @@
 
     for step in range(1, f):
         sums(step).start()
+    proj_total = proj[ring.mine]
+    router_total = router[...]
+    for step in range(1, f):
+        proj_side(step).wait()
+        router_side(step).wait()
+        proj_total = proj_total + proj_in[step - 1].astype(F32)
+        router_total = router_total + router_low[step].astype(F32)
+    proj_out[...] = proj_total
+    router_out[...] = router_total
     fold.close()
     for i in (chips - 2, chips - 1):
         for which in range(3):
@@ -1868,61 +2051,81 @@
     for step in range(1, n):
         push(step).wait()
     local.wait()
+    piece = qkv_rows.shape[2] // 3
+    for h in range(n):
+        for k in range(3):
+            start = k * width + h * piece
+            qkv_out[:, start : start + piece] = qkv_rows[
+                h, :, k * piece : (k + 1) * piece
+            ].astype(F32)
     for step in range(1, f):
         sums(step).wait()
         total = total + gain_side[step]
     gains_out[...] = total
-    for step in range(1, f):
-        far(step).wait()
+    for j in range(f - 1):
+        for kind, first_tile in ((0, EARLY), (1, 0)):
+            for i in range(first_tile, chips):
+                far(kind, i, j).wait_recv()
+                if i >= chips - 2:
+                    far(kind, i, j).wait_send()
 
 
 def last_stage(
     n, f, d_mixed, w_head, qkv_part, tokens, gain, d_middle, gain_two, gain_head,
-    middle, third, moe_part, rows_in, d_in, d_gate, d_up, inner_in
+    middle, proj, router, moe_part, rows_in, d_in, d_gate, d_up, inner_in, second
 ):
     tok, width = tokens.shape
     rows, across = qkv_part.shape[2:]
-    units = third.shape[2]
+    units = second.shape[2]
     kind = pltpu.SemaphoreType.DMA
     shape = jax.ShapeDtypeStruct
     return pl.pallas_call(
         partial(last_kernel, n, f),
         out_shape=[
             shape((tok, width), F32),
-            shape((n, rows, across), BF16),
+            shape((rows, n * across), F32),
             shape((8, width // n), F32),
-            shape(third.shape, BF16),
-            shape((3, width, units), F32),
+            shape(second.shape, BF16),
+            shape(second.shape, BF16),
+            shape((3, width, units), BF16),
             shape((tok, width), BF16),
+            shape((rows, width), F32),
+            shape(router.shape, F32),
         ],
-        in_specs=[VMEM] * 9 + [ANY] * 7,
-        out_specs=[VMEM] * 3 + [ANY] * 2 + [VMEM],
+        in_specs=[VMEM] * 11 + [ANY] * 6,
+        out_specs=[VMEM] * 3 + [ANY] * 3 + [VMEM] * 3,
         scratch_shapes=[
             pltpu.VMEM((max(f - 1, 1), n, rows, across), BF16),
+            pltpu.VMEM((n, rows, across), BF16),
             pltpu.VMEM((n, rows, across), BF16),
             pltpu.VMEM((8, width), F32),
             pltpu.VMEM((n, 8, width // n), F32),
             pltpu.VMEM((f, 8, width // n), F32),
-            pltpu.VMEM((2, 3, 2 * width // n, units), F32),
+            pltpu.VMEM((2, 3, 2 * width // n, units), BF16),
+            pltpu.VMEM((2, 2, max(f - 1, 1), 2 * width // n, units), BF16),
+            pltpu.VMEM(proj.shape, BF16),
+            pltpu.VMEM((max(f - 1, 1),) + proj.shape[1:], BF16),
+            pltpu.VMEM((f,) + router.shape, BF16),
             pltpu.VMEM(rows_in.shape, BF16),
             pltpu.VMEM(rows_in.shape, BF16),
             pltpu.VMEM((rows_in.shape[0], units), BF16),
-            pltpu.VMEM((rows_in.shape[0], units), BF16),
-            pltpu.VMEM((rows_in.shape[0], units), BF16),
+            pltpu.VMEM(d_up.shape, BF16),
+            pltpu.VMEM(inner_in.shape, BF16),
         ]
         + Fold.buffers(n, tok, width)
         + Fold.semaphores(n)
         + Stored.buffers(n, tok, width)
         + Stored.semaphores(n)
-        + [kind((3, f)), kind((3, f)), kind((2, n)), kind((2, n)), kind((2,)), kind((2, 3))]
-        + [kind((5,))],
+        + [kind((5, f)), kind((5, f)), kind((2, n)), kind((2, n)), kind((2,)), kind((2, 3))]
+        + [kind((5,))]
+        + [kind((2, n // 2, max(f - 1, 1))), kind((2, n // 2, max(f - 1, 1)))],
         compiler_params=pltpu.CompilerParams(
             collective_id=4, has_side_effects=True, vmem_limit_bytes=67_000_000
         ),
         name="last_stage",
     )(
         d_mixed, w_head, qkv_part, tokens, gain, d_middle, gain_two, gain_head,
-        middle, third, moe_part, rows_in, d_in, d_gate, d_up, inner_in
+        middle, proj, router, moe_part, rows_in, d_in, d_gate, d_up, inner_in
     )
 
 
@@ -1947,7 +2150,6 @@
     tokens_low = inputs[0]
     upstream_low = cotangent[0]
     local_routes = routes[0].T
-    me = lax.axis_index("seq")
     mine = lax.axis_index("fsdp")
     tok, width = tokens_low.shape
     length = tok * n
@@ -1958,8 +2160,6 @@
     capacity = min(tok, 5 * tok * TOPK // (4 * experts))
     factor = head_size ** (-0.5)
 
-    by_head = w_qkv.reshape(rows, 3, HEADS, head_size).transpose(2, 0, 1, 3)
-    by_head = by_head.reshape(HEADS, rows, across)
     small = jnp.concatenate([w_router, norm_gains], 1)
     small = jnp.pad(small, ((0, 0), (0, 128 - small.shape[1])))
     (
@@ -1972,19 +2172,28 @@
         gate_near,
         up_near,
         w_out_all,
-    ) = first_gather(n, f, tokens_low, by_head, small, local_routes, w_out, w_gate[0], w_up[0])
+    ) = first_gather(n, f, tokens_low, w_qkv, small, local_routes, w_out, w_gate[0], w_up[0])
     w_out_all = w_out_all.reshape(width, width)
-    gates = [w_gate[0]] + [gate_near[j] for j in range(f - 1)]
-    ups = [w_up[0]] + [up_near[j] for j in range(f - 1)]
-    w_low, _ = lax.optimization_barrier((w_down[0], mixed))
-    downs = [shift_fsdp(w_low, j, f) for j in range(f)]
+    up_low, down_low, _ = lax.optimization_barrier((w_up[0, width // 2 :], w_down[0], mixed))
+    halves = [w_gate[0], w_down[0], w_up[0]]
+    for j in range(1, f):
+        up_rest = shift_fsdp(up_low, j, f)
+        down = shift_fsdp(down_low, j, f)
+        halves += [gate_near[j - 1], down, up_near[j - 1], up_rest]
     hidden_one = hidden_one.reshape(length, width)
     w_head = w_head.reshape(width, across)
-    own = lax.dynamic_slice_in_dim(gains, me * head_size, head_size, 1)
     tables, starts = angles_of(n, tok, head_size)
-    queries, keys, values, attended, exact, sums, squares, cosine, sine, upstream_all = attention(
-        n, f, mixed, tables, starts, own, upstream_low, factor
-    )
+    (
+        queries,
+        keys,
+        values,
+        attended,
+        exact,
+        sums,
+        squares,
+        upstream_all,
+        by_token,
+    ) = attention(n, f, mixed, tables, starts, gains, upstream_low, factor)
 
     (
         d_middle,
@@ -2003,7 +2212,7 @@
     ) = core_stage(
         n,
         f,
-        attended.reshape(n, tok, head_size),
+        by_token,
         w_out_all,
         tokens_low,
         upstream_low,
@@ -2012,59 +2221,49 @@
         local_routes,
         routes_all,
         upstream_all,
-        gates + ups + downs,
+        halves,
     )
     flat = n * capacity
     units = w_gate.shape[2]
     expert_rows = expert_rows.reshape(flat, width)
     d_produced = d_produced.reshape(flat, width)
     inner, d_gate, d_up = (v.reshape(flat, f * units) for v in (inner, d_gate, d_up))
-    pairs = ((expert_rows, d_gate), (expert_rows, d_up), (d_produced, inner))
-
-    def others(which):
-        left, right = pairs[which]
-        return [
-            dot(left, right[:, j * units : (j + 1) * units], BY_FIRST).astype(BF16)
-            for j in range(1, f)
-        ]
-
-    first, second = others(0), others(1)
-    d_attended, first, second = lax.optimization_barrier((d_attended, first, second))
-    first = [shift_fsdp(v, f - 1 - j, f) for j, v in enumerate(first)]
-    second = [shift_fsdp(v, f - 1 - j, f) for j, v in enumerate(second)]
-    d_mixed, gain_head, d_attn_all, third, qkv_part = attention_back(
+    d_mixed, gain_head, qkv_part, proj, router_part, first, second = attention_back(
         n,
         f,
         queries,
         keys,
         values,
-        d_attended.reshape(length, head_size),
+        d_attended,
         sums,
         exact,
         mixed,
-        cosine,
-        sine,
-        own,
+        tables,
+        starts,
+        gains,
         squares,
         d_attn,
-        d_produced,
-        inner,
+        attended,
+        own_hidden,
+        d_logits_all,
+        expert_rows,
+        d_gate,
+        d_up,
         hidden_one,
         rows,
         factor,
     )
-    d_attn_all = d_attn_all.reshape(length, width)
-    proj_part = dot(attended, d_attn_all, BY_FIRST)
-    router_part = jnp.einsum(
-        "ntc,nkt->ck", own_hidden, d_logits_all, preferred_element_type=F32
-    )
-    both = jnp.concatenate([proj_part, router_part], 1).reshape(f, rows, width + experts)
-    d_mixed, both = lax.optimization_barrier((d_mixed, both))
-    proj = lax.dynamic_index_in_dim(both, mine, 0, keepdims=False)
-    for j in range(1, f):
-        part = lax.dynamic_index_in_dim(both, (mine + j) % f, 0, keepdims=False)
-        proj = proj + shift_fsdp(part.astype(BF16), j, f).astype(F32)
-    grad_inputs, qkv_rows, gains_own, third, grads_own, result = last_stage(
+    (
+        grad_inputs,
+        grad_qkv,
+        gains_own,
+        second_rest,
+        third,
+        grads_own,
+        result,
+        grad_proj,
+        grad_router,
+    ) = last_stage(
         n,
         f,
         d_mixed.reshape(n, tok, across),
@@ -2076,34 +2275,37 @@
         gain_two,
         gain_head,
         middle,
-        third,
+        proj.reshape(f, rows, width),
+        router_part,
         moe_part,
         expert_rows,
         d_produced,
         d_gate,
         d_up,
         inner,
+        second,
     )
+    grad_router = lax.dynamic_slice_in_dim(grad_router, mine * rows, rows, 1).T
+    split = EARLY * (width // (n // 2))
     grads = []
-    for which, arrived in enumerate((first, second, [third[j] for j in range(f - 1)])):
-        total = grads_own[which]
-        for part in arrived:
+    for which in range(3):
+        total = grads_own[which].astype(F32)
+        for j in range(f - 1):
+            if which == 1:
+                late = jnp.arange(width)[:, None] >= split
+                part = jnp.where(late, second_rest[j], second[j])
+            else:
+                part = (first if which == 0 else third)[j]
             total = total + part.astype(F32)
         grads.append(total[None])
-    grad_qkv = (
-        qkv_rows.reshape(HEADS, rows, 3, head_size)
-        .transpose(1, 2, 0, 3)
-        .reshape(rows, 3 * width)
-        .astype(F32)
-    )
     gains_out = jnp.stack([gains_own[0], gains_own[2], gains_own[3], gains_own[1]], 1)
     grad_gains = lax.dynamic_slice_in_dim(gains_out, mine * rows, rows, 0)
     return (
         result[None],
         grad_inputs[None],
         grad_qkv,
-        proj[:, :width],
-        proj[:, width:],
+        grad_proj,
+        grad_router,
         grad_gains,
         *grads,
     )

time: 638 us -> 553 us (0.87)
  the two profiles are of different devices: /device:TPU:0 before, /device:TPU:13 now
where the time goes in v3:
time: 553 us; the launch traced here: 544 us
  Pallas kernels  518 us (94%)
  other arithmetic  12.1 us (2%)
  local copies, waits for them, and re-layouts  11.7 us (2%)
    pallas_call x1, Pallas kernels, first_gather(): pl.pallas_call(partial(first_kernel, n, f), out_shape=[shape((n, tok, wid...  126 us
    pallas_call x1, Pallas kernels, core_stage(): pl.pallas_call(partial(core_kernel, n, f), out_shape=[shape((tok, width),...  121 us
    pallas_call x1, Pallas kernels, last_stage(): pl.pallas_call(partial(last_kernel, n, f), out_shape=[shape((tok, width),...  114 us
    pallas_call x1, Pallas kernels, attention_back(): pl.pallas_call(partial(attention_back_kernel, n, f, factor), out_shape=[s...  83.6 us
    pallas_call x1, Pallas kernels, attention(): pl.pallas_call(partial(attention_kernel, n, f, factor), out_shape=[shape(...  73.5 us
  transfers between devices with their start and end apart: 2, of which 0 were waited for; matrix products, arithmetic and copies ran while one was open for 1% of the time, Pallas kernels for 14%

profile of v3, /device:TPU:13, one launch (start us, length us, event | category | flops | bytes accessed | tf_op | source)
XLA Modules:
  0.0 544.2 jit_solution(17263257479052773316)
XLA Ops:
  0.6 0.7 pad_maximum_fusion
  1.4 0.1 copy.21
  1.5 2.3 slice_bitcast_fusion
  3.7 0.6 pad.4.refs_2_
  4.3 126.4 %first_gather.1 = (bf16[16,128,2048]{2,1,0:T(8,128)(2,1)}, f32[2048,384]{1,0:T(8,128)}, bf16[16,2,64,384]{3,2,1,0:T(8,128)(2,1)}, bf16[16,2048]{1,0:T(8,128)(2,1...) custom-call(bf16[128,2048]{1,0:T(8,128)(2,1)} %bitcast.48, ...), custom_call_target="tpu_custom_call" | custom-call | tf_op jit(solution)/shard_map/first_gather/pallas_call | solution.py:785
  130.7 0.3 collective-permute-start
  131.1 1.2 collective-permute-start.1
  132.3 0.3 multiply_cosine_fusion
  132.7 0.1 maximum_maximum_fusion
  132.8 0.7 slice.48.refs_1_.refs_7_
  133.4 0.7 maximum_maximum_fusion.1
  134.1 73.5 %attention.1 = (bf16[2048,128]{1,0:T(8,128)(2,1)}, bf16[2048,128]{1,0:T(8,128)(2,1)}, bf16[2048,128]{1,0:T(8,128)(2,1)}, bf16[2048,128]{1,0:T(8,128)(2,1)}, f32[...) custom-call(f32[2048,384]{1,0:T(8,128)} %get-tuple-element.58.refs_0, ...), custom_call_target="tpu_custom_call" | custom-call | flops 1073741824 | bytes 2097152 | tf_op jit(solution)/shard_map/attention/pallas_call | solution.py:1025
  207.6 1.5 fusion
  209.2 0.0 collective-permute-done.1.refs_15_
  209.2 0.0 collective-permute-done.refs_13_
  209.2 120.5 %core_stage.1 = (f32[128,2048]{1,0:T(8,128)}, f32[128,2048]{1,0:T(8,128)}, bf16[128,2048]{1,0:T(8,128)(2,1)}, bf16[128,2048]{1,0:T(8,128)(2,1)}, bf16[16,16,128]...) custom-call(bf16[128,2048]{1,0:T(8,128)(2,1)} %get-tuple-element.63., ...), custom_call_target="tpu_custom_call" | custom-call | tf_op jit(solution)/shard_map/core_stage/pallas_call | solution.py:1754
  329.7 83.6 %attention_back.1 = (bf16[2048,384]{1,0:T(8,128)(2,1)}, f32[8,128]{1,0:T(8,128)}, bf16[2,16,64,384]{3,2,1,0:T(8,128)(2,1)}, f32[128,2048]{1,0:T(8,128)}, f32[16,...) custom-call(bf16[2048,128]{1,0:T(8,128)(2,1)} %get-tuple-element.60.refs_0_, ...), custom_call_target="tpu_custom_call" | custom-call | tf_op jit(solution)/shard_map/attention_back/pallas_call | solution.py:1286
  413.3 113.9 %last_stage.1 = (f32[128,2048]{1,0:T(8,128)}, f32[64,6144]{1,0:T(8,128)}, f32[8,128]{1,0:T(8,128)}, bf16[1,2048,512]{2,1,0:T(8,128)(2,1)}, bf16[1,2048,512]{2,1,...) custom-call(bf16[16,128,384]{2,1,0:T(8,128)(2,1)} %bitcast.56, ...), custom_call_target="tpu_custom_call" | custom-call | tf_op jit(solution)/shard_map/last_stage/pallas_call | solution.py:2082
  527.3 0.8 slice_bitcast_fusion.4
  528.1 0.7 constant_dynamic-slice_fusion
  528.7 1.4 dynamic-slice_bitcast_fusion
  530.1 0.0 copy-start.3
  530.1 0.0 copy-start.1
  530.1 10.2 %convert_add_fusion = (f32[1,2048,512]{2,1,0:T(8,128)}, f32[1,2048,512]{2,1,0:T(8,128)}, f32[1,2048,512]{2,1,0:T(8,128)}) fusion(bf16[1,2048,512]{2,1,0:T(8,128)(2,1)} %get-tuple-element.106, bf16[3,2048,512]{2,1,0:T(8,128)(2,1)} %get-tuple-element.102, bf16[1,2048,512]{2,1,0:T(8,128)(2,1)} %get-tuple-element.104, bf16[1,2048,512]{2,1,0:T(8,128)(2,1)} %get-tuple-element.105, ...), kind=kLoop, calls=%fused_computation | loop fusion | flops 10485760 | bytes 27265024 | tf_op jit(solution)/shard_map/add | solution.py:2299
  540.3 0.0 copy-start
  540.3 0.0 copy-done.3
  540.3 0.8 copy.26
  541.1 0.0 copy-done.1
  541.1 0.0 copy-start.2
  541.1 1.0 copy.27
  542.1 0.0 copy-done
  542.1 1.1 copy.28
  543.2 0.0 copy-done.2
  543.2 0.8 copy.29
  (6 shorter events, 0.0 us)
Async XLA Ops:
  130.7 78.4 %collective-permute-start = (bf16[2048,512]{1,0:T(8,128)(2,1)}, bf16[2048,512]{1,0:T(8,128)(2,1)}, u32[]{:S(2)}, u32[]{:S(2)}) collective-permute-start(bf16[2048,512]{1,0:T(8,128)(2,1)} %bitcast.52), channel_id=1, source_target_pairs={{0,1},{1,0},{2,3},{3,2},{4,5},{5,4},{6,7},{7,6},{8,9},{9,8},{10,11... | collective-permute-start | bytes 6291464 | tf_op jit(solution)/shard_map/ppermute | solution.py:2146
  131.1 78.1 %collective-permute-start.1 = (bf16[1024,512]{1,0:T(8,128)(2,1)}, bf16[1024,512]{1,0:T(8,128)(2,1)}, u32[]{:S(2)}, u32[]{:S(2)}) collective-permute-start(bf16[1024,512]{1,0:T(8,128)(2,1)} %slice_bitcast_fusion), channel_id=1, source_target_pairs={{0,1},{1,0},{2,3},{3,2},{4,5},{5,4},{6,7},{7,6},{8,9},{9,8},{10,11... | collective-permute-start | bytes 3145736 | tf_op jit(solution)/shard_map/ppermute | solution.py:2146
  530.1 10.2 %copy-start.3 = (bf16[128,2048]{1,0:T(8,128)(2,1)S(1)}, bf16[128,2048]{1,0:T(8,128)(2,1)}, u32[]{:S(2)}) copy-start(bf16[128,2048]{1,0:T(8,128)(2,1)} %get-tuple-element.96) | copy-start | bytes 1572868
  530.1 11.0 %copy-start.1 = (f32[128,2048]{1,0:T(8,128)S(1)}, f32[128,2048]{1,0:T(8,128)}, u32[]{:S(2)}) copy-start(f32[128,2048]{1,0:T(8,128)} %get-tuple-element.97) | copy-start | bytes 3145732
  540.3 1.8 copy-start
  541.1 2.1 copy-start.2

commit v4 on v3

--- a/solution.py
+++ b/solution.py
@@ -6,7 +6,6 @@
 from jax.experimental import pallas as pl
 from jax.experimental.pallas import tpu as pltpu
 from jax.sharding import PartitionSpec as P
-
 
 HEADS = 16
 TOPK = 8
@@ -17,6 +16,8 @@
 MESH = pl.DeviceIdType.MESH
 PIECES = 2
 EARLY = 3
+UPPER = 4
+DOWN = 7
 ANY = pl.BlockSpec(memory_space=pl.ANY)
 VMEM = pl.BlockSpec(memory_space=pltpu.VMEM)
 MATMUL = (((1,), (0,)), ((), ()))
@@ -68,10 +69,14 @@
     barrier = pltpu.get_barrier_semaphore()
     count = 0
     if everyone:
-        for step in range(1, ring.n):
+
+        def each_0(step, carry):
             pl.semaphore_signal(
                 barrier, inc=1, device_id={"seq": ring.peer(step)}, device_id_type=MESH
             )
+            return carry
+
+        lax.fori_loop(1, ring.n, each_0, 0)
         count += ring.n - 1
     else:
         for other in (ring.right, ring.left, ring.mate):
@@ -460,17 +465,18 @@
             self.going[lax.rem(i, 2), rows] = value.astype(BF16)
             self.hop(i, s).start()
 
-    def run(self, finish, filler, after):
+    def run(self, finish, filler, before, after):
         last = self.last
 
         def body(i, carry):
             self.produce(i)
+            before(i)
             self.step(i)
             after(i)
             filler(i)
             return carry
 
-        lax.fori_loop(1, last, body, 0)
+        lax.fori_loop(0, last, body, 0)
         self.produce(last)
         filler(last)
         self.swap(last).wait_recv()
@@ -550,17 +556,18 @@
 
     def begin(self):
         self.load(0).start()
-
-        def body(i, carry):
-            self.swap(i).start()
-            return carry
-
-        lax.fori_loop(0, self.last + 1, body, 0)
+        self.swap(0).start()
+        self.swap(1).start()
 
     def step(self, i):
         self.load(i).wait()
         self.load(i + 1).start()
         self.swap(i).wait_recv()
+
+        @pl.when(i + 2 <= self.last)
+        def _():
+            self.swap(i + 2).start()
+
         slot = lax.rem(i, 2)
 
         @pl.when(i >= 2)
@@ -667,7 +674,7 @@
             {"fsdp": ring.beside(over)},
         )
 
-    half_parts = ring.chips + ring.chips // 2
+    half_parts = ring.chips + ring.chips * UPPER // 8
 
     gather.begin()
     for over in range(1, f):
@@ -680,9 +687,13 @@
     ]
     for copy in copies:
         copy.start()
-    for step in range(1, n):
+
+    def each_1(step, carry):
         for kind in (1, 0, 2):
             push(kind, step).start()
+        return carry
+
+    lax.fori_loop(1, n, each_1, 0)
     for over in range(1, f):
         aside(1, 0, over, True).start()
         aside(0, 0, over, True).start()
@@ -704,7 +715,8 @@
                     push(kind, step).wait_recv()
                     for over in range(1, f):
                         aside(kind, step, over, False).start()
-        else:
+        parts = widen(parts)
+        while i >= 4 and parts < half_parts:
             parts = widen(parts)
         if i == hops - 2:
             copies[3].wait()
@@ -714,14 +726,22 @@
     gather.finish()
     for copy in copies[:3]:
         copy.wait()
-    for step in range(1, n):
+
+    def each_2(step, carry):
         push(2, step).wait_recv()
         for kind in (0, 1, 2):
             push(kind, step).wait_send()
-    for step in range(n):
+        return carry
+
+    lax.fori_loop(1, n, each_2, 0)
+
+    def each_3(step, carry):
         for kind in (0, 1):
             for over in range(1, f):
                 aside(kind, step, over, False).wait()
+        return carry
+
+    lax.fori_loop(0, n, each_3, 0)
 
     lanes = lax.broadcasted_iota(jnp.int32, (32, small.shape[1]), 1)
     places = lax.broadcasted_iota(jnp.int32, (32, small.shape[1]), 0)
@@ -758,15 +778,15 @@
         mixed[here, :] = total
         return carry
 
-    done = 0
-    for i in range(hops):
-        parts = widen(parts)
-        upto = min(n, -(-n * (i + 1) // hops))
-        lax.fori_loop(done, upto, project, 0)
-        done = upto
-        gather_out.pass_on(i)
     while parts < half_parts:
         parts = widen(parts)
+
+    def second_phase(i, carry):
+        lax.fori_loop(n * i // hops, n * (i + 1) // hops, project, 0)
+        gather_out.pass_on(i)
+        return carry
+
+    lax.fori_loop(0, hops, second_phase, 0)
     for c in range(n):
         out(c).wait()
     gather_out.finish()
@@ -792,7 +812,7 @@
             shape((8, width), F32),
             shape((n,) + routes.shape, jnp.int32),
             shape((max(f - 1, 1),) + w_gate.shape, BF16),
-            shape((max(f - 1, 1), w_up.shape[0] // 2, w_up.shape[1]), BF16),
+            shape((max(f - 1, 1), w_up.shape[0] * UPPER // 8, w_up.shape[1]), BF16),
             shape((n, f * w_out.shape[0], w_out.shape[1]), BF16),
         ],
         in_specs=[VMEM] * 5 + [ANY] * 2,
@@ -877,13 +897,21 @@
         return pltpu.make_async_copy(self.block, self.out.at[self.ring.me], self.keep.at[0])
 
     def begin(self):
-        for step in range(1, self.ring.n):
+
+        def each_4(step, carry):
             self.push(step).start()
+            return carry
+
+        lax.fori_loop(1, self.ring.n, each_4, 0)
         self.local().start()
 
     def finish(self):
-        for step in range(1, self.ring.n):
+
+        def each_5(step, carry):
             self.push(step).wait()
+            return carry
+
+        lax.fori_loop(1, self.ring.n, each_5, 0)
         self.local().wait()
 
     def total(self):
@@ -894,17 +922,32 @@
 
 
 def attention_kernel(n, f, factor, *refs):
-    mixed, tables, starts, gains, upstream = refs[:5]
-    q_ref, k_ref, v_ref, out_ref, exact_ref, sums_ref, squares = refs[5:12]
-    upstream_all, by_token = refs[12:14]
-    partial_sums, arrived, cosine, sine = refs[14:18]
-    sems, walk_sems = refs[18:21], refs[21:26]
-    deal_send, deal_recv, deal_keep = refs[26:]
+    mixed, tables, starts, gains, upstream, w_up, w_down = refs[:7]
+    q_ref, k_ref, v_ref, out_ref, exact_ref, sums_ref, squares = refs[7:14]
+    upstream_all, by_token, up_rest, down_near = refs[14:18]
+    partial_sums, arrived, cosine, sine = refs[18:22]
+    sems, walk_sems = refs[22:25], refs[25:30]
+    deal_send, deal_recv, deal_keep, wide_send, wide_recv = refs[30:]
     ring = Ring(n, f)
     length, head = q_ref.shape
     width = head * n
     block, count = blocks_of(length)
-    greet(ring, True, False)
+    greet(ring, True, True)
+    rest = up_rest.shape[1]
+    later = pl.ds(w_up.shape[0] - rest, rest)
+
+    def wide(kind, over):
+        return remote(
+            [w_up.at[later], w_down.at[pl.ds(0, down_near.shape[1])]][kind],
+            [up_rest, down_near][kind].at[over - 1],
+            wide_send.at[kind, over],
+            wide_recv.at[kind, over],
+            {"fsdp": ring.beside(over)},
+        )
+
+    for over in range(1, f):
+        wide(0, over).start()
+        wide(1, over).start()
     walk = Gather(ring, upstream, upstream_all, walk_sems)
     last = walk.last
     mine = pl.ds(pl.multiple_of(ring.me * head, head), head)
@@ -1012,13 +1055,20 @@
     for i in range(count, last):
         walk.pass_on(i)
     walk.finish()
-    for step in range(1, n):
+
+    def each_6(step, carry):
         deal(ring.peer(step)).wait_send()
         dealt(ring.peer(step)).wait_recv()
+        return carry
+
+    lax.fori_loop(1, n, each_6, 0)
     local.wait()
-
-
-def attention(n, f, mixed, tables, starts, gains, upstream, factor):
+    for over in range(1, f):
+        wide(0, over).wait()
+        wide(1, over).wait()
+
+
+def attention(n, f, mixed, tables, starts, gains, upstream, w_up, w_down, factor):
     length, head = mixed.shape[0], mixed.shape[1] // 3
     block, count = blocks_of(length)
     shape = jax.ShapeDtypeStruct
@@ -1034,9 +1084,11 @@
             shape((2 * count, block), F32),
             shape((n,) + upstream.shape, BF16),
             shape((length // n, head * n), BF16),
+            shape((max(f - 1, 1), w_up.shape[0] - w_up.shape[0] * UPPER // 8, w_up.shape[1]), BF16),
+            shape((max(f - 1, 1), w_down.shape[0] * DOWN // 8, w_down.shape[1]), BF16),
         ],
-        in_specs=[VMEM] * 5,
-        out_specs=[VMEM] * 7 + [ANY, VMEM],
+        in_specs=[VMEM] * 5 + [ANY] * 2,
+        out_specs=[VMEM] * 7 + [ANY, VMEM, ANY, ANY],
         scratch_shapes=[
             pltpu.VMEM((2 * count, block), F32),
             pltpu.VMEM((n, 2 * count, block), F32),
@@ -1046,7 +1098,8 @@
         + Spread.semaphores(n)
         + Gather.semaphores(n)
         + [pltpu.SemaphoreType.DMA((n,)), pltpu.SemaphoreType.DMA((n,))]
-        + [pltpu.SemaphoreType.DMA((1,))],
+        + [pltpu.SemaphoreType.DMA((1,))]
+        + [pltpu.SemaphoreType.DMA((2, f)), pltpu.SemaphoreType.DMA((2, f))],
         compiler_params=pltpu.CompilerParams(
             collective_id=5, has_side_effects=True, vmem_limit_bytes=67_000_000
         ),
@@ -1056,7 +1109,7 @@
             bytes_accessed=8 * length * head,
         ),
         name="attention",
-    )(mixed, tables, starts, gains, upstream)
+    )(mixed, tables, starts, gains, upstream, w_up, w_down)
 
 
 def attention_back_kernel(n, f, factor, *refs):
@@ -1103,8 +1156,12 @@
         d_ref.at[here_rows],
         deal_keep.at[0],
     )
-    for step in range(1, n):
+
+    def each_7(step, carry):
         deal(step).start()
+        return carry
+
+    lax.fori_loop(1, n, each_7, 0)
     local.start()
     walk = Gather(ring, d_attn, d_attn_all, walk_sems)
     walk.begin()
@@ -1112,9 +1169,9 @@
     tiles = ring.chips
     size = width // tiles
 
-    def send_first(tile, j):
-        kind, at = divmod(tile, tiles)
-        these = pl.ds(at * size, size)
+    def send_first(kind, at, j):
+        these = pl.ds(pl.multiple_of(at * size, size), size)
+        tile = kind * tiles + at
         return remote(
             first.at[tile, j],
             [first_in, second_in][kind].at[j, these],
@@ -1126,16 +1183,27 @@
     set_angles(n, tables, starts, cosine, sine)
     for load in loads[:3]:
         load.wait()
-    for tile in range(tiles + EARLY):
-        kind, at = divmod(tile, tiles)
-        for j in range(f - 1):
-            part = slice(j * units, (j + 1) * units)
-            right = [d_gate, d_up][kind]
-            value = dot(rows_in[:, at * size : (at + 1) * size], right[:, part], BY_FIRST)
-            first[tile, j] = value.astype(BF16)
-            send_first(tile, j).start()
-    for step in range(1, n):
+
+    def early(kind, right):
+        def body(at, carry):
+            these = pl.ds(pl.multiple_of(at * size, size), size)
+            for j in range(f - 1):
+                part = slice(j * units, (j + 1) * units)
+                value = dot(rows_in[:, these], right[:, part], BY_FIRST)
+                first[kind * tiles + at, j] = value.astype(BF16)
+                send_first(kind, at, j).start()
+            return carry
+
+        lax.fori_loop(0, EARLY if kind else tiles, body, 0)
+
+    early(0, d_gate)
+    early(1, d_up)
+
+    def each_8(step, carry):
         deal(step).wait()
+        return carry
+
+    lax.fori_loop(1, n, each_8, 0)
     local.wait()
     dq_ref[...] = jnp.zeros_like(dq_ref)
 
@@ -1266,7 +1334,7 @@
     lax.fori_loop(0, count, project, 0)
     for at in range(tiles + EARLY):
         for j in range(f - 1):
-            send_first(at, j).wait()
+            send_first(at // tiles, at % tiles, j).wait()
 
 
 def attention_back(
@@ -1340,7 +1408,8 @@
     rows_now, lifted, d_now, inner_now, d_gate_now, d_up_now, moe_now, d_weight, places = refs[:9]
     refs = refs[9:]
     hop_send, hop_recv, share_send, share_recv, swap_send, swap_recv = refs[:6]
-    sum_send, sum_recv, send, recv, keep, load_sem, lift_sem, stage_sem, own_sem = refs[6:]
+    sum_send, sum_recv, send, recv, keep, load_sem, lift_sem, stage_sem, own_sem = refs[6:15]
+    down_send, down_recv = refs[15:]
     ring = Ring(n, f)
     tok, width = tokens.shape
     head = width // n
@@ -1354,15 +1423,16 @@
     local_units = hidden_units // f
 
     loads = [pltpu.make_async_copy(w_out, w_near, keep.at[0])]
-    half_width = width // 2
+    half_width = width * UPPER // 8
+    soon = width * DOWN // 8
     sources = []
     for j in range(f):
         cols = slice(j * local_units, (j + 1) * local_units)
         sources.append((w_gate.at[:, cols], 0, j))
-        sources.append((w_down.at[:, cols], 2, j))
+        sources.append((w_down.at[pl.ds(0, soon), cols] if j else w_down.at[:, cols], 2, j))
         if j:
             sources.append((w_up.at[pl.ds(0, half_width), cols], 1, j))
-            sources.append((w_up.at[pl.ds(half_width, half_width), cols], 3, j))
+            sources.append((w_up.at[pl.ds(half_width, width - half_width), cols], 3, j))
         else:
             sources.append((w_up.at[:, cols], 1, j))
     for source, (target, kind, j) in zip(shards_in, sources):
@@ -1385,19 +1455,35 @@
 
     lift_copy(0, 0).start()
     lift_copy(0, 1).start()
-    greet(ring, True, False)
+    greet(ring, True, True)
+
+    def down_rest(over):
+        rows = pl.ds(soon, width - soon)
+        return remote(
+            shards_in[1].at[rows],
+            w_down.at[rows, over * local_units : (over + 1) * local_units],
+            down_send.at[over],
+            down_recv.at[over],
+            {"fsdp": ring.beside(over)},
+        )
+
+    for over in range(1, f):
+        down_rest(over).start()
 
     mine = pl.ds(pl.multiple_of(ring.me * head, head), head)
 
     before = lax.broadcasted_iota(jnp.int32, (tok, tok), 0)
     after = lax.broadcasted_iota(jnp.int32, (tok, tok), 1)
     earlier = jnp.where(before < after, 1.0, 0.0).astype(BF16)
-    for c in range(n):
+
+    def stand(c, carry):
         here = jnp.where(routes_all[c] == ring.me, 1.0, 0.0)
         here = jnp.sum(here, 0, keepdims=True)
         count = dot(jnp.broadcast_to(here, (8, tok)).astype(BF16), earlier, MATMUL)
         places[c] = jnp.where(jnp.broadcast_to(here, (8, tok)) > 0.5, count, -1.0)
-
+        return carry
+
+    lax.fori_loop(0, n, stand, 0)
     loads[0].wait()
     tile = min(512, width)
     squares = jnp.zeros((tok, 1), F32)
@@ -1464,11 +1550,16 @@
             {"seq": origin},
         )
 
-    for step in range(1, n):
+    def each_9(step, carry):
         push(ring.peer(step)).start()
+        return carry
+
+    lax.fori_loop(1, n, each_9, 0)
     weights_in[ring.me] = outgoing[ring.me]
     for load in loads[1:]:
         load.wait()
+    for over in range(1, f):
+        down_rest(over).wait_recv()
 
     def swap(i):
         return remote(
@@ -1658,22 +1749,26 @@
         def _():
             report(chunks[0], slot, 0).start()
 
-    pass_on(0)
-    work(0)
-
     def body(i, carry):
         @pl.when(i < last)
         def _():
             pass_on(i)
 
-        sum_step(i - 1)
+        @pl.when(i > 0)
+        def _():
+            sum_step(i - 1)
+
         work(i)
         return carry
 
-    lax.fori_loop(1, chips, body, 0)
+    lax.fori_loop(0, chips, body, 0)
     arrived[ring.me] = d_weight[last % 2, 0]
-    for step in range(1, n):
+
+    def each_10(step, carry):
         reported(ring.peer(step)).wait_recv()
+        return carry
+
+    lax.fori_loop(1, n, each_10, 0)
     gate_back = jnp.concatenate([arrived[e, 0:1, :] for e in range(n)], 0)
     gate_back = gate * (gate_back - jnp.sum(gate * gate_back, 0, keepdims=True))
     d_logits[...] = gate_back.astype(BF16)
@@ -1705,10 +1800,16 @@
     for start in range(0, width, tile):
         cols = slice(start, start + tile)
         d_by_token[:, cols] = dot(d_attn[...], w_near[cols, :], BY_LAST).astype(BF16)
-    for step in range(1, n):
+
+    def each_11(step, carry):
         publish(step).start()
+        return carry
+
+    lax.fori_loop(1, n, each_11, 0)
     kept.start()
 
+    for over in range(1, f):
+        down_rest(over).wait_send()
     for s in range(PIECES):
         share(last, s).wait_send()
 
@@ -1733,10 +1834,18 @@
                 give(kind, chunk_of(i, other), other, i % 2).wait()
             if other or i < last:
                 report(chunk_of(i, other), i % 2, other).wait_send()
-    for step in range(1, n):
+
+    def each_12(step, carry):
         push(ring.peer(step)).wait_send()
-    for step in range(1, n):
+        return carry
+
+    lax.fori_loop(1, n, each_12, 0)
+
+    def each_13(step, carry):
         publish(step).wait()
+        return carry
+
+    lax.fori_loop(1, n, each_13, 0)
     kept.wait()
 
 
@@ -1811,6 +1920,8 @@
             kind((2, 2)),
             kind((2, 6, 2)),
             kind((2, chips)),
+            kind((f,)),
+            kind((f,)),
         ],
         compiler_params=pltpu.CompilerParams(
             collective_id=1, has_side_effects=True, vmem_limit_bytes=67_000_000
@@ -1959,16 +2070,43 @@
     local = pltpu.make_async_copy(summed.at[ring.me], qkv_rows.at[ring.me], keep.at[0])
 
     stored = Stored(ring, moe_part, stored_buffers, stored_sems)
-    fold.produce(0)
-    stored.begin()
-    for load in loads:
-        load.start()
-    fold.step(0)
-    stored.step(0)
-    for load in loads:
-        load.wait()
-    filler(0)
-    fold.run(finish, filler, stored.step)
+
+    def before(i):
+        @pl.when(i == 0)
+        def _():
+            stored.begin()
+            for load in loads:
+                load.start()
+
+    def spread_qkv():
+        for step in range(1, f):
+            side(step).wait_recv()
+
+        def add(block, carry):
+            value = qkv_part[ring.mine, block].astype(F32)
+            for step in range(1, f):
+                value = value + beside_rows[step - 1, block].astype(F32)
+            summed[block] = value.astype(BF16)
+            return carry
+
+        lax.fori_loop(0, n, add, 0)
+
+        def each_14(step, carry):
+            push(step).start()
+            return carry
+
+        lax.fori_loop(1, n, each_14, 0)
+        local.start()
+
+    def after(i):
+        stored.step(i)
+
+        @pl.when(i == 0)
+        def _():
+            for load in loads:
+                load.wait()
+
+    fold.run(finish, filler, before, after)
 
     def settle(rows, value):
         result[rows, :] = (middle[rows, :] + value).astype(BF16)
@@ -1995,27 +2133,22 @@
 
     mine = pl.ds(pl.multiple_of(ring.me * slice_width, slice_width), slice_width)
     kept = pltpu.make_async_copy(gain_rows.at[:, mine], gain_in.at[ring.me], keep.at[1])
-    for step in range(1, n):
+
+    def each_15(step, carry):
         gains(step).start()
+        return carry
+
+    lax.fori_loop(1, n, each_15, 0)
     kept.start()
+    spread_qkv()
     d_value = inverse * gain[...] * grad - value * (inverse * inverse * inverse) * inner
     d_inputs[...] = d_middle[...] + d_value
-    for step in range(1, f):
-        side(step).wait_recv()
-
-    def add(block, carry):
-        value = qkv_part[ring.mine, block].astype(F32)
-        for step in range(1, f):
-            value = value + beside_rows[step - 1, block].astype(F32)
-        summed[block] = value.astype(BF16)
-        return carry
-
-    lax.fori_loop(0, n, add, 0)
-    for step in range(1, n):
-        push(step).start()
-    local.start()
-    for step in range(1, n):
+
+    def each_16(step, carry):
         gains(step).wait()
+        return carry
+
+    lax.fori_loop(1, n, each_16, 0)
     kept.wait()
     total = gain_head[...]
     for device in range(n):
@@ -2048,8 +2181,12 @@
             store(i, which).wait()
     for step in range(1, f):
         side(step).wait_send()
-    for step in range(1, n):
+
+    def each_17(step, carry):
         push(step).wait()
+        return carry
+
+    lax.fori_loop(1, n, each_17, 0)
     local.wait()
     piece = qkv_rows.shape[2] // 3
     for h in range(n):
@@ -2140,12 +2277,6 @@
     return both[:, :tok], both[:, tok:, None, :]
 
 
-def shift_fsdp(values, step, f):
-    if step == 0:
-        return values
-    return lax.ppermute(values, "fsdp", [(i, (i + step) % f) for i in range(f)])
-
-
 def shards(n, f, inputs, routes, w_qkv, w_out, w_router, norm_gains, w_gate, w_up, w_down, cotangent):
     tokens_low = inputs[0]
     upstream_low = cotangent[0]
@@ -2174,12 +2305,6 @@
         w_out_all,
     ) = first_gather(n, f, tokens_low, w_qkv, small, local_routes, w_out, w_gate[0], w_up[0])
     w_out_all = w_out_all.reshape(width, width)
-    up_low, down_low, _ = lax.optimization_barrier((w_up[0, width // 2 :], w_down[0], mixed))
-    halves = [w_gate[0], w_down[0], w_up[0]]
-    for j in range(1, f):
-        up_rest = shift_fsdp(up_low, j, f)
-        down = shift_fsdp(down_low, j, f)
-        halves += [gate_near[j - 1], down, up_near[j - 1], up_rest]
     hidden_one = hidden_one.reshape(length, width)
     w_head = w_head.reshape(width, across)
     tables, starts = angles_of(n, tok, head_size)
@@ -2193,7 +2318,12 @@
         squares,
         upstream_all,
         by_token,
-    ) = attention(n, f, mixed, tables, starts, gains, upstream_low, factor)
+        up_rest,
+        down_near,
+    ) = attention(n, f, mixed, tables, starts, gains, upstream_low, w_up[0], w_down[0], factor)
+    halves = [w_gate[0], w_down[0], w_up[0]]
+    for j in range(f - 1):
+        halves += [gate_near[j], down_near[j], up_near[j], up_rest[j]]
 
     (
         d_middle,

time: 553 us -> 540 us (0.976)
  the two profiles are of different devices: /device:TPU:13 before, /device:TPU:0 now
where the time goes in v4:
time: 540 us; the launch traced here: 536 us
  Pallas kernels  515 us (95%)
  other arithmetic  12.1 us (2%)
  local copies, waits for them, and re-layouts  7.97 us (1%)
    pallas_call x1, Pallas kernels, first_gather(): pl.pallas_call(partial(first_kernel, n, f), out_shape=[shape((n, tok, wid...  131 us
    pallas_call x1, Pallas kernels, core_stage(): pl.pallas_call(partial(core_kernel, n, f), out_shape=[shape((tok, width),...  121 us
    pallas_call x1, Pallas kernels, last_stage(): pl.pallas_call(partial(last_kernel, n, f), out_shape=[shape((tok, width),...  109 us
    pallas_call x1, Pallas kernels, attention_back(): pl.pallas_call(partial(attention_back_kernel, n, f, factor), out_shape=[s...  82.3 us
    pallas_call x1, Pallas kernels, attention(): pl.pallas_call(partial(attention_kernel, n, f, factor), out_shape=[shape(...  71.9 us

profile of v4, /device:TPU:0, one launch (start us, length us, event | category | flops | bytes accessed | tf_op | source)
XLA Modules:
  0.0 535.9 jit_solution(10401846464121031719)
XLA Ops:
  0.6 0.7 pad_maximum_fusion
  1.4 0.1 copy.21
  1.5 0.6 pad.4.refs_2_
  2.1 131.0 %first_gather.1 = (bf16[16,128,2048]{2,1,0:T(8,128)(2,1)}, f32[2048,384]{1,0:T(8,128)}, bf16[16,2,64,384]{3,2,1,0:T(8,128)(2,1)}, bf16[16,2048]{1,0:T(8,128)(2,1...) custom-call(bf16[128,2048]{1,0:T(8,128)(2,1)} %bitcast.51, ...), custom_call_target="tpu_custom_call" | custom-call | tf_op jit(solution)/shard_map/first_gather/pallas_call | solution.py:805
  133.1 0.3 multiply_cosine_fusion
  133.5 0.1 maximum_maximum_fusion
  133.6 0.7 slice.44.refs_1_.refs_7_
  134.2 0.7 maximum_maximum_fusion.1
  134.9 71.9 %attention.1 = (bf16[2048,128]{1,0:T(8,128)(2,1)}, bf16[2048,128]{1,0:T(8,128)(2,1)}, bf16[2048,128]{1,0:T(8,128)(2,1)}, bf16[2048,128]{1,0:T(8,128)(2,1)}, f32[...) custom-call(f32[2048,384]{1,0:T(8,128)} %get-tuple-element.58.refs_0, ...), custom_call_target="tpu_custom_call" | custom-call | flops 1073741824 | bytes 2097152 | tf_op jit(solution)/shard_map/attention/pallas_call | solution.py:1075
  206.8 1.5 fusion
  208.3 120.9 %core_stage.1 = (f32[128,2048]{1,0:T(8,128)}, f32[128,2048]{1,0:T(8,128)}, bf16[128,2048]{1,0:T(8,128)(2,1)}, bf16[128,2048]{1,0:T(8,128)(2,1)}, bf16[16,16,128]...) custom-call(bf16[128,2048]{1,0:T(8,128)(2,1)} %get-tuple-element.63., ...), custom_call_target="tpu_custom_call" | custom-call | tf_op jit(solution)/shard_map/core_stage/pallas_call | solution.py:1863
  329.2 82.3 %attention_back.1 = (bf16[2048,384]{1,0:T(8,128)(2,1)}, f32[8,128]{1,0:T(8,128)}, bf16[2,16,64,384]{3,2,1,0:T(8,128)(2,1)}, f32[128,2048]{1,0:T(8,128)}, f32[16,...) custom-call(bf16[2048,128]{1,0:T(8,128)(2,1)} %get-tuple-element.60.refs_0_, ...), custom_call_target="tpu_custom_call" | custom-call | tf_op jit(solution)/shard_map/attention_back/pallas_call | solution.py:1354
  411.5 109.0 %last_stage.1 = (f32[128,2048]{1,0:T(8,128)}, f32[64,6144]{1,0:T(8,128)}, f32[8,128]{1,0:T(8,128)}, bf16[1,2048,512]{2,1,0:T(8,128)(2,1)}, bf16[1,2048,512]{2,1,...) custom-call(bf16[16,128,384]{2,1,0:T(8,128)(2,1)} %bitcast.60, ...), custom_call_target="tpu_custom_call" | custom-call | tf_op jit(solution)/shard_map/last_stage/pallas_call | solution.py:2219
  520.5 0.0 copy-start.5
  520.5 0.0 copy-start.4
  520.6 0.0 copy-start.3
  520.6 0.0 copy-start.1
  520.6 10.2 %convert_add_fusion = (f32[1,2048,512]{2,1,0:T(8,128)}, f32[1,2048,512]{2,1,0:T(8,128)}, f32[1,2048,512]{2,1,0:T(8,128)}) fusion(bf16[1,2048,512]{2,1,0:T(8,128)(2,1)} %get-tuple-element.106, bf16[3,2048,512]{2,1,0:T(8,128)(2,1)} %get-tuple-element.102, bf16[1,2048,512]{2,1,0:T(8,128)(2,1)} %get-tuple-element.104, bf16[1,2048,512]{2,1,0:T(8,128)(2,1)} %get-tuple-element.105, ...), kind=kLoop, calls=%fused_computation | loop fusion | flops 10485760 | bytes 27265024 | tf_op jit(solution)/shard_map/add | solution.py:2429
  530.8 0.0 copy-start
  530.8 0.0 copy-done.5
  530.8 0.7 constant_dynamic-slice_fusion
  531.5 0.0 copy-done.4
  531.5 0.7 dynamic-slice_bitcast_fusion
  532.1 0.0 copy-done.3
  532.1 0.8 copy.26
  532.9 0.0 copy-done.1
  532.9 0.0 copy-start.2
  532.9 1.0 copy.27
  533.9 0.0 copy-done
  533.9 1.1 copy.28
  535.1 0.0 copy-done.2
  535.1 0.8 copy.29
  (7 shorter events, 0.0 us)
Async XLA Ops:
  520.5 10.2 %copy-start.5 = (f32[8,128]{1,0:T(8,128)S(1)}, f32[8,128]{1,0:T(8,128)}, u32[]{:S(2)}) copy-start(f32[8,128]{1,0:T(8,128)} %get-tuple-element.101) | copy-start | bytes 12292
  520.5 10.9 %copy-start.4 = (f32[16,128]{1,0:T(8,128)S(1)}, f32[16,128]{1,0:T(8,128)}, u32[]{:S(2)}) copy-start(f32[16,128]{1,0:T(8,128)} %get-tuple-element.100) | copy-start | bytes 24580
  520.6 11.6 %copy-start.3 = (bf16[128,2048]{1,0:T(8,128)(2,1)S(1)}, bf16[128,2048]{1,0:T(8,128)(2,1)}, u32[]{:S(2)}) copy-start(bf16[128,2048]{1,0:T(8,128)(2,1)} %get-tuple-element.96) | copy-start | bytes 1572868
  520.6 12.4 %copy-start.1 = (f32[128,2048]{1,0:T(8,128)S(1)}, f32[128,2048]{1,0:T(8,128)}, u32[]{:S(2)}) copy-start(f32[128,2048]{1,0:T(8,128)} %get-tuple-element.97) | copy-start | bytes 3145732
  530.8 3.1 copy-start
  532.9 2.1 copy-start.2

commit v5 on v4

--- a/solution.py
+++ b/solution.py
@@ -611,10 +611,10 @@
 def first_kernel(n, f, *refs):
     own, w_qkv, small, routes, w_out, w_gate, w_up = refs[:7]
     hidden_all, mixed, w_head, router, gains, routes_all, gate_near, up_near, out_all = refs[7:16]
-    near, small_all, out_rows, by_head = refs[16:20]
-    sems, out_sems = refs[20:25], refs[25:30]
-    send, recv, beside_send, beside_recv, keep = refs[30:35]
-    wide_send, wide_recv, row_send, row_recv, out_sem = refs[35:]
+    near, small_all, out_rows, by_head, small_rows = refs[16:21]
+    sems, out_sems, small_sems = refs[21:26], refs[26:31], refs[31:36]
+    send, recv, beside_send, beside_recv, keep = refs[36:41]
+    wide_send, wide_recv, row_send, row_recv, out_sem = refs[41:]
     ring = Ring(n, f)
     experts = router.shape[0]
     tok, width = own.shape
@@ -629,13 +629,14 @@
     greet(ring, True, True)
     gather = Gather(ring, own, near, sems)
     gather_out = Gather(ring, out_rows, out_all, out_sems)
+    gather_small = Gather(ring, small_rows, small_all, small_sems)
     out_mine = pl.ds(pl.multiple_of(ring.mine * rows, rows), rows)
 
     def push(kind, step):
         there = ring.peer(step)
         source, target = [
             (by_head.at[there], w_head.at[ring.me, ring.mine]),
-            (small, small_all.at[ring.me, ring.mine]),
+            (small, small),
             (routes, routes_all.at[ring.me]),
         ][kind]
         return remote(
@@ -644,8 +645,8 @@
 
     def aside(kind, step, over, first):
         origin = lax.rem(ring.me + n - step, n)
-        block = [w_head, small_all][kind].at[origin, ring.mine]
-        source = [by_head.at[ring.me], small][kind] if first else block
+        block = w_head.at[origin, ring.mine]
+        source = by_head.at[ring.me] if first else block
         return remote(
             source,
             block,
@@ -654,12 +655,12 @@
             {"fsdp": ring.beside(over)},
         )
 
-    def row(over):
-        return remote(
-            w_out,
-            out_rows.at[out_mine],
-            row_send.at[over],
-            row_recv.at[over],
+    def row(over, kind=0):
+        return remote(
+            [w_out, small][kind],
+            [out_rows, small_rows][kind].at[out_mine],
+            row_send.at[kind, over],
+            row_recv.at[kind, over],
             {"fsdp": ring.beside(over)},
         )
 
@@ -678,10 +679,11 @@
 
     gather.begin()
     for over in range(1, f):
+        row(over, 1).start()
         row(over).start()
     copies = [
         pltpu.make_async_copy(by_head.at[ring.me], w_head.at[ring.me, ring.mine], keep.at[0]),
-        pltpu.make_async_copy(small, small_all.at[ring.me, ring.mine], keep.at[1]),
+        pltpu.make_async_copy(small, small_rows.at[out_mine], keep.at[1]),
         pltpu.make_async_copy(routes, routes_all.at[ring.me], keep.at[2]),
         pltpu.make_async_copy(w_out, out_rows.at[out_mine], keep.at[3]),
     ]
@@ -689,15 +691,18 @@
         copy.start()
 
     def each_1(step, carry):
-        for kind in (1, 0, 2):
+        for kind in (0, 2):
             push(kind, step).start()
         return carry
 
     lax.fori_loop(1, n, each_1, 0)
     for over in range(1, f):
-        aside(1, 0, over, True).start()
         aside(0, 0, over, True).start()
         wide(0, over).start()
+    copies[1].wait()
+    for over in range(1, f):
+        row(over, 1).wait_recv()
+    gather_small.begin()
     each = -(-(n - 1) // 3)
     parts = 1
 
@@ -709,9 +714,10 @@
 
     for i in range(hops):
         gather.pass_on(i)
+        gather_small.pass_on(i)
         if 2 <= i < 5:
             for step in range((i - 2) * each + 1, min((i - 1) * each, n - 1) + 1):
-                for kind in (1, 0):
+                for kind in (0,):
                     push(kind, step).wait_recv()
                     for over in range(1, f):
                         aside(kind, step, over, False).start()
@@ -724,21 +730,21 @@
                 row(over).wait_recv()
             gather_out.begin()
     gather.finish()
-    for copy in copies[:3]:
-        copy.wait()
+    gather_small.finish()
+    copies[0].wait()
+    copies[2].wait()
 
     def each_2(step, carry):
         push(2, step).wait_recv()
-        for kind in (0, 1, 2):
+        for kind in (0, 2):
             push(kind, step).wait_send()
         return carry
 
     lax.fori_loop(1, n, each_2, 0)
 
     def each_3(step, carry):
-        for kind in (0, 1):
-            for over in range(1, f):
-                aside(kind, step, over, False).wait()
+        for over in range(1, f):
+            aside(0, step, over, False).wait()
         return carry
 
     lax.fori_loop(0, n, each_3, 0)
@@ -749,7 +755,7 @@
     for c in range(n):
         for x in range(f):
             start = (c * f + x) * rows
-            flipped = dot(chosen, small_all[c, x], BY_LAST)
+            flipped = dot(chosen, small_all[c, x * rows : (x + 1) * rows], BY_LAST)
             router[:, start : start + rows] = flipped[0:experts, :].astype(BF16)
             gains[:, start : start + rows] = flipped[experts : experts + 8, :]
 
@@ -792,6 +798,7 @@
     gather_out.finish()
     for over in range(1, f):
         row(over).wait_send()
+        row(over, 1).wait_send()
         for part in range(half_parts):
             wide(part, over).wait()
 
@@ -819,14 +826,16 @@
         out_specs=[ANY] + [VMEM] * 4 + [ANY] * 4,
         scratch_shapes=[
             pltpu.VMEM((n, tok, width), BF16),
-            pltpu.VMEM((n, f) + small.shape, BF16),
+            pltpu.VMEM((n, f * small.shape[0], small.shape[1]), BF16),
             pltpu.VMEM((f * w_out.shape[0], w_out.shape[1]), BF16),
             pltpu.VMEM(by_head.shape, BF16),
+            pltpu.VMEM((f * small.shape[0], small.shape[1]), BF16),
         ]
         + Gather.semaphores(n)
         + Gather.semaphores(n)
+        + Gather.semaphores(n)
         + [kind((3, n)), kind((3, n)), kind((2, n, f)), kind((2, n, f)), kind((4,))]
-        + [kind((2, n // 2, f)), kind((2, n // 2, f)), kind((f,)), kind((f,)), kind((n,))],
+        + [kind((2, n // 2, f)), kind((2, n // 2, f)), kind((2, f)), kind((2, f)), kind((n,))],
         compiler_params=pltpu.CompilerParams(
             collective_id=0, has_side_effects=True, vmem_limit_bytes=67_000_000
         ),

time: 540 us -> 531 us (0.983)
  Pallas kernels: 515 us -> 506 us
    pallas_call x1, Pallas kernels: 131 us -> 122 us  [first_gather(): pl.pallas_call(partial(first_kernel, n, f), out_shape=[shape((n, tok, wid...]
where the time goes in v5:
time: 531 us; the launch traced here: 527 us
  Pallas kernels  506 us (95%)
  other arithmetic  12.1 us (2%)
  local copies, waits for them, and re-layouts  7.97 us (2%)
    pallas_call x1, Pallas kernels, first_gather(): pl.pallas_call(partial(first_kernel, n, f), out_shape=[shape((n, tok, wid...  122 us
    pallas_call x1, Pallas kernels, core_stage(): pl.pallas_call(partial(core_kernel, n, f), out_shape=[shape((tok, width),...  121 us
    pallas_call x1, Pallas kernels, last_stage(): pl.pallas_call(partial(last_kernel, n, f), out_shape=[shape((tok, width),...  109 us
    pallas_call x1, Pallas kernels, attention_back(): pl.pallas_call(partial(attention_back_kernel, n, f, factor), out_shape=[s...  82.3 us
    pallas_call x1, Pallas kernels, attention(): pl.pallas_call(partial(attention_kernel, n, f, factor), out_shape=[shape(...  71.9 us

profile of v5, /device:TPU:0, one launch (start us, length us, event | category | flops | bytes accessed | tf_op | source)
XLA Modules:
  0.0 527.1 jit_solution(6579446190702280940)
XLA Ops:
  0.6 0.7 pad_maximum_fusion
  1.4 0.1 copy.21
  1.5 0.6 pad.4.refs_2_
  2.1 122.3 %first_gather.1 = (bf16[16,128,2048]{2,1,0:T(8,128)(2,1)}, f32[2048,384]{1,0:T(8,128)}, bf16[16,2,64,384]{3,2,1,0:T(8,128)(2,1)}, bf16[16,2048]{1,0:T(8,128)(2,1...) custom-call(bf16[128,2048]{1,0:T(8,128)(2,1)} %bitcast.51, ...), custom_call_target="tpu_custom_call" | custom-call | tf_op jit(solution)/shard_map/first_gather/pallas_call | solution.py:812
  124.4 0.3 multiply_cosine_fusion
  124.7 0.1 maximum_maximum_fusion
  124.9 0.7 slice.44.refs_1_.refs_7_
  125.5 0.7 maximum_maximum_fusion.1
  126.2 71.9 %attention.1 = (bf16[2048,128]{1,0:T(8,128)(2,1)}, bf16[2048,128]{1,0:T(8,128)(2,1)}, bf16[2048,128]{1,0:T(8,128)(2,1)}, bf16[2048,128]{1,0:T(8,128)(2,1)}, f32[...) custom-call(f32[2048,384]{1,0:T(8,128)} %get-tuple-element.58.refs_0, ...), custom_call_target="tpu_custom_call" | custom-call | flops 1073741824 | bytes 2097152 | tf_op jit(solution)/shard_map/attention/pallas_call | solution.py:1084
  198.1 1.5 fusion
  199.6 120.9 %core_stage.1 = (f32[128,2048]{1,0:T(8,128)}, f32[128,2048]{1,0:T(8,128)}, bf16[128,2048]{1,0:T(8,128)(2,1)}, bf16[128,2048]{1,0:T(8,128)(2,1)}, bf16[16,16,128]...) custom-call(bf16[128,2048]{1,0:T(8,128)(2,1)} %get-tuple-element.63., ...), custom_call_target="tpu_custom_call" | custom-call | tf_op jit(solution)/shard_map/core_stage/pallas_call | solution.py:1872
  320.5 82.3 %attention_back.1 = (bf16[2048,384]{1,0:T(8,128)(2,1)}, f32[8,128]{1,0:T(8,128)}, bf16[2,16,64,384]{3,2,1,0:T(8,128)(2,1)}, f32[128,2048]{1,0:T(8,128)}, f32[16,...) custom-call(bf16[2048,128]{1,0:T(8,128)(2,1)} %get-tuple-element.60.refs_0_, ...), custom_call_target="tpu_custom_call" | custom-call | tf_op jit(solution)/shard_map/attention_back/pallas_call | solution.py:1363
  402.8 109.0 %last_stage.1 = (f32[128,2048]{1,0:T(8,128)}, f32[64,6144]{1,0:T(8,128)}, f32[8,128]{1,0:T(8,128)}, bf16[1,2048,512]{2,1,0:T(8,128)(2,1)}, bf16[1,2048,512]{2,1,...) custom-call(bf16[16,128,384]{2,1,0:T(8,128)(2,1)} %bitcast.60, ...), custom_call_target="tpu_custom_call" | custom-call | tf_op jit(solution)/shard_map/last_stage/pallas_call | solution.py:2228
  511.8 0.0 copy-start.5
  511.8 0.0 copy-start.4
  511.8 0.0 copy-start.3
  511.8 0.0 copy-start.1
  511.8 10.2 %convert_add_fusion = (f32[1,2048,512]{2,1,0:T(8,128)}, f32[1,2048,512]{2,1,0:T(8,128)}, f32[1,2048,512]{2,1,0:T(8,128)}) fusion(bf16[1,2048,512]{2,1,0:T(8,128)(2,1)} %get-tuple-element.106, bf16[3,2048,512]{2,1,0:T(8,128)(2,1)} %get-tuple-element.102, bf16[1,2048,512]{2,1,0:T(8,128)(2,1)} %get-tuple-element.104, bf16[1,2048,512]{2,1,0:T(8,128)(2,1)} %get-tuple-element.105, ...), kind=kLoop, calls=%fused_computation | loop fusion | flops 10485760 | bytes 27265024 | tf_op jit(solution)/shard_map/add | solution.py:2438
  522.0 0.0 copy-start
  522.0 0.0 copy-done.5
  522.1 0.7 constant_dynamic-slice_fusion
  522.7 0.0 copy-done.4
  522.7 0.7 dynamic-slice_bitcast_fusion
  523.4 0.0 copy-done.3
  523.4 0.8 copy.26
  524.2 0.0 copy-done.1
  524.2 0.0 copy-start.2
  524.2 1.0 copy.27
  525.2 0.0 copy-done
  525.2 1.1 copy.28
  526.3 0.0 copy-done.2
  526.3 0.8 copy.29
  (7 shorter events, 0.0 us)
Async XLA Ops:
  511.8 10.2 %copy-start.5 = (f32[8,128]{1,0:T(8,128)S(1)}, f32[8,128]{1,0:T(8,128)}, u32[]{:S(2)}) copy-start(f32[8,128]{1,0:T(8,128)} %get-tuple-element.101) | copy-start | bytes 12292
  511.8 10.9 %copy-start.4 = (f32[16,128]{1,0:T(8,128)S(1)}, f32[16,128]{1,0:T(8,128)}, u32[]{:S(2)}) copy-start(f32[16,128]{1,0:T(8,128)} %get-tuple-element.100) | copy-start | bytes 24580
  511.8 11.6 %copy-start.3 = (bf16[128,2048]{1,0:T(8,128)(2,1)S(1)}, bf16[128,2048]{1,0:T(8,128)(2,1)}, u32[]{:S(2)}) copy-start(bf16[128,2048]{1,0:T(8,128)(2,1)} %get-tuple-element.96) | copy-start | bytes 1572868
  511.8 12.4 %copy-start.1 = (f32[128,2048]{1,0:T(8,128)S(1)}, f32[128,2048]{1,0:T(8,128)}, u32[]{:S(2)}) copy-start(f32[128,2048]{1,0:T(8,128)} %get-tuple-element.97) | copy-start | bytes 3145732
  522.0 3.1 copy-start
  524.2 2.1 copy-start.2
